TPU v7x, 128 devices: a whole 4x4x4 slice. The times are simulated.
128 devices in a mesh: seq: 64 (over y, z_hi, x, core), tp: 2 (over z_lo).
Axes of the slice: x: 4, y: 4, z: 4 (z_hi: 2, z_lo: 2; z = z_hi * 2 + z_lo), core: 2. Of those that a mesh axis runs over, the one named last changes fastest.
Arguments:
- query_rows: bfloat16 [8192, 2048], P('seq', 'tp'), may hold values from -350 to 350
- key_rows: bfloat16 [8192, 512], P('seq', 'tp'), may hold values from -6 to 6
- stored_value_rows: bfloat16 [8192, 512], P('seq', 'tp'), may hold values from -6 to 6
- output_grad: bfloat16 [8192, 2048], P('seq', 'tp'), may hold values from -96 to 96
- layer_input: bfloat16 [8192, 4096], P('seq', 'tp'), may hold values from -16 to 16
- key_matrix: bfloat16 [4096, 512], P(None, 'tp'), may hold values from -0.09375 to 0.09375
- value_matrix: bfloat16 [4096, 512], P(None, 'tp'), may hold values from -0.09375 to 0.09375
- run_placement: int32 [64, 64], replicated, may hold values from 0 to 63, as said below
Outputs:
- query_grad: bfloat16 [8192, 2048], P('seq', 'tp')
- input_grad: bfloat16 [8192, 4096], P('seq', 'tp')
- key_weight_grad: float32 [4096, 512], P('seq', 'tp')
- value_weight_grad: float32 [4096, 512], P('seq', 'tp')
Inputs may be any that keep to these rules, and one draw needn't show every extreme that they name: `run_placement`: row j gives, for each storing index d of seq, the slot within sequence block j of the 2 consecutive positions that d holds; every row is a permutation of 0 to 63.
All inputs are finite; a program needn't handle non-finite values.
Results may differ from a plain program's by a relative error of at most 0.0081.
Values may be sent and summed in bfloat16 or wider, within the bound.
A program may use at most 128 MiB of HBM per device.

v0:
```python
import math

import jax
import jax.numpy as jnp
from jax import lax
from jax.sharding import Mesh
from jax.sharding import PartitionSpec as P

HEAD_SIZE = 128
WINDOW_LENGTH = 4096
SPAN = 32
GROUP = 4
SEQ = ("seq_0", "seq_1", "seq_2", "seq_3")


masked_value = -1e30


def laid_out(pieces, dim):
    shape = list(pieces.shape[1:])
    shape[dim] *= pieces.shape[0]
    return jnp.moveaxis(pieces, 0, dim).reshape(shape)


def from_everyone(array, axis):
    copies = jnp.broadcast_to(array, (lax.axis_size(axis), *array.shape))
    return lax.all_to_all(copies, axis, split_axis=0, concat_axis=0, tiled=True)


def gathered_copies(array, axis, dim):
    return laid_out(from_everyone(array, axis), dim)


def sent_together(arrays, axis, split_dim, concat_dim, along):
    widths = [a.shape[along] for a in arrays]
    both = jnp.concatenate(arrays, axis=along)
    result = lax.all_to_all(both, axis, split_axis=split_dim, concat_axis=concat_dim, tiled=True)
    return tuple(jnp.split(result, [sum(widths[:k]) for k in range(1, len(widths))], axis=along))


def from_behind(array, axis, by):
    peers = lax.axis_size(axis)
    pairs = [(i, i + by) for i in range(peers) if 0 <= i + by < peers]
    return lax.ppermute(array, axis, pairs)


def in_blocks(array, dim, peers):
    shape = array.shape
    pieces = array.reshape(*shape[:dim], peers, shape[dim] // peers, *shape[dim + 1 :])
    return jnp.moveaxis(pieces, dim, 0)


def summed_on_arrival(array, axis, dim):
    pieces = in_blocks(array, dim, lax.axis_size(axis))
    arrived = lax.all_to_all(pieces, axis, split_axis=0, concat_axis=0, tiled=True)
    return arrived.sum(axis=0)


def moved_by_axis(pieces, axes, turns):
    inside = pieces.shape[1:]
    result = pieces.reshape(*(lax.axis_size(a) for a in axes), *inside)
    for k in turns:
        result = lax.all_to_all(result, axes[k], k, k, tiled=True)
    return result.reshape(-1, *inside)


def exchange_by_chip(array, groups, turns, split_dim, concat_dim):
    peers = lax.axis_size(groups[0]) * lax.axis_size(groups[1])
    pieces = in_blocks(array, split_dim, peers)
    return laid_out(moved_by_axis(pieces, groups, turns), concat_dim)


def doubling_plan(span_blocks):
    hop_list = []
    reached = 1
    while reached < span_blocks + 1:
        sending = min(reached, span_blocks + 1 - reached)
        hop_list.append((reached, sending))
        reached = reached + sending
    return hop_list


def head_major(matrix, kv_local):
    rows_here = matrix.shape[0]
    shaped = matrix.reshape(rows_here, kv_local, GROUP, HEAD_SIZE).transpose(1, 2, 0, 3)
    return shaped.reshape(kv_local, GROUP * rows_here, HEAD_SIZE)


def local(
    query_rows,
    key_rows,
    stored_value_rows,
    output_grad,
    layer_input,
    key_matrix,
    value_matrix,
    run_placement,
):
    seq_count = lax.axis_size(SEQ)
    seq_index = lax.axis_index(SEQ)
    rows_here = query_rows.shape[0]
    run_rows = rows_here // seq_count
    kv_width = key_rows.shape[1]
    kv_local = kv_width // HEAD_SIZE
    score_scale = 1.0 / math.sqrt(HEAD_SIZE)
    full_input = gathered_copies(layer_input, "tp", 1)
    arrived = sent_together((query_rows, key_rows, stored_value_rows, output_grad), SEQ, 0, 0, 1)
    slot_row = lax.dynamic_index_in_dim(run_placement, seq_index, 0, keepdims=False)
    inverse = jnp.argsort(slot_row)

    def to_sequence(matrix):
        col_count = matrix.shape[1]
        return jnp.take(matrix.reshape(seq_count, run_rows, col_count), inverse, axis=0).reshape(
            rows_here, col_count
        )

    def into_stored_order(matrix):
        col_count = matrix.shape[1]
        return jnp.take(matrix.reshape(seq_count, run_rows, col_count), slot_row, axis=0).reshape(
            rows_here, col_count
        )

    query_seq = head_major(to_sequence(arrived[0]), kv_local)
    grad_seq = head_major(to_sequence(arrived[3]), kv_local)
    own_kv = jnp.concatenate([to_sequence(arrived[1]), to_sequence(arrived[2])], axis=1)
    gathered = own_kv[None]
    for reached, sending in doubling_plan(SPAN):
        fetched = from_behind(gathered[gathered.shape[0] - sending :], SEQ, reached)
        gathered = jnp.concatenate([fetched, gathered], axis=0)
    past_blocks = gathered[:SPAN]
    tile_keys = WINDOW_LENGTH // 4
    query_pos = seq_index * rows_here + jnp.arange(rows_here, dtype=jnp.int32)
    first_past = (seq_index - SPAN) * rows_here
    past_tiles = past_blocks.reshape(4, tile_keys, 2 * kv_width)
    key_tiles = []
    for tile_index in range(4):
        key_tiles.append(
            (
                past_tiles[tile_index],
                first_past + tile_index * tile_keys + jnp.arange(tile_keys, dtype=jnp.int32),
            )
        )
    key_tiles.append((own_kv, query_pos))

    def scores_for(kv_tile, key_pos):
        key_count = key_pos.shape[0]
        keys_here = kv_tile[:, :kv_width].reshape(key_count, kv_local, HEAD_SIZE)
        values_here = kv_tile[:, kv_width:].reshape(key_count, kv_local, HEAD_SIZE)
        logits = (
            jnp.einsum("gqd,kgd->gqk", query_seq, keys_here, preferred_element_type=jnp.float32)
            * score_scale
        )
        prob_grad = jnp.einsum(
            "gqd,kgd->gqk", grad_seq, values_here, preferred_element_type=jnp.float32
        )
        in_window = (
            (key_pos[None, :] <= query_pos[:, None])
            & (key_pos[None, :] > query_pos[:, None] - WINDOW_LENGTH)
            & (key_pos[None, :] >= 0)
        )
        shape_four = (kv_local, GROUP, rows_here, key_count)
        return (logits.reshape(shape_four), prob_grad.reshape(shape_four), in_window, keys_here)

    running = jnp.full((kv_local, GROUP, rows_here), masked_value, jnp.float32)
    row_total = jnp.zeros((kv_local, GROUP, rows_here), jnp.float32)
    weighted = jnp.zeros((kv_local, GROUP, rows_here), jnp.float32)
    for kv_tile, key_pos in key_tiles:
        logits, prob_grad, in_window, keys_here = scores_for(kv_tile, key_pos)
        row_top = jnp.max(jnp.where(in_window, logits, masked_value), axis=-1)
        new_top = jnp.maximum(running, row_top)
        exponent = jnp.where(in_window, jnp.exp(logits - new_top[..., None]), 0.0)
        factor = jnp.exp(running - new_top)
        row_total = row_total * factor + jnp.sum(exponent, axis=-1)
        weighted = weighted * factor + jnp.sum(exponent * prob_grad, axis=-1)
        running = new_top
    log_total = running + jnp.log(row_total)
    row_delta = weighted / row_total
    query_acc = jnp.zeros((kv_local, GROUP * rows_here, HEAD_SIZE), jnp.float32)
    tile_grads = []
    for kv_tile, key_pos in key_tiles:
        logits, prob_grad, in_window, keys_here = scores_for(kv_tile, key_pos)
        key_count = key_pos.shape[0]
        probs = jnp.where(in_window, jnp.exp(logits - log_total[..., None]), 0.0)
        score_grad = probs * (prob_grad - row_delta[..., None])
        probs_b = probs.astype(jnp.bfloat16).reshape(kv_local, GROUP * rows_here, key_count)
        score_b = score_grad.astype(jnp.bfloat16).reshape(kv_local, GROUP * rows_here, key_count)
        query_acc = query_acc + jnp.einsum(
            "gqk,kgd->gqd", score_b, keys_here, preferred_element_type=jnp.float32
        )
        key_portion = (
            jnp.einsum("gqk,gqd->kgd", score_b, query_seq, preferred_element_type=jnp.float32)
            * score_scale
        )
        value_portion = jnp.einsum(
            "gqk,gqd->kgd", probs_b, grad_seq, preferred_element_type=jnp.float32
        )
        tile_grads.append(
            jnp.concatenate(
                [
                    key_portion.reshape(key_count, kv_width),
                    value_portion.reshape(key_count, kv_width),
                ],
                axis=1,
            )
        )
    past_grads = jnp.stack(tile_grads[:4]).reshape(SPAN, rows_here, 2 * kv_width)
    own_grad = tile_grads[4]
    holding = jnp.concatenate([past_grads, own_grad[None]], axis=0)
    for reached, sending in reversed(doubling_plan(SPAN)):
        outgoing = holding[:sending]
        holding = holding[sending:]
        returned = from_behind(outgoing.astype(jnp.bfloat16), SEQ, -reached).astype(outgoing.dtype)
        holding = holding.at[holding.shape[0] - sending :].add(returned)
    own_grad = holding[0]
    query_seq_grad = (
        (query_acc * score_scale)
        .reshape(kv_local, GROUP, rows_here, HEAD_SIZE)
        .transpose(2, 0, 1, 3)
    )
    query_seq_grad = query_seq_grad.reshape(rows_here, kv_local * GROUP * HEAD_SIZE).astype(
        jnp.bfloat16
    )
    kv_seq_grad = own_grad.astype(jnp.bfloat16)
    query_grad, kv_grad = sent_together(
        (into_stored_order(query_seq_grad), into_stored_order(kv_seq_grad)), SEQ, 0, 0, 1
    )
    contract_cols = (((1,), (1,)), ((), ()))
    partial_input = lax.dot_general(
        kv_grad[:, :kv_width], key_matrix, contract_cols, preferred_element_type=jnp.float32
    )
    partial_input = partial_input + lax.dot_general(
        kv_grad[:, kv_width:], value_matrix, contract_cols, preferred_element_type=jnp.float32
    )
    input_grad = summed_on_arrival(partial_input, "tp", 1).astype(jnp.bfloat16)
    contract_rows = (((0,), (0,)), ((), ()))
    input_columns = exchange_by_chip(
        full_input, (("seq_0", "seq_1", "seq_2"), "seq_3"), (1, 0), 1, 0
    )
    weight_rows = lax.dot_general(
        input_columns,
        lax.all_gather(kv_grad, SEQ, axis=0, tiled=True),
        contract_rows,
        preferred_element_type=jnp.float32,
    )
    return (query_grad, input_grad, weight_rows[:, :kv_width], weight_rows[:, kv_width:])


def solution(mesh):
    torus = Mesh(
        mesh.devices.reshape(4, 2, 4, 2, mesh.shape["tp"]),
        ("seq_0", "seq_1", "seq_2", "seq_3", "tp"),
    )
    placed = (
        P(SEQ, "tp"),
        P(SEQ, "tp"),
        P(SEQ, "tp"),
        P(SEQ, "tp"),
        P(SEQ, "tp"),
        P(None, "tp"),
        P(None, "tp"),
        P(),
    )
    return jax.shard_map(
        local,
        mesh=torus,
        in_specs=placed,
        out_specs=(P(SEQ, "tp"), P(SEQ, "tp"), P(SEQ, "tp"), P(SEQ, "tp")),
        check_vma=False,
    )
```

profile of v0, /device:TPU:0, one launch (start us, length us, event | category | flops | bytes accessed | tf_op | source)
XLA Modules:
  0.0 512.2 jit_solution(3167616125775860426)
XLA Ops:
  9.6 11.4 %all-to-all-start = ((bf16[64,2,2560]{2,1,0:T(2,128)(2,1)}), bf16[64,2,2560]{2,1,0:T(2,128)(2,1)S(1)}, u32[]{:S(2)}, u32[]{:S(2)}) async-start(bf16[64,2,2560]{2,1,0:T(2,128)(2,1)} %all_to_all.26), calls=%async_computation | async-start | bytes 1310720 | tf_op jit(solution)/shard_map/all_to_all | solution.py:37
  23.8 12.6 %all-to-all-done = bf16[64,2,2560]{2,1,0:T(2,128)(2,1)S(1)} async-done(((bf16[64,2,2560]{2,1,0:T(2,128)(2,1)}), bf16[64,2,2560]{2,1,0:T(2,128)(2,1)S(1)}, u32[]{:S(2)}, u32[]{:S(2)}) %all-to-all-start) | async-done | bytes 655392 | tf_op jit(solution)/shard_map/all_to_all | solution.py:37
  41.4 5.8 %collective-permute-start.2 = (bf16[2,128,512]{2,1,0:T(8,128)(2,1)S(1)}, bf16[2,128,512]{2,1,0:T(8,128)(2,1)S(1)}, u32[]{:S(2)}, u32[]{:S(2)}) collective-permute-start(bf16[2,128,512]{2,1,0:T(8,128)(2,1)S(1)} %pad_maximum_fusion.11), channel_id=1, source_target_pairs={{0,4},{2,6},{4,8},{6,10},{8,12},{10,14},{12,16},{14,18},{16,20},{1... | collective-permute-start | bytes 786440 | tf_op jit(solution)/shard_map/ppermute | solution.py:44
  47.2 4.2 collective-permute-done.2
  51.6 5.1 collective-permute-start.3
  56.7 10.7 %collective-permute-done.3 = bf16[4,128,512]{2,1,0:T(8,128)(2,1)S(1)} collective-permute-done((bf16[4,128,512]{2,1,0:T(8,128)(2,1)S(1)}, bf16[4,128,512]{2,1,0:T(8,128)(2,1)S(1)}, u32[]{:S(2)}, u32[]{:S(2)}) %collective-permute-start.3) | collective-permute-done | bytes 524320 | tf_op jit(solution)/shard_map/ppermute | solution.py:44
  67.6 10.4 %collective-permute-start.4 = (bf16[8,128,512]{2,1,0:T(8,128)(2,1)S(1)}, bf16[8,128,512]{2,1,0:T(8,128)(2,1)S(1)}, u32[]{:S(2)}, u32[]{:S(2)}) collective-permute-start(bf16[8,128,512]{2,1,0:T(8,128)(2,1)S(1)} %pad_maximum_fusion.7), channel_id=1, source_target_pairs={{0,16},{2,18},{4,20},{6,22},{8,24},{10,26},{12,28},{14,30},{16,32}... | collective-permute-start | bytes 3145736 | tf_op jit(solution)/shard_map/ppermute | solution.py:44
  78.0 16.2 %collective-permute-done.4 = bf16[8,128,512]{2,1,0:T(8,128)(2,1)S(1)} collective-permute-done((bf16[8,128,512]{2,1,0:T(8,128)(2,1)S(1)}, bf16[8,128,512]{2,1,0:T(8,128)(2,1)S(1)}, u32[]{:S(2)}, u32[]{:S(2)}) %collective-permute-start.4) | collective-permute-done | bytes 1048608 | tf_op jit(solution)/shard_map/ppermute | solution.py:44
  99.2 11.4 %collective-permute-start.5 = (bf16[16,128,512]{2,1,0:T(8,128)(2,1)}, bf16[16,128,512]{2,1,0:T(8,128)(2,1)}, u32[]{:S(2)}, u32[]{:S(2)}) collective-permute-start(bf16[16,128,512]{2,1,0:T(8,128)(2,1)} %constant_dynamic-update-slice_fusion), channel_id=1, source_target_pairs={{0,32},{2,34},{4,36},{6,38},{8,40},{10,42},{12,44},{14,46},{16,48}... | collective-permute-start | bytes 6291464 | tf_op jit(solution)/shard_map/ppermute | solution.py:44
  112.8 2.5 collective-permute-start
  122.4 2.2 broadcast_select_fusion.2
  129.6 18.7 %collective-permute-done = bf16[1,128,512]{2,1,0:T(8,128)(2,1)} collective-permute-done((bf16[1,128,512]{2,1,0:T(8,128)(2,1)}, bf16[1,128,512]{2,1,0:T(8,128)(2,1)}, u32[]{:S(2)}, u32[]{:S(2)}) %collective-permute-start) | collective-permute-done | bytes 131104 | tf_op jit(solution)/shard_map/ppermute | solution.py:44
  148.3 3.7 pad_maximum_fusion.6
  154.9 2.3 fusion.65
  159.2 2.3 fusion.64
  163.6 2.2 fusion.67
  175.2 2.1 select_reduce_fusion.1
  177.6 3.0 select_reduce_fusion.2
  183.4 3.4 multiply_reduce_fusion.3
  186.8 3.5 multiply_reduce_fusion.2
  190.3 3.4 multiply_reduce_fusion.1
  193.8 3.6 multiply_reduce_fusion
  198.5 2.3 fusion.14
  200.9 2.3 fusion.12
  203.2 2.3 fusion.10
  205.5 2.3 fusion.8
  208.1 2.5 copy.169
  212.7 17.5 %multiply_convert_fusion.3 = (bf16[2,512,1024]{2,1,0:T(8,128)(2,1)}, bf16[2,512,1024]{2,1,0:T(8,128)(2,1)}, bf16[2,512,1024]{2,1,0:T(8,128)(2,1)}, bf16[2,512,1024]{2,1,0:T(8,128)(2,1)}) fusion(f32[2,512,1024]{2,1,0:T(8,128)} %get-tuple-element.183, f32[2,512,1024]{2,1,0:T(8,128)} %copy-done.3, f32[2,512]{1,0:T(2,128)S(1)} %get-tuple-element.132, ...), kind=kLoop, calls=%fused_computation.17 | loop fusion | flops 25165824 | bytes 44048384 | tf_op jit(solution)/shard_map/convert_element_type | solution.py:186
  230.3 2.1 convolution_multiply_fusion.3
  233.7 2.6 copy.173
  236.2 2.1 convolution_multiply_fusion.2
  243.1 2.5 copy.177
  249.0 2.6 copy.181
  262.5 5.5 %collective-permute-done.6 = bf16[1,128,512]{2,1,0:T(8,128)(2,1)S(1)} collective-permute-done((bf16[1,128,512]{2,1,0:T(8,128)(2,1)S(1)}, bf16[1,128,512]{2,1,0:T(8,128)(2,1)S(1)}, u32[]{:S(2)}, u32[]{:S(2)}) %collective-permute-start.6) | collective-permute-done | bytes 131104 | tf_op jit(solution)/shard_map/ppermute | solution.py:44
  269.7 42.5 %collective-permute-done.7 = bf16[16,128,512]{2,1,0:T(8,128)(2,1)S(1)} collective-permute-done((bf16[16,128,512]{2,1,0:T(8,128)(2,1)S(1)}, bf16[16,128,512]{2,1,0:T(8,128)(2,1)S(1)}, u32[]{:S(2)}, u32[]{:S(2)}) %collective-permute-start.7) | collective-permute-done | bytes 2097184 | tf_op jit(solution)/shard_map/ppermute | solution.py:44
  316.3 15.3 %collective-permute-done.8 = bf16[8,128,512]{2,1,0:T(8,128)(2,1)S(1)} collective-permute-done((bf16[8,128,512]{2,1,0:T(8,128)(2,1)S(1)}, bf16[8,128,512]{2,1,0:T(8,128)(2,1)S(1)}, u32[]{:S(2)}, u32[]{:S(2)}) %collective-permute-start.8) | collective-permute-done | bytes 1048608 | tf_op jit(solution)/shard_map/ppermute | solution.py:44
  335.1 9.5 %collective-permute-done.9 = bf16[4,128,512]{2,1,0:T(8,128)(2,1)S(1)} collective-permute-done((bf16[4,128,512]{2,1,0:T(8,128)(2,1)S(1)}, bf16[4,128,512]{2,1,0:T(8,128)(2,1)S(1)}, u32[]{:S(2)}, u32[]{:S(2)}) %collective-permute-start.9) | collective-permute-done | bytes 524320 | tf_op jit(solution)/shard_map/ppermute | solution.py:44
  360.0 35.9 %all_to_all.41 = bf16[64,2,1536]{2,1,0:T(2,128)(2,1)S(1)} all-to-all(bf16[64,2,1536]{2,1,0:T(2,128)(2,1)S(1)} %pad_maximum_fusion.10), channel_id=1, replica_groups=mesh['seq_0'=4,'seq_1'=2,'seq_2'=4,'seq_3'=2,'tp'=2] {'seq_0','seq_1','s..., dimensions={0} | all-to-all | bytes 786432 | tf_op jit(solution)/shard_map/all_to_all | solution.py:37
  397.1 17.5 %all_to_all.42 = bf16[2,128,2048]{1,2,0:T(8,128)(2,1)S(1)} all-to-all(bf16[2,128,2048]{1,2,0:T(8,128)(2,1)S(1)} %broadcast_in_dim.201), channel_id=1, replica_groups=mesh['seq_0'=4,'seq_1'=2,'seq_2'=4,'seq_3'=2,'tp'=2] {'tp'}, dimensions={0} | all-to-all | bytes 2097152 | tf_op jit(solution)/shard_map/all_to_all | solution.py:27
  415.2 4.6 all_to_all.43
  421.8 3.9 all-to-all-start.5
  429.7 16.1 %all-to-all-done.5 = bf16[32,2,128,64]{2,1,3,0:T(2,128)(2,1)S(1)} async-done(((bf16[32,2,128,64]{2,1,3,0:T(2,128)(2,1)}), bf16[32,2,128,64]{2,1,3,0:T(2,128)(2,1)S(1)}, u32[]{:S(2)}, u32[]{:S(2)}) %all-to-all-start.5) | async-done | bytes 1048608 | tf_op jit(solution)/shard_map/all_to_all | solution.py:63
  445.8 4.8 all-to-all-start.2
  450.6 2.1 copy.192
  455.3 34.7 %all-to-all-done.2 = f32[2,128,2048]{2,1,0:T(8,128)} async-done(((f32[2,128,2048]{2,1,0:T(8,128)}), f32[2,128,2048]{2,1,0:T(8,128)}, u32[]{:S(2)}, u32[]{:S(2)}) %all-to-all-start.2) | async-done | bytes 2097184 | tf_op jit(solution)/shard_map/all_to_all | solution.py:55
  490.1 2.7 reduce_sum.109
  492.7 6.6 %all-gather.2.cloned.1.call-done = bf16[8192,512]{1,0:T(8,128)(2,1)} async-done(((bf16[128,512]{1,0:T(8,128)(2,1)}), bf16[8192,512]{1,0:T(8,128)(2,1)}) %all-gather.2.cloned.1.call-update) | async-done | bytes 8388624 | tf_op jit(solution)/shard_map/all_gather | solution.py:241
  499.3 4.9 convolution_bitcast_fusion
  (238 shorter events, 107.8 us)
Async XLA Ops:
  7.2 418.6 %copy-start = (bf16[4096,256]{1,0:T(8,128)(2,1)S(1)}, bf16[4096,256]{1,0:T(8,128)(2,1)}, u32[]{:S(2)}) copy-start(bf16[4096,256]{1,0:T(8,128)(2,1)} %param.39) | copy-start | bytes 6291460
  9.6 26.8 %all-to-all-start = ((bf16[64,2,2560]{2,1,0:T(2,128)(2,1)}), bf16[64,2,2560]{2,1,0:T(2,128)(2,1)S(1)}, u32[]{:S(2)}, u32[]{:S(2)}) async-start(bf16[64,2,2560]{2,1,0:T(2,128)(2,1)} %all_to_all.26), calls=%async_computation | async-start | bytes 1310720 | tf_op jit(solution)/shard_map/all_to_all | solution.py:37
  20.9 478.4 %all-gather.2.cloned.1.call-start = ((), (), s32[]{:S(2)}) async-start(), calls=%async_computation.6 | async-start | bytes 8519680 | tf_op jit(solution)/shard_map/all_gather | solution.py:241
  36.6 14.9 %copy-start.26 = (bf16[128,2560]{1,0:T(8,128)(2,1)}, bf16[128,2560]{1,0:T(8,128)(2,1)S(1)}, u32[]{:S(2)}) copy-start(bf16[128,2560]{1,0:T(8,128)(2,1)S(1)} %all_to_all.28) | copy-start | bytes 1966084
  38.3 13.2 %copy-start.36 = (bf16[64,2,256]{2,1,0:T(2,128)(2,1)}, bf16[64,2,256]{2,1,0:T(2,128)(2,1)S(1)}, u32[]{:S(2)}) copy-start(bf16[64,2,256]{2,1,0:T(2,128)(2,1)S(1)} %get-tuple-element.165) | copy-start | bytes 196612
  38.3 13.2 %copy-start.38 = (bf16[64,2,256]{2,1,0:T(2,128)(2,1)}, bf16[64,2,256]{2,1,0:T(2,128)(2,1)S(1)}, u32[]{:S(2)}) copy-start(bf16[64,2,256]{2,1,0:T(2,128)(2,1)S(1)} %get-tuple-element.166) | copy-start | bytes 196612
  38.4 13.1 %copy-start.40 = (bf16[128,256]{1,0:T(8,128)(2,1)}, bf16[128,256]{1,0:T(8,128)(2,1)S(1)}, u32[]{:S(2)}) copy-start(bf16[128,256]{1,0:T(8,128)(2,1)S(1)} %reshape.715) | copy-start | bytes 196612
  38.4 13.1 %copy-start.42 = (bf16[128,256]{1,0:T(8,128)(2,1)}, bf16[128,256]{1,0:T(8,128)(2,1)S(1)}, u32[]{:S(2)}) copy-start(bf16[128,256]{1,0:T(8,128)(2,1)S(1)} %reshape.717) | copy-start | bytes 196612
  38.4 57.9 %copy-start.33 = (bf16[1,128,512]{2,1,0:T(8,128)(2,1)}, bf16[1,128,512]{2,1,0:T(8,128)(2,1)S(1)}, u32[]{:S(2)}) copy-start(bf16[1,128,512]{2,1,0:T(8,128)(2,1)S(1)} %maximum_bitcast_fusion.5) | copy-start | bytes 393220
  38.5 2.9 collective-permute-start.1
  41.4 10.1 %collective-permute-start.2 = (bf16[2,128,512]{2,1,0:T(8,128)(2,1)S(1)}, bf16[2,128,512]{2,1,0:T(8,128)(2,1)S(1)}, u32[]{:S(2)}, u32[]{:S(2)}) collective-permute-start(bf16[2,128,512]{2,1,0:T(8,128)(2,1)S(1)} %pad_maximum_fusion.11), channel_id=1, source_target_pairs={{0,4},{2,6},{4,8},{6,10},{8,12},{10,14},{12,16},{14,18},{16,20},{1... | collective-permute-start | bytes 786440 | tf_op jit(solution)/shard_map/ppermute | solution.py:44
  51.5 47.0 %copy-start.41 = (bf16[128,256]{1,0:T(8,128)(2,1)S(1)}, bf16[128,256]{1,0:T(8,128)(2,1)}, u32[]{:S(2)}) copy-start(bf16[128,256]{1,0:T(8,128)(2,1)} %copy-done.40) | copy-start | bytes 196612
  51.6 47.0 %copy-start.43 = (bf16[128,256]{1,0:T(8,128)(2,1)S(1)}, bf16[128,256]{1,0:T(8,128)(2,1)}, u32[]{:S(2)}) copy-start(bf16[128,256]{1,0:T(8,128)(2,1)} %copy-done.42) | copy-start | bytes 196612
  51.6 63.7 %copy-start.39 = (bf16[64,2,256]{2,1,0:T(2,128)(2,1)S(1)}, bf16[64,2,256]{2,1,0:T(2,128)(2,1)}, u32[]{:S(2)}) copy-start(bf16[64,2,256]{2,1,0:T(2,128)(2,1)} %copy-done.38) | copy-start | bytes 196612
  51.6 64.4 %copy-start.37 = (bf16[64,2,256]{2,1,0:T(2,128)(2,1)S(1)}, bf16[64,2,256]{2,1,0:T(2,128)(2,1)}, u32[]{:S(2)}) copy-start(bf16[64,2,256]{2,1,0:T(2,128)(2,1)} %copy-done.36) | copy-start | bytes 196612
  51.6 15.8 %collective-permute-start.3 = (bf16[4,128,512]{2,1,0:T(8,128)(2,1)S(1)}, bf16[4,128,512]{2,1,0:T(8,128)(2,1)S(1)}, u32[]{:S(2)}, u32[]{:S(2)}) collective-permute-start(bf16[4,128,512]{2,1,0:T(8,128)(2,1)S(1)} %pad_maximum_fusion.9), channel_id=1, source_target_pairs={{0,8},{2,10},{4,12},{6,14},{8,16},{10,18},{12,20},{14,22},{16,24},... | collective-permute-start | bytes 1572872 | tf_op jit(solution)/shard_map/ppermute | solution.py:44
  67.6 26.7 %collective-permute-start.4 = (bf16[8,128,512]{2,1,0:T(8,128)(2,1)S(1)}, bf16[8,128,512]{2,1,0:T(8,128)(2,1)S(1)}, u32[]{:S(2)}, u32[]{:S(2)}) collective-permute-start(bf16[8,128,512]{2,1,0:T(8,128)(2,1)S(1)} %pad_maximum_fusion.7), channel_id=1, source_target_pairs={{0,16},{2,18},{4,20},{6,22},{8,24},{10,26},{12,28},{14,30},{16,32}... | collective-permute-start | bytes 3145736 | tf_op jit(solution)/shard_map/ppermute | solution.py:44
  99.2 49.1 %collective-permute-start.5 = (bf16[16,128,512]{2,1,0:T(8,128)(2,1)}, bf16[16,128,512]{2,1,0:T(8,128)(2,1)}, u32[]{:S(2)}, u32[]{:S(2)}) collective-permute-start(bf16[16,128,512]{2,1,0:T(8,128)(2,1)} %constant_dynamic-update-slice_fusion), channel_id=1, source_target_pairs={{0,32},{2,34},{4,36},{6,38},{8,40},{10,42},{12,44},{14,46},{16,48}... | collective-permute-start | bytes 6291464 | tf_op jit(solution)/shard_map/ppermute | solution.py:44
  112.8 35.4 %collective-permute-start = (bf16[1,128,512]{2,1,0:T(8,128)(2,1)}, bf16[1,128,512]{2,1,0:T(8,128)(2,1)}, u32[]{:S(2)}, u32[]{:S(2)}) collective-permute-start(bf16[1,128,512]{2,1,0:T(8,128)(2,1)} %copy-done.33), channel_id=1, source_target_pairs={{0,64},{2,66},{4,68},{6,70},{8,72},{10,74},{12,76},{14,78},{16,80}... | collective-permute-start | bytes 393224 | tf_op jit(solution)/shard_map/ppermute | solution.py:44
  161.5 13.6 %copy-start.48 = (pred[128,1024]{1,0:T(8,128)(4,1)S(1)}, pred[128,1024]{1,0:T(8,128)(4,1)}, u32[]{:S(2)}) copy-start(pred[128,1024]{1,0:T(8,128)(4,1)} %get-tuple-element.163) | copy-start | bytes 393220
  172.0 5.4 %copy-start.47 = (pred[128,1024]{1,0:T(8,128)(4,1)S(1)}, pred[128,1024]{1,0:T(8,128)(4,1)}, u32[]{:S(2)}) copy-start(pred[128,1024]{1,0:T(8,128)(4,1)} %get-tuple-element.162) | copy-start | bytes 393220
  177.3 25.8 %copy-start.1 = (f32[2,512,1024]{2,1,0:T(8,128)}, f32[2,512,1024]{2,1,0:T(8,128)S(1)}, u32[]{:S(2)}) copy-start(f32[2,512,1024]{2,1,0:T(8,128)S(1)} %get-tuple-element.174) | copy-start | bytes 12582916
  177.5 23.3 %copy-start.9 = (pred[4,128,1024]{2,1,0:T(8,128)(4,1)}, pred[4,128,1024]{2,1,0:T(8,128)(4,1)S(1)}, u32[]{:S(2)}) copy-start(pred[4,128,1024]{2,1,0:T(8,128)(4,1)S(1)} %broadcast_in_dim.183) | copy-start | bytes 1572868
  180.6 20.3 %copy-start.2 = (f32[2,512,1024]{2,1,0:T(8,128)}, f32[2,512,1024]{2,1,0:T(8,128)S(1)}, u32[]{:S(2)}) copy-start(f32[2,512,1024]{2,1,0:T(8,128)S(1)} %get-tuple-element.176) | copy-start | bytes 12582916
  180.8 17.7 %copy-start.10 = (pred[4,128,1024]{2,1,0:T(8,128)(4,1)}, pred[4,128,1024]{2,1,0:T(8,128)(4,1)S(1)}, u32[]{:S(2)}) copy-start(pred[4,128,1024]{2,1,0:T(8,128)(4,1)S(1)} %broadcast_in_dim.177) | copy-start | bytes 1572868
  181.9 16.6 %copy-start.3 = (f32[2,512,1024]{2,1,0:T(8,128)}, f32[2,512,1024]{2,1,0:T(8,128)S(1)}, u32[]{:S(2)}) copy-start(f32[2,512,1024]{2,1,0:T(8,128)S(1)} %get-tuple-element.178) | copy-start | bytes 12582916
  182.1 23.4 %copy-start.11 = (pred[4,128,1024]{2,1,0:T(8,128)(4,1)}, pred[4,128,1024]{2,1,0:T(8,128)(4,1)S(1)}, u32[]{:S(2)}) copy-start(pred[4,128,1024]{2,1,0:T(8,128)(4,1)S(1)} %broadcast_in_dim.189) | copy-start | bytes 1572868
  183.3 22.2 %copy-start.4 = (f32[2,512,1024]{2,1,0:T(8,128)}, f32[2,512,1024]{2,1,0:T(8,128)S(1)}, u32[]{:S(2)}) copy-start(f32[2,512,1024]{2,1,0:T(8,128)S(1)} %get-tuple-element.172) | copy-start | bytes 12582916
  249.0 7.6 %copy-start.20 = (f32[1024,256]{1,0:T(8,128)S(1)}, f32[1024,256]{1,0:T(8,128)}, u32[]{:S(2)}) copy-start(f32[1024,256]{1,0:T(8,128)} %copy.173) | copy-start | bytes 3145732
  259.6 8.4 %collective-permute-start.6 = (bf16[1,128,512]{2,1,0:T(8,128)(2,1)S(1)}, bf16[1,128,512]{2,1,0:T(8,128)(2,1)S(1)}, u32[]{:S(2)}, u32[]{:S(2)}) collective-permute-start(bf16[1,128,512]{2,1,0:T(8,128)(2,1)S(1)} %slice.314), channel_id=1, source_target_pairs={{64,0},{66,2},{68,4},{70,6},{72,8},{74,10},{76,12},{78,14},{80,16}... | collective-permute-start | bytes 393224 | tf_op jit(solution)/shard_map/ppermute | solution.py:44
  268.3 47.1 %copy-start.8 = (bf16[2,512,1024]{2,1,0:T(8,128)(2,1)S(1)}, bf16[2,512,1024]{2,1,0:T(8,128)(2,1)}, u32[]{:S(2)}) copy-start(bf16[2,512,1024]{2,1,0:T(8,128)(2,1)} %get-tuple-element.156) | copy-start | bytes 6291460
  268.3 47.1 %copy-start.18 = (bf16[1024,256]{0,1:T(8,128)(2,1)S(1)}, bf16[1024,256]{0,1:T(8,128)(2,1)}, u32[]{:S(2)}) copy-start(bf16[1024,256]{0,1:T(8,128)(2,1)} %copy.223) | copy-start | bytes 1572868
  268.3 44.0 %collective-permute-start.7 = (bf16[16,128,512]{2,1,0:T(8,128)(2,1)S(1)}, bf16[16,128,512]{2,1,0:T(8,128)(2,1)S(1)}, u32[]{:S(2)}, u32[]{:S(2)}) collective-permute-start(bf16[16,128,512]{2,1,0:T(8,128)(2,1)S(1)} %slice.309), channel_id=1, source_target_pairs={{32,0},{34,2},{36,4},{38,6},{40,8},{42,10},{44,12},{46,14},{48,16}... | collective-permute-start | bytes 6291464 | tf_op jit(solution)/shard_map/ppermute | solution.py:44
  313.4 18.2 %collective-permute-start.8 = (bf16[8,128,512]{2,1,0:T(8,128)(2,1)S(1)}, bf16[8,128,512]{2,1,0:T(8,128)(2,1)S(1)}, u32[]{:S(2)}, u32[]{:S(2)}) collective-permute-start(bf16[8,128,512]{2,1,0:T(8,128)(2,1)S(1)} %slice.310), channel_id=1, source_target_pairs={{16,0},{18,2},{20,4},{22,6},{24,8},{26,10},{28,12},{30,14},{32,16}... | collective-permute-start | bytes 3145736 | tf_op jit(solution)/shard_map/ppermute | solution.py:44
  315.4 17.9 %copy-start.7 = (bf16[2,512,1024]{2,1,0:T(8,128)(2,1)S(1)}, bf16[2,512,1024]{2,1,0:T(8,128)(2,1)}, u32[]{:S(2)}) copy-start(bf16[2,512,1024]{2,1,0:T(8,128)(2,1)} %get-tuple-element.157) | copy-start | bytes 6291460
  315.4 17.9 %copy-start.16 = (bf16[1024,256]{0,1:T(8,128)(2,1)S(1)}, bf16[1024,256]{0,1:T(8,128)(2,1)}, u32[]{:S(2)}) copy-start(bf16[1024,256]{0,1:T(8,128)(2,1)} %copy.224) | copy-start | bytes 1572868
  316.3 17.9 %copy-start.6 = (bf16[2,512,1024]{2,1,0:T(8,128)(2,1)S(1)}, bf16[2,512,1024]{2,1,0:T(8,128)(2,1)}, u32[]{:S(2)}) copy-start(bf16[2,512,1024]{2,1,0:T(8,128)(2,1)} %get-tuple-element.158) | copy-start | bytes 6291460
  316.3 17.9 %copy-start.13 = (bf16[1024,256]{0,1:T(8,128)(2,1)S(1)}, bf16[1024,256]{0,1:T(8,128)(2,1)}, u32[]{:S(2)}) copy-start(bf16[1024,256]{0,1:T(8,128)(2,1)} %copy.225) | copy-start | bytes 1572868
  332.0 12.6 %collective-permute-start.9 = (bf16[4,128,512]{2,1,0:T(8,128)(2,1)S(1)}, bf16[4,128,512]{2,1,0:T(8,128)(2,1)S(1)}, u32[]{:S(2)}, u32[]{:S(2)}) collective-permute-start(bf16[4,128,512]{2,1,0:T(8,128)(2,1)S(1)} %slice.311), channel_id=1, source_target_pairs={{8,0},{10,2},{12,4},{14,6},{16,8},{18,10},{20,12},{22,14},{24,16},... | collective-permute-start | bytes 1572872 | tf_op jit(solution)/shard_map/ppermute | solution.py:44
  334.2 12.8 %copy-start.5 = (bf16[2,512,1024]{2,1,0:T(8,128)(2,1)S(1)}, bf16[2,512,1024]{2,1,0:T(8,128)(2,1)}, u32[]{:S(2)}) copy-start(bf16[2,512,1024]{2,1,0:T(8,128)(2,1)} %get-tuple-element.159) | copy-start | bytes 6291460
  334.2 12.8 %copy-start.15 = (bf16[1024,256]{0,1:T(8,128)(2,1)S(1)}, bf16[1024,256]{0,1:T(8,128)(2,1)}, u32[]{:S(2)}) copy-start(bf16[1024,256]{0,1:T(8,128)(2,1)} %copy.226) | copy-start | bytes 1572868
  335.1 12.8 %copy-start.27 = (bf16[2,512,128]{1,2,0:T(8,128)(2,1)S(1)}, bf16[2,512,128]{1,2,0:T(8,128)(2,1)}, u32[]{:S(2)}) copy-start(bf16[2,512,128]{1,2,0:T(8,128)(2,1)} %multiply_convert_fusion.4) | copy-start | bytes 786436
  335.1 12.8 %copy-start.35 = (bf16[128,2,128]{2,1,0:T(2,128)(2,1)S(1)}, bf16[128,2,128]{2,1,0:T(2,128)(2,1)}, u32[]{:S(2)}) copy-start(bf16[128,2,128]{2,1,0:T(2,128)(2,1)} %reshape_reshape.21) | copy-start | bytes 196612
  345.5 8.6 %collective-permute-start.10 = (bf16[2,128,512]{2,1,0:T(8,128)(2,1)}, bf16[2,128,512]{2,1,0:T(8,128)(2,1)}, u32[]{:S(2)}, u32[]{:S(2)}) collective-permute-start(bf16[2,128,512]{2,1,0:T(8,128)(2,1)} %slice.312), channel_id=1, source_target_pairs={{4,0},{6,2},{8,4},{10,6},{12,8},{14,10},{16,12},{18,14},{20,16},{2... | collective-permute-start | bytes 786440 | tf_op jit(solution)/shard_map/ppermute | solution.py:44
  355.1 41.6 %copy-start.44 = (bf16[128,2048]{1,0:T(8,128)(2,1)S(1)}, bf16[128,2048]{1,0:T(8,128)(2,1)}, u32[]{:S(2)}) copy-start(bf16[128,2048]{1,0:T(8,128)(2,1)} %param.38) | copy-start | bytes 1572868
  355.1 3.4 collective-permute-start.11
  421.8 24.0 %all-to-all-start.5 = ((bf16[32,2,128,64]{2,1,3,0:T(2,128)(2,1)}), bf16[32,2,128,64]{2,1,3,0:T(2,128)(2,1)S(1)}, u32[]{:S(2)}, u32[]{:S(2)}) async-start(bf16[32,2,128,64]{2,1,3,0:T(2,128)(2,1)} %copy.191), calls=%async_computation.5 | async-start | bytes 2097152 | tf_op jit(solution)/shard_map/all_to_all | solution.py:63
  445.8 44.2 %all-to-all-start.2 = ((f32[2,128,2048]{2,1,0:T(8,128)}), f32[2,128,2048]{2,1,0:T(8,128)}, u32[]{:S(2)}, u32[]{:S(2)}) async-start(f32[2,128,2048]{2,1,0:T(8,128)} %bitcast.186), calls=%async_computation.2 | async-start | bytes 4194304 | tf_op jit(solution)/shard_map/all_to_all | solution.py:55
  (18 other events, 44.9 us)
Sparse Core Ops, SparseCore 0:
  396.8 102.4 all-gather.1
where the time goes:
time: 521 us; the launch traced here: 512 us
  waiting for transfers between devices  196 us (38%)
  local copies, waits for them, and re-layouts  78.1 us (15%)
  starting transfers between devices  65.6 us (13%)
  blocking collectives  57.9 us (11%)
  matrix products  54.3 us (10%)
  other arithmetic  44.4 us (9%)
  between operations  15.7 us (3%)
    ppermute x12, waiting for transfers between devices, from_behind(): return lax.ppermute(array, axis, pairs)  126 us
    ppermute x12, starting transfers between devices, from_behind(): return lax.ppermute(array, axis, pairs)  45.5 us
    all_to_all x1, blocking collectives, sent_together(): lax.all_to_all(both, axis, split_axis=split_dim, concat_axis=concat_dim,...  35.9 us
    all_to_all x1, waiting for transfers between devices, summed_on_arrival(): lax.all_to_all(pieces, axis, split_axis=0, concat_axis=0, tiled=True)  34.7 us
    unnamed x114, local copies, waits for them, and re-layouts  22.7 us
    convert_element_type x2, other arithmetic, local(): score_grad.astype(jnp.bfloat16)  19.6 us
    all_to_all x1, blocking collectives, from_everyone(): return lax.all_to_all(copies, axis, split_axis=0, concat_axis=0, tiled=True)  17.5 us
    all_to_all x1, waiting for transfers between devices, moved_by_axis(): result = lax.all_to_all(result, axes[k], k, k, tiled=True)  16.1 us
  transfers between devices with their start and end apart: 16, of which 15 were waited for; matrix products, arithmetic and copies ran while one was open for 9% of the time, Pallas kernels for 0%

commit v1 on v0

v1 whole, which is shorter than its diff:
```python
import math

import jax
import jax.numpy as jnp
from jax import lax
from jax.experimental import pallas as pl
from jax.experimental.pallas import tpu as pltpu
from jax.sharding import Mesh
from jax.sharding import PartitionSpec as P

F32 = jnp.float32
BF16 = jnp.bfloat16
Y, ZH, X, CORE, ZL = "seq_0", "seq_1", "seq_2", "seq_3", "tp"
SEQ = (Y, ZH, X, CORE)
MESH = pl.DeviceIdType.MESH

HEAD = 128
GROUP = 4
WINDOW = 4096
CHUNKS = 8
BAND = 4
FEATS = 4096
SCALE = 1.0 / math.sqrt(HEAD)
SCALE2 = SCALE * math.log2(math.e)
MASKED = -1e30
QROWS = 256
KROWS = 128
NSEM = 96
NLOCAL = 24


def key_chunks(cq):
    return list(range(max(0, cq - BAND), cq + 1))


TILE_AT = [KROWS * sum(len(key_chunks(c)) for c in range(cq)) for cq in range(CHUNKS)]
TILE_ROWS = KROWS * sum(len(key_chunks(c)) for c in range(CHUNKS))

UNIT_KV = (2, 4, 2, 16, HEAD)
UNIT_W = (2, 64, HEAD)


def reduce_buffers(name, unit):
    half = unit[1:]
    return {
        name + "_far": ((2, 4) + unit, BF16),
        name + "_rfar": ((2, 2, 2) + unit, BF16),
        name + "_near": ((2, 2, 4) + unit, BF16),
        name + "_rnear": ((2, 2, 4) + unit, BF16),
        name + "_row": ((2, 4) + unit, F32),
        name + "_far2": ((2,) + unit, BF16),
        name + "_rfar2": ((2, 2) + half, BF16),
        name + "_near2": ((2, 2) + unit, BF16),
        name + "_rnear2": ((2, 2) + unit, BF16),
    }


BUFFERS = {
    "kv": ((2, 4, 4) + UNIT_KV, BF16),
    "qg": ((2, CHUNKS, 4, GROUP, 16, HEAD), BF16),
    "kpb": ((32, KROWS, 128), F32),
    "e": ((4, TILE_ROWS, QROWS), F32),
    "dp": ((4, TILE_ROWS, QROWS), F32),
    "st": ((3, 4, CHUNKS, QROWS), F32),
    "ss": ((3, CHUNKS, QROWS), F32),
    "sr": ((3, CHUNKS, QROWS), F32),
    "fac": ((4, CHUNKS, QROWS), F32),
    "delta": ((CHUNKS, QROWS), F32),
    "acc": ((2, 4) + UNIT_KV, F32),
    "dqt": ((CHUNKS, HEAD, QROWS), F32),
    "dqf": ((CHUNKS, 2, 2, GROUP, 16, HEAD), F32),
    "dqr": ((CHUNKS, 2, GROUP, 16, HEAD), F32),
    "dqs": ((CHUNKS, GROUP, 16, HEAD), BF16),
    "dqz": ((CHUNKS, GROUP, 16, HEAD), BF16),
    "xg": ((CHUNKS, 2, 16, FEATS), BF16),
    "mat": ((2, FEATS, 2 * HEAD), BF16),
    "d2": ((2, CHUNKS, 2, 16, HEAD), BF16),
    "dd": ((4, CHUNKS, 16, HEAD), BF16),
    "wown": ((2, 4, 4) + UNIT_W, F32),
    "wsend": ((2, 4, 4) + UNIT_W, BF16),
    "wrecv": ((2, 4, 4) + UNIT_W, BF16),
    "wfin": ((2,) + UNIT_W, F32),
    "wswap": ((2, 64, HEAD), F32),
    "igs": ((128, FEATS // 2), BF16),
    "igr": ((128, FEATS // 2), BF16),
    "igo": ((128, FEATS // 2), F32),
    **reduce_buffers("a", UNIT_KV),
    **reduce_buffers("w", UNIT_W),
}


def dot_tt(a, b):
    return lax.dot_general(a, b, (((1,), (1,)), ((), ())), preferred_element_type=F32)


def dot_nn(a, b):
    return lax.dot_general(a, b, (((1,), (0,)), ((), ())), preferred_element_type=F32)


def dot_tn(a, b):
    return lax.dot_general(a, b, (((0,), (0,)), ((), ())), preferred_element_type=F32)


def stack_rows(parts):
    return parts[0] if len(parts) == 1 else jnp.concatenate(parts, axis=0)


def kernel(
    q_in, g_in, k_in, v_in, x_in, mk_in, mv_in, kp_in, qp_in, dq_out, ig_out, w_out, *scratch
):
    ssem, rsem, lsem = scratch[-3:]
    b = dict(zip(BUFFERS, scratch[:-3]))
    y, zh, x, core, zl = (lax.axis_index(a) for a in (Y, ZH, X, CORE, ZL))

    def turn(i, by):
        return lax.rem(i + by, 4)

    z = 2 * zh + zl
    zp, zm = turn(z, 1), turn(z, 3)
    zp_h, zp_l = lax.div(zp, 2), lax.rem(zp, 2)
    zm_h, zm_l = lax.div(zm, 2), lax.rem(zm, 2)
    oh, oc, ol = 1 - zh, 1 - core, 1 - zl
    d_zh, d_core, d_tp = {ZH: oh}, {CORE: oc}, {ZL: ol}
    d_zp, d_zm = {ZH: zp_h, ZL: zp_l}, {ZH: zm_h, ZL: zm_l}
    step_of = {a: ({a: turn(i, 1)}, {a: turn(i, 3)}) for a, i in ((X, x), (Y, y))}
    qi, pi = (y, x), (x, y)
    q_to = (step_of[Y], step_of[X])
    p_to = (step_of[X], step_of[Y])

    names = {}
    pending = []

    def remote(name, src, dst, dev):
        i = names.setdefault(name, len(names))
        return pltpu.make_async_remote_copy(
            src_ref=src,
            dst_ref=dst,
            send_sem=ssem.at[i],
            recv_sem=rsem.at[i],
            device_id=dev,
            device_id_type=MESH,
        )

    def send(name, src, dst, dev):
        remote(name, src, dst, dev).start()
        pending.append((name, src, dst, dev))

    def arrived(name, dst):
        remote(name, dst, dst, d_core).wait_recv()

    local_names = {}

    def local(name, src, dst):
        i = local_names.setdefault(name, len(local_names))
        return pltpu.make_async_copy(src, dst, lsem.at[i])

    def lanes(start, width=128):
        return pl.ds(pl.multiple_of(start, 128), width)

    kv, qg, xg, mat = b["kv"], b["qg"], b["xg"], b["mat"]
    own_kv = []
    for h in range(2):
        for t, ref in enumerate((k_in, v_in)):
            own_kv.append(
                local(
                    ("kv", h, t),
                    ref.at[pl.ds(4 * h, 4), :, lanes(zh * HEAD)],
                    kv.at[h, qi[h], pi[h], t, :, zh],
                )
            )
    own_q = []
    for t, ref in enumerate((q_in, g_in)):
        for g in range(GROUP):
            own_q.append(
                local(
                    ("qg", t, g),
                    ref.at[:, :, lanes(zh * GROUP * HEAD + g * HEAD)],
                    qg.at[t, :, 2 * zh + core, g],
                )
            )
    own_x = local("x", x_in, xg.at[:, zh, :, lanes(zl * (FEATS // 2), FEATS // 2)])
    own_m = [local("mk", mk_in, mat.at[0]), local("mv", mv_in, mat.at[1])]
    for c in own_kv + own_q:
        c.start()

    barrier = pltpu.get_barrier_semaphore()
    peers = [d_zh, d_core, *step_of[X], *step_of[Y], d_zp, d_zm]
    for dev in peers:
        pl.semaphore_signal(barrier, inc=1, device_id=dev, device_id_type=MESH)
    pl.semaphore_wait(barrier, len(peers))

    for h in range(2):
        for t, ref in enumerate((k_in, v_in)):
            send(
                ("zkv", h, t),
                ref.at[pl.ds(4 * h, 4), :, lanes(oh * HEAD)],
                kv.at[h, qi[h], pi[h], t, :, zh],
                d_zh,
            )
    for t, ref in enumerate((q_in, g_in)):
        for g in range(GROUP):
            send(
                ("qz", t, g),
                ref.at[:, :, lanes(oh * GROUP * HEAD + g * HEAD)],
                qg.at[t, :, 2 * zh + core, g],
                d_zh,
            )
    for t, ref in enumerate((q_in, g_in)):
        for g in range(GROUP):
            send(
                ("qc", t, g),
                ref.at[:, :, lanes(zh * GROUP * HEAD + g * HEAD)],
                qg.at[t, :, 2 * zh + core, g],
                d_core,
            )
    for c in own_kv:
        c.wait()

    for h in range(2):
        for t in range(2):
            arrived(("zkv", h, t), kv.at[h, qi[h], pi[h], t, :, oh])
        for side in range(2):
            unit = kv.at[h, qi[h], pi[h]]
            send(("p", h, side), unit, unit, p_to[h][side])
    own_x.start()
    for c in own_m:
        c.start()
    dqt = b["dqt"]
    dqt[...] = jnp.zeros(dqt.shape, F32)
    kpt = kp_in[...].T
    for i in range(32):
        b["kpb"][i] = jnp.broadcast_to(kpt[:, i : i + 1], (KROWS, 128))
    for h in range(2):
        for side in range(2):
            src = kv.at[h, qi[h], turn(pi[h], 3 if side == 0 else 1)]
            arrived(("p", h, side), src)
            send(("pf", h, side), src.at[side], src.at[side], p_to[h][side])
    for h in range(2):
        for side in range(2):
            arrived(("pf", h, side), kv.at[h, qi[h], turn(pi[h], 2), side])
        for side in range(2):
            row = kv.at[h, qi[h]]
            send(("q", h, side), row, row, q_to[h][side])

    for t in range(2):
        for g in range(GROUP):
            arrived(("qz", t, g), qg.at[t, :, 2 * oh + core, g])
        src = qg.at[t, :, 2 * oh + core]
        send(("qf", t), src, src, d_core)
    half_feats = FEATS // 2
    quarter_feats = FEATS // 4
    mine = xg.at[:, zh, :, lanes(zl * half_feats, half_feats)]
    send("x+", x_in, mine, d_zp)
    send("x-", x_in, mine, d_zm)
    for c in own_q:
        c.wait()
    for t in range(2):
        for g in range(GROUP):
            arrived(("qc", t, g), qg.at[t, :, 2 * zh + oc, g])
        arrived(("qf", t), qg.at[t, :, 2 * oh + oc])

    def queries(t, cq):
        return qg[t, cq].reshape(QROWS, HEAD)

    def keys(t, at, cks):
        return stack_rows(
            [kv[ck // 4, at[ck // 4], :, t, ck % 4].reshape(KROWS, HEAD) for ck in cks]
        )

    def row_far(h, side):
        return kv.at[h, turn(qi[h], 2), pl.ds(2 * side, 2)]

    def row_near(h, side):
        return kv.at[h, turn(qi[h], 3 if side == 0 else 1)]

    def forward(h, side):
        src = row_near(h, side).at[pl.ds(2 * side, 2)]
        return ("qfar", h, side), src, src, q_to[h][side]

    st, e_ref, dp_ref = b["st"], b["e"], b["dp"]

    def first_pass(s, carry):
        late = lax.div(s, 2)
        off = (1 - late) * s + late * (5 - s)

        @pl.when(s == 1)
        def _():
            for h in range(2):
                for side in range(2):
                    arrived(("q", h, side), row_near(h, side))
                    remote(*forward(h, side)).start()

        @pl.when(s == 3)
        def _():
            for h in range(2):
                for side in range(2):
                    arrived(("qfar", h, side), row_far(h, side))

        at = (turn(y, off), turn(x, off))
        for cq in range(CHUNKS):
            cks = key_chunks(cq)
            rows = pl.ds(TILE_AT[cq], KROWS * len(cks))
            score = dot_tt(keys(0, at, cks), queries(0, cq)) * SCALE2
            qpos = qp_in[cq : cq + 1, :]
            parts = []
            for n, ck in enumerate(cks):
                part = score[n * KROWS : (n + 1) * KROWS]
                if ck == cq or ck == cq - BAND:
                    kpb = b["kpb"][ck // 4 * 16 + at[ck // 4] * 4 + ck % 4]
                    kpos = jnp.concatenate([kpb, kpb], axis=1)
                    seen = kpos <= qpos if ck == cq else kpos > qpos - WINDOW
                    part = jnp.where(seen, part, MASKED)
                parts.append(part)
            score = stack_rows(parts)
            top = jnp.max(score, axis=0, keepdims=True)
            expo = jnp.exp2(score - top)
            dprob = dot_tt(keys(1, at, cks), queries(1, cq))
            e_ref[off, rows, :] = expo
            dp_ref[off, rows, :] = dprob
            st[0, off, cq : cq + 1, :] = top
            st[1, off, cq : cq + 1, :] = jnp.sum(expo, axis=0, keepdims=True)
            st[2, off, cq : cq + 1, :] = jnp.sum(expo * dprob, axis=0, keepdims=True)
        return carry

    lax.fori_loop(0, 4, first_pass, 0)
    for h in range(2):
        for side in range(2):
            pending.append(forward(h, side))

    ss, sr = b["ss"], b["sr"]
    top_l = jnp.max(st[0], axis=0)
    fac_l = jnp.exp2(st[0] - top_l[None])
    sum_l = jnp.sum(st[1] * fac_l, axis=0)
    wgt_l = jnp.sum(st[2] * fac_l, axis=0)
    ss[0] = top_l
    ss[1] = sum_l
    ss[2] = wgt_l
    send("stat", ss, sr, d_core)
    arrived("x+", xg.at[:, zm_h, :, lanes(zm_l * half_feats, half_feats)])
    src = xg.at[:, zm_h, :, lanes(zm_l * half_feats, quarter_feats)]
    send("xf+", src, src, d_zp)
    arrived("x-", xg.at[:, zp_h, :, lanes(zp_l * half_feats, half_feats)])
    src = xg.at[:, zp_h, :, lanes(zp_l * half_feats + quarter_feats, quarter_feats)]
    send("xf-", src, src, d_zm)
    arrived("stat", sr)
    top = jnp.maximum(top_l, sr[0])
    mine_f = jnp.exp2(top_l - top)
    other_f = jnp.exp2(sr[0] - top)
    total = sum_l * mine_f + sr[1] * other_f
    b["delta"][...] = (wgt_l * mine_f + sr[2] * other_f) / total
    b["fac"][...] = fac_l * (mine_f / total)[None]

    def reducer(name, row):
        far, rfar = b[name + "_far"], b[name + "_rfar"]
        near, rnear = b[name + "_near"], b[name + "_rnear"]
        rows = b[name + "_row"]
        far2, rfar2 = b[name + "_far2"], b[name + "_rfar2"]
        near2, rnear2 = b[name + "_near2"], b[name + "_rnear2"]

        def far_copy(h, side):
            return (
                (name, "far", h, side),
                far.at[h, pl.ds(2 * side, 2)],
                rfar.at[h, side],
                q_to[h][side],
            )

        def near_copy(h, side):
            return (name, "near", h, side), near.at[h, side], rnear.at[h, side], q_to[h][side]

        def start_far():
            for h in range(2):
                far[h] = row(h, turn(qi[h], 2)).astype(BF16)
                for side in range(2):
                    remote(*far_copy(h, side)).start()

        def start_near(side):
            for h in range(2):
                value = row(h, turn(qi[h], 1 if side == 0 else 3))
                arrived((name, "far", h, side), rfar.at[h, side])
                lo, hi = value[:2], value[2:]
                if side == 0:
                    lo = lo + rfar[h, side].astype(F32)
                else:
                    hi = hi + rfar[h, side].astype(F32)
                near[h, side, :2] = lo.astype(BF16)
                near[h, side, 2:] = hi.astype(BF16)
                remote(*near_copy(h, side)).start()

        def note_sends():
            for h in range(2):
                for side in range(2):
                    pending.append(far_copy(h, side))
                    pending.append(near_copy(h, side))

        def own_row():
            for h in range(2):
                for side in range(2):
                    arrived((name, "near", h, side), rnear.at[h, side])
                rows[h] = row(h, qi[h]) + rnear[h, 0].astype(F32) + rnear[h, 1].astype(F32)
                far2[h] = rows[h, turn(pi[h], 2)].astype(BF16)
                for side in range(2):
                    send(
                        (name, "far2", h, side),
                        far2.at[h, side],
                        rfar2.at[h, side],
                        p_to[h][side],
                    )

        def near_unit():
            for h in range(2):
                for side in range(2):
                    arrived((name, "far2", h, side), rfar2.at[h, side])
                    at = turn(pi[h], 1 if side == 0 else 3)
                    near2[h, side, 1 - side] = rows[h, at, 1 - side].astype(BF16)
                    near2[h, side, side] = (
                        rows[h, at, side] + rfar2[h, side].astype(F32)
                    ).astype(BF16)
                    send(
                        (name, "near2", h, side), near2.at[h, side], rnear2.at[h, side], p_to[h][side]
                    )

        def final(h):
            for side in range(2):
                arrived((name, "near2", h, side), rnear2.at[h, side])
            return rows[h, pi[h]] + rnear2[h, 0].astype(F32) + rnear2[h, 1].astype(F32)

        return start_far, start_near, note_sends, own_row, near_unit, final

    acc = b["acc"]
    start_far, start_near, note_sends, own_row, near_unit, final = reducer(
        "a", lambda h, at: acc[h]
    )

    fac, delta = b["fac"], b["delta"]

    def second_pass(s, carry):
        late = lax.div(s, 2)
        off = (1 - late) * (2 + s) + late * (3 - s)
        at = (turn(y, off), turn(x, off))
        for cq in range(CHUNKS):
            cks = key_chunks(cq)
            rows = pl.ds(TILE_AT[cq], KROWS * len(cks))
            prob = e_ref[off, rows, :] * fac[off, cq : cq + 1, :]
            dscore = (prob * (dp_ref[off, rows, :] - delta[cq : cq + 1, :])).astype(BF16)
            grads = (dot_nn(dscore, queries(0, cq)), dot_nn(prob.astype(BF16), queries(1, cq)))
            for t in range(2):
                for n, ck in enumerate(cks):
                    part = grads[t][n * KROWS : (n + 1) * KROWS].reshape(4, 2, 16, HEAD)
                    if ck == cq:
                        acc[ck // 4, :, t, ck % 4] = part
                    else:
                        acc[ck // 4, :, t, ck % 4] = acc[ck // 4, :, t, ck % 4] + part
            dqt[cq] = dqt[cq] + dot_tn(keys(0, at, cks), dscore)

        @pl.when(s == 0)
        def _():
            start_far()

        @pl.when(s == 1)
        def _():
            start_near(1)

        @pl.when(s == 2)
        def _():
            start_near(0)

        return carry

    lax.fori_loop(0, 4, second_pass, 0)
    note_sends()

    dqf, dqr, dqs, dqz = b["dqf"], b["dqr"], b["dqs"], b["dqz"]
    for cq in range(CHUNKS):
        dqf[cq] = (dqt[cq].T * SCALE).reshape(2, 2, GROUP, 16, HEAD)
    send("dqc", dqf.at[:, :, oc], dqr, d_core)
    own_row()
    arrived("dqc", dqr)
    dqs[...] = (dqf[:, oh, core] + dqr[:, oh]).astype(BF16)
    send("dqz", dqs, dqz, d_zh)
    dq_out[zh] = (dqf[:, zh, core] + dqr[:, zh]).astype(BF16)
    near_unit()
    own_x.wait()
    for c in own_m:
        c.wait()
    far_h = 1 - zh
    arrived("xf+", xg.at[:, far_h, :, lanes(zl * half_feats, quarter_feats)])
    arrived("xf-", xg.at[:, far_h, :, lanes(zl * half_feats + quarter_feats, quarter_feats)])
    arrived("dqz", dqz)
    dq_out[oh] = dqz[...]
    d2, dd = b["d2"], b["dd"]
    for h in range(2):
        value = final(h)
        d2[0, 4 * h : 4 * h + 4] = (value[0] * SCALE).astype(BF16)
        d2[1, 4 * h : 4 * h + 4] = value[1].astype(BF16)
    for t in range(2):
        send(("dz", t), d2.at[t, :, oh], dd.at[2 * t + zh], d_zh)
        dd[2 * t + zh] = d2[t, :, zh]

    wown, wsend, wrecv = b["wown"], b["wsend"], b["wrecv"]
    grad_cols = jnp.concatenate([d2[0].reshape(256, HEAD), d2[1].reshape(256, HEAD)], axis=1)

    def weight_block(i, carry):
        wx = lax.rem(i, 4)
        wz = lax.rem(lax.div(i, 4), 2)
        wy = lax.div(i, 8)
        block = xg[:, :, :, lanes(i * 128)].reshape(256, 128)
        part = dot_tn(block, grad_cols)
        for h, (wq, wp) in enumerate(((wy, wx), (wx, wy))):
            cols = part[:, h * HEAD : (h + 1) * HEAD]
            wown[h, wq, wp, wz] = jnp.where(core == 0, cols[:64], cols[64:])
            wsend[h, wq, wp, wz] = jnp.where(core == 0, cols[64:], cols[:64]).astype(BF16)
        return carry

    lax.fori_loop(0, 32, weight_block, 0)
    send("wc", wsend, wrecv, d_core)

    igs, igr, igo = b["igs"], b["igr"], b["igo"]
    for t in range(2):
        arrived(("dz", t), dd.at[2 * t + oh])
    dk_dv = [
        jnp.concatenate([dd[2 * t].reshape(128, HEAD), dd[2 * t + 1].reshape(128, HEAD)], axis=1)
        for t in range(2)
    ]

    def input_block(base, out):
        def body(i, carry):
            rows = pl.ds(pl.multiple_of(base + i * 512, 512), 512)
            part = dot_tt(dk_dv[0], mat[0, rows, :]) + dot_tt(dk_dv[1], mat[1, rows, :])
            out[:, lanes(i * 512, 512)] = part.astype(out.dtype)
            return carry

        lax.fori_loop(0, 4, body, 0)

    input_block(ol * half_feats, igs)
    send("ig", igs, igr, d_tp)

    arrived("wc", wrecv)
    w_far, w_near, w_note, w_own, w_unit, w_final = reducer(
        "w", lambda h, at: wown[h, at] + wrecv[h, at].astype(F32)
    )
    w_far()
    input_block(zl * half_feats, igo)
    w_near(0)
    w_near(1)
    w_note()
    w_own()
    w_unit()
    wfin, wswap = b["wfin"], b["wswap"]
    for h in range(2):
        wfin[h] = w_final(h)
    for h in range(2):
        send(("ws", h), wfin.at[h, oh], wswap.at[h], d_zh)
        w_out[h, zh] = wfin[h, zh]
    arrived("ig", igr)
    ig_out[...] = (igo[...] + igr[...].astype(F32)).astype(BF16)
    for h in range(2):
        arrived(("ws", h), wswap.at[h])
        w_out[h, oh] = wswap[h]

    for copy in pending:
        remote(*copy).wait_send()
    assert len(names) <= NSEM and len(local_names) <= NLOCAL


def local_step(q, k, v, g, x, mk, mv, placement):
    core = lax.axis_index(CORE)
    pos = (
        (jnp.arange(64, dtype=jnp.int32) * 128)[:, None, None]
        + placement[:, :, None] * 2
        + jnp.arange(2, dtype=jnp.int32)
    ).astype(F32)
    pos = pos.reshape(CHUNKS, 8, 4, 2, 4, 2, 2)
    kpos = lax.dynamic_index_in_dim(pos, core, 5, keepdims=False)
    kpos = kpos.reshape(2, 4, 8, 4, 2, 4, 2)
    half_a = kpos[0].transpose(2, 0, 4, 3, 1, 5)
    half_b = kpos[1].transpose(4, 0, 2, 3, 1, 5)
    kp = jnp.stack([half_a, half_b]).reshape(32, KROWS)
    qpos = lax.dynamic_index_in_dim(pos, lax.axis_index(Y), 2, keepdims=False)
    qpos = lax.dynamic_index_in_dim(qpos, lax.axis_index(X), 3, keepdims=False)
    qpos = qpos.transpose(0, 2, 3, 1, 4).reshape(CHUNKS, 4, 1, 16)
    qp = jnp.broadcast_to(qpos, (CHUNKS, 4, GROUP, 16)).reshape(CHUNKS, QROWS)

    anywhere = pl.BlockSpec(memory_space=pl.ANY)
    vmem = pl.BlockSpec(memory_space=pltpu.VMEM)
    dq, ig, w = pl.pallas_call(
        kernel,
        out_shape=(
            jax.ShapeDtypeStruct((2, CHUNKS, GROUP, 16, HEAD), BF16),
            jax.ShapeDtypeStruct((128, FEATS // 2), BF16),
            jax.ShapeDtypeStruct((2, 2, 64, HEAD), F32),
        ),
        in_specs=[anywhere] * 7 + [vmem] * 2,
        out_specs=(vmem, vmem, vmem),
        scratch_shapes=[pltpu.VMEM(shape, dtype) for shape, dtype in BUFFERS.values()]
        + [
            pltpu.SemaphoreType.DMA((NSEM,)),
            pltpu.SemaphoreType.DMA((NSEM,)),
            pltpu.SemaphoreType.DMA((NLOCAL,)),
        ],
        compiler_params=pltpu.CompilerParams(
            collective_id=0, has_side_effects=True, vmem_limit_bytes=67043328
        ),
    )(
        q.reshape(CHUNKS, 16, -1),
        g.reshape(CHUNKS, 16, -1),
        k.reshape(CHUNKS, 16, -1),
        v.reshape(CHUNKS, 16, -1),
        x.reshape(CHUNKS, 16, -1),
        mk,
        mv,
        kp,
        qp,
    )
    query_grad = dq.transpose(1, 3, 0, 2, 4).reshape(128, -1)
    weights = [w[t].transpose(1, 0, 2).reshape(64, 2 * HEAD) for t in range(2)]
    return (query_grad, ig, weights[0], weights[1])


def solution(mesh):
    torus = Mesh(
        mesh.devices.reshape(4, 2, 4, 2, mesh.shape["tp"]), ("seq_0", "seq_1", "seq_2", "seq_3", "tp")
    )
    rows = P(SEQ, "tp")
    return jax.shard_map(
        local_step,
        mesh=torus,
        in_specs=(rows, rows, rows, rows, rows, P(None, "tp"), P(None, "tp"), P()),
        out_specs=(rows, rows, rows, rows),
        check_vma=False,
    )
```

time: 521 us -> 99 us (0.19); the launches traced: 512 us -> 98.6 us
  waiting for transfers between devices: 196 us -> 0 us
  Pallas kernels: 0 us -> 88.6 us
  local copies, waits for them, and re-layouts: 78.1 us -> 8.39 us
  starting transfers between devices: 65.6 us -> 0 us
  blocking collectives: 57.9 us -> 0 us
  matrix products: 54.3 us -> 0 us
  other arithmetic: 44.4 us -> 0.96 us
  between operations: 15.7 us -> 0.73 us
    ppermute x12 -> x0, waiting for transfers between devices: 126 us -> none  [from_behind(): return lax.ppermute(array, axis, pairs)]
    pallas_call x0 -> x1, Pallas kernels: none -> 88.6 us  [local_step(): pl.pallas_call(kernel, out_shape=(jax.ShapeDtypeStruct((2, CHUNKS, GROUP,...]
    all_to_all x3 -> x0, waiting for transfers between devices: 63.4 us -> none  [the longest x1 34.7 us: summed_on_arrival(): lax.all_to_all(pieces, axis, split_axis=0, concat_axis=0, tiled=True)]
    all_to_all x3 -> x0, blocking collectives: 57.9 us -> none  [the longest x1 35.9 us: sent_together(): lax.all_to_all(both, axis, split_axis=split_dim, concat_axis=concat_dim,...]
    dot_general x28 -> x0, matrix products: 54.3 us -> none  [the longest x5 15 us: scores_for(): jnp.einsum('gqd,kgd->gqk', grad_seq, values_here, preferred_element_type=...]
    ppermute x12 -> x0, starting transfers between devices: 45.5 us -> none  [from_behind(): return lax.ppermute(array, axis, pairs)]
    all_to_all x3 -> x0, starting transfers between devices: 20.1 us -> none  [the longest x1 11.4 us: sent_together(): lax.all_to_all(both, axis, split_axis=split_dim, concat_axis=concat_dim,...]
    unnamed x114 -> x3, local copies, waits for them, and re-layouts: 22.7 us -> 2.77 us
  transfers between devices with their start and end apart: 16 -> 0, of which waited for: 15 -> 0; matrix products, arithmetic and copies ran while one was open for 9% -> 0% of each run, Pallas kernels for 0% -> 0%
where the time goes in v1:
time: 99 us; the launch traced here: 98.6 us
  Pallas kernels  88.6 us (89%)
  local copies, waits for them, and re-layouts  8.39 us (8%)
    pallas_call x1, Pallas kernels, local_step(): pl.pallas_call(kernel, out_shape=(jax.ShapeDtypeStruct((2, CHUNKS, GROUP,...  88.6 us
    unnamed x3, local copies, waits for them, and re-layouts  2.77 us

profile of v1, /device:TPU:0, one launch (start us, length us, event | category | flops | bytes accessed | tf_op | source)
XLA Modules:
  0.0 98.6 jit_solution(3091180785296690968)
XLA Ops:
  0.7 0.8 multiply_add_fusion
  1.5 0.1 copy.14
  1.6 0.1 add.46
  1.7 0.1 add_convert_fusion
  1.8 0.1 constant_dynamic-slice_fusion
  1.9 0.1 pad_maximum_fusion
  2.0 0.1 copy.17
  2.0 0.1 copy.18
  2.1 0.7 reshape.66.qp_in
  2.9 0.8 copy.16
  3.7 0.3 reshape.65
  4.0 0.7 copy.19.kp_in
  4.7 88.6 %shard_map.111 = (bf16[2,8,4,16,128]{4,3,2,1,0:T(8,128)(2,1)}, bf16[128,2048]{1,0:T(8,128)(2,1)}, f32[2,2,64,128]{3,2,1,0:T(8,128)}) custom-call(bf16[8,16,1024]{2,1,0:T(8,128)(2,1)} %bitcast.45, bf16[8,16,1024]{2,1,0:T(8,128)(2,1)} %bitcast.46, bf16[8,16,256]{2,1,0:T(8,128)(2,1)} %bitcast.48, bf16[8,16,256]{2,1,0:T(8,128)(2,1)} %bitcast.49, ...), custom_call_target="tpu_custom_call" | custom-call | tf_op jit(solution)/shard_map/pallas_call | solution.py:586
  93.3 1.1 %copy.20 = bf16[8,16,2,4,128]{4,3,2,1,0:T(4,128)(2,1)S(1)} copy(bf16[8,16,2,4,128]{4,1,3,0,2:T(8,128)(2,1)} %bitcast.44) | data formatting | bytes 524288 | tf_op jit(solution)/shard_map/transpose | solution.py:615
  94.3 0.9 reshape.67
  95.2 0.9 slice_bitcast_fusion
  96.1 0.7 copy_bitcast_fusion.1
  96.8 1.9 %copy.31 = bf16[128,2048]{1,0:T(8,128)(2,1)} copy(bf16[128,2048]{1,0:T(8,128)(2,1)} %get-tuple-element.21) | data formatting | bytes 1048576
  (4 shorter events, 0.0 us)

commit v2 on v1

--- a/solution.py
+++ b/solution.py
@@ -61,10 +61,10 @@
     "kpb": ((32, KROWS, 128), F32),
     "e": ((4, TILE_ROWS, QROWS), F32),
     "dp": ((4, TILE_ROWS, QROWS), F32),
-    "st": ((3, 4, CHUNKS, QROWS), F32),
+    "st": ((3, 4, BAND + 1, CHUNKS, QROWS), F32),
     "ss": ((3, CHUNKS, QROWS), F32),
     "sr": ((3, CHUNKS, QROWS), F32),
-    "fac": ((4, CHUNKS, QROWS), F32),
+    "fac": ((4, BAND + 1, CHUNKS, QROWS), F32),
     "delta": ((CHUNKS, QROWS), F32),
     "acc": ((2, 4) + UNIT_KV, F32),
     "dqt": ((CHUNKS, HEAD, QROWS), F32),
@@ -72,7 +72,10 @@
     "dqr": ((CHUNKS, 2, GROUP, 16, HEAD), F32),
     "dqs": ((CHUNKS, GROUP, 16, HEAD), BF16),
     "dqz": ((CHUNKS, GROUP, 16, HEAD), BF16),
+    "kt": ((CHUNKS, HEAD, KROWS), BF16),
+    "qp": ((CHUNKS, QROWS), F32),
     "xg": ((CHUNKS, 2, 16, FEATS), BF16),
+    "xt": ((FEATS, 256), BF16),
     "mat": ((2, FEATS, 2 * HEAD), BF16),
     "d2": ((2, CHUNKS, 2, 16, HEAD), BF16),
     "dd": ((4, CHUNKS, 16, HEAD), BF16),
@@ -105,8 +108,44 @@
     return parts[0] if len(parts) == 1 else jnp.concatenate(parts, axis=0)
 
 
+def positions(rp_in, kpb, qp, y, x, core):
+    slots = rp_in[...].astype(F32).astype(BF16)
+
+    def iota(shape, dim):
+        return lax.broadcasted_iota(jnp.int32, shape, dim)
+
+    def bits(a, at, width):
+        return jnp.bitwise_and(jnp.right_shift(a, at), (1 << width) - 1)
+
+    row, dev = iota((KROWS, 64), 0), iota((KROWS, 64), 1)
+    p, zh, jj = bits(row, 5, 2), bits(row, 4, 1), bits(row, 1, 3)
+    wide = iota((KROWS, 128), 0)
+    inside = (bits(wide, 1, 3) * 128 + bits(wide, 0, 1)).astype(F32)
+    ones = jnp.ones((64, 128), BF16)
+    owner = [
+        [((q * 2 + zh) * 4 + p) * 2 + core == dev for q in range(4)],
+        [((p * 2 + zh) * 4 + q) * 2 + core == dev for q in range(4)],
+    ]
+    for c in range(CHUNKS):
+        block = (dev == jj + 8 * c).astype(F32).astype(BF16)
+        rows = dot_nn(block, slots)
+        for q in range(4):
+            picked = jnp.where(owner[c // 4][q], rows, 0.0).astype(BF16)
+            kpb[c // 4 * 16 + q * 4 + c % 4] = (
+                dot_nn(picked, ones) * 2.0 + (inside + float(c * 1024))
+            )
+
+    dev, lane = iota((64, QROWS), 0), iota((64, QROWS), 1)
+    zh, co, jj = bits(lane, 7, 1), bits(lane, 6, 1), bits(lane, 1, 3)
+    pick = (((y * 2 + zh) * 4 + x) * 2 + co == dev).astype(F32).astype(BF16)
+    slot = dot_nn(slots, pick)
+    here = bits(dev, 0, 3) == jj
+    pos = jnp.where(here, slot * 2.0 + (dev * 128 + bits(lane, 0, 1)).astype(F32), 0.0)
+    qp[...] = jnp.sum(pos.reshape(CHUNKS, 8, QROWS), axis=1)
+
+
 def kernel(
-    q_in, g_in, k_in, v_in, x_in, mk_in, mv_in, kp_in, qp_in, dq_out, ig_out, w_out, *scratch
+    q_in, g_in, k_in, v_in, x_in, mk_in, mv_in, rp_in, dq_out, ig_out, w_out, *scratch
 ):
     ssem, rsem, lsem = scratch[-3:]
     b = dict(zip(BUFFERS, scratch[:-3]))
@@ -227,9 +266,9 @@
         c.start()
     dqt = b["dqt"]
     dqt[...] = jnp.zeros(dqt.shape, F32)
-    kpt = kp_in[...].T
-    for i in range(32):
-        b["kpb"][i] = jnp.broadcast_to(kpt[:, i : i + 1], (KROWS, 128))
+    b["st"][0] = jnp.full(b["st"].shape[1:], MASKED, F32)
+    b["st"][1:] = jnp.zeros((2,) + b["st"].shape[1:], F32)
+    positions(rp_in, b["kpb"], b["qp"], y, x, core)
     for h in range(2):
         for side in range(2):
             src = kv.at[h, qi[h], turn(pi[h], 3 if side == 0 else 1)]
@@ -299,27 +338,26 @@
         at = (turn(y, off), turn(x, off))
         for cq in range(CHUNKS):
             cks = key_chunks(cq)
-            rows = pl.ds(TILE_AT[cq], KROWS * len(cks))
-            score = dot_tt(keys(0, at, cks), queries(0, cq)) * SCALE2
-            qpos = qp_in[cq : cq + 1, :]
-            parts = []
+            scores = dot_tt(keys(0, at, cks), queries(0, cq))
+            dprobs = dot_tt(keys(1, at, cks), queries(1, cq))
+            qpos = b["qp"][cq : cq + 1, :]
             for n, ck in enumerate(cks):
-                part = score[n * KROWS : (n + 1) * KROWS]
+                part = slice(n * KROWS, (n + 1) * KROWS)
+                score, dprob = scores[part] * SCALE2, dprobs[part]
                 if ck == cq or ck == cq - BAND:
                     kpb = b["kpb"][ck // 4 * 16 + at[ck // 4] * 4 + ck % 4]
                     kpos = jnp.concatenate([kpb, kpb], axis=1)
                     seen = kpos <= qpos if ck == cq else kpos > qpos - WINDOW
-                    part = jnp.where(seen, part, MASKED)
-                parts.append(part)
-            score = stack_rows(parts)
-            top = jnp.max(score, axis=0, keepdims=True)
-            expo = jnp.exp2(score - top)
-            dprob = dot_tt(keys(1, at, cks), queries(1, cq))
-            e_ref[off, rows, :] = expo
-            dp_ref[off, rows, :] = dprob
-            st[0, off, cq : cq + 1, :] = top
-            st[1, off, cq : cq + 1, :] = jnp.sum(expo, axis=0, keepdims=True)
-            st[2, off, cq : cq + 1, :] = jnp.sum(expo * dprob, axis=0, keepdims=True)
+                    score = jnp.where(seen, score, MASKED)
+                top = jnp.max(score, axis=0, keepdims=True)
+                expo = jnp.exp2(score - top)
+                rows = pl.ds(TILE_AT[cq] + n * KROWS, KROWS)
+                e_ref[off, rows, :] = expo
+                dp_ref[off, rows, :] = dprob
+                row = slice(cq, cq + 1)
+                st[0, off, cq - ck, row, :] = top
+                st[1, off, cq - ck, row, :] = jnp.sum(expo, axis=0, keepdims=True)
+                st[2, off, cq - ck, row, :] = jnp.sum(expo * dprob, axis=0, keepdims=True)
         return carry
 
     lax.fori_loop(0, 4, first_pass, 0)
@@ -328,10 +366,10 @@
             pending.append(forward(h, side))
 
     ss, sr = b["ss"], b["sr"]
-    top_l = jnp.max(st[0], axis=0)
-    fac_l = jnp.exp2(st[0] - top_l[None])
-    sum_l = jnp.sum(st[1] * fac_l, axis=0)
-    wgt_l = jnp.sum(st[2] * fac_l, axis=0)
+    top_l = jnp.max(st[0], axis=(0, 1))
+    fac_l = jnp.exp2(st[0] - top_l[None, None])
+    sum_l = jnp.sum(st[1] * fac_l, axis=(0, 1))
+    wgt_l = jnp.sum(st[2] * fac_l, axis=(0, 1))
     ss[0] = top_l
     ss[1] = sum_l
     ss[2] = wgt_l
@@ -348,7 +386,7 @@
     other_f = jnp.exp2(sr[0] - top)
     total = sum_l * mine_f + sr[1] * other_f
     b["delta"][...] = (wgt_l * mine_f + sr[2] * other_f) / total
-    b["fac"][...] = fac_l * (mine_f / total)[None]
+    b["fac"][...] = fac_l * (mine_f / total)[None, None]
 
     def reducer(name, row):
         far, rfar = b[name + "_far"], b[name + "_rfar"]
@@ -432,18 +470,25 @@
         "a", lambda h, at: acc[h]
     )
 
-    fac, delta = b["fac"], b["delta"]
+    fac, delta, kt = b["fac"], b["delta"], b["kt"]
 
     def second_pass(s, carry):
         late = lax.div(s, 2)
         off = (1 - late) * (2 + s) + late * (3 - s)
         at = (turn(y, off), turn(x, off))
+        for ck in range(CHUNKS):
+            kt[ck] = keys(0, at, [ck]).T
         for cq in range(CHUNKS):
             cks = key_chunks(cq)
-            rows = pl.ds(TILE_AT[cq], KROWS * len(cks))
-            prob = e_ref[off, rows, :] * fac[off, cq : cq + 1, :]
-            dscore = (prob * (dp_ref[off, rows, :] - delta[cq : cq + 1, :])).astype(BF16)
-            grads = (dot_nn(dscore, queries(0, cq)), dot_nn(prob.astype(BF16), queries(1, cq)))
+            probs, dscores = [], []
+            for n, ck in enumerate(cks):
+                rows = pl.ds(TILE_AT[cq] + n * KROWS, KROWS)
+                prob = e_ref[off, rows, :] * fac[off, cq - ck, cq : cq + 1, :]
+                diff = dp_ref[off, rows, :] - delta[cq : cq + 1, :]
+                probs.append(prob.astype(BF16))
+                dscores.append((prob * diff).astype(BF16))
+            prob, dscore = stack_rows(probs), stack_rows(dscores)
+            grads = (dot_nn(dscore, queries(0, cq)), dot_nn(prob, queries(1, cq)))
             for t in range(2):
                 for n, ck in enumerate(cks):
                     part = grads[t][n * KROWS : (n + 1) * KROWS].reshape(4, 2, 16, HEAD)
@@ -451,7 +496,8 @@
                         acc[ck // 4, :, t, ck % 4] = part
                     else:
                         acc[ck // 4, :, t, ck % 4] = acc[ck // 4, :, t, ck % 4] + part
-            dqt[cq] = dqt[cq] + dot_tn(keys(0, at, cks), dscore)
+            flipped = jnp.concatenate([kt[ck] for ck in cks], axis=1)
+            dqt[cq] = dqt[cq] + dot_nn(flipped, dscore)
 
         @pl.when(s == 0)
         def _():
@@ -474,18 +520,27 @@
     for cq in range(CHUNKS):
         dqf[cq] = (dqt[cq].T * SCALE).reshape(2, 2, GROUP, 16, HEAD)
     send("dqc", dqf.at[:, :, oc], dqr, d_core)
+    own_x.wait()
+    for c in own_m:
+        c.wait()
+    far_h = 1 - zh
+    arrived("xf+", xg.at[:, far_h, :, lanes(zl * half_feats, quarter_feats)])
+    arrived("xf-", xg.at[:, far_h, :, lanes(zl * half_feats + quarter_feats, quarter_feats)])
+    xt = b["xt"]
+
+    def flip_input(i, carry):
+        for n in range(4):
+            at = i * 512 + n * 128
+            xt[pl.ds(pl.multiple_of(at, 128), 128), :] = xg[:, :, :, lanes(at)].reshape(256, 128).T
+        return carry
+
+    lax.fori_loop(0, 8, flip_input, 0)
     own_row()
     arrived("dqc", dqr)
     dqs[...] = (dqf[:, oh, core] + dqr[:, oh]).astype(BF16)
     send("dqz", dqs, dqz, d_zh)
     dq_out[zh] = (dqf[:, zh, core] + dqr[:, zh]).astype(BF16)
     near_unit()
-    own_x.wait()
-    for c in own_m:
-        c.wait()
-    far_h = 1 - zh
-    arrived("xf+", xg.at[:, far_h, :, lanes(zl * half_feats, quarter_feats)])
-    arrived("xf-", xg.at[:, far_h, :, lanes(zl * half_feats + quarter_feats, quarter_feats)])
     arrived("dqz", dqz)
     dq_out[oh] = dqz[...]
     d2, dd = b["d2"], b["dd"]
@@ -501,18 +556,17 @@
     grad_cols = jnp.concatenate([d2[0].reshape(256, HEAD), d2[1].reshape(256, HEAD)], axis=1)
 
     def weight_block(i, carry):
-        wx = lax.rem(i, 4)
-        wz = lax.rem(lax.div(i, 4), 2)
-        wy = lax.div(i, 8)
-        block = xg[:, :, :, lanes(i * 128)].reshape(256, 128)
-        part = dot_tn(block, grad_cols)
-        for h, (wq, wp) in enumerate(((wy, wx), (wx, wy))):
-            cols = part[:, h * HEAD : (h + 1) * HEAD]
-            wown[h, wq, wp, wz] = jnp.where(core == 0, cols[:64], cols[64:])
-            wsend[h, wq, wp, wz] = jnp.where(core == 0, cols[64:], cols[:64]).astype(BF16)
+        wz = lax.rem(i, 2)
+        wy = lax.div(i, 2)
+        part = dot_nn(xt[pl.ds(pl.multiple_of(i * 512, 512), 512), :], grad_cols)
+        for wx in range(4):
+            for h, (wq, wp) in enumerate(((wy, wx), (wx, wy))):
+                cols = part[wx * 128 : (wx + 1) * 128, h * HEAD : (h + 1) * HEAD]
+                wown[h, wq, wp, wz] = jnp.where(core == 0, cols[:64], cols[64:])
+                wsend[h, wq, wp, wz] = jnp.where(core == 0, cols[64:], cols[:64]).astype(BF16)
         return carry
 
-    lax.fori_loop(0, 32, weight_block, 0)
+    lax.fori_loop(0, 8, weight_block, 0)
     send("wc", wsend, wrecv, d_core)
 
     igs, igr, igo = b["igs"], b["igr"], b["igo"]
@@ -563,24 +617,19 @@
     assert len(names) <= NSEM and len(local_names) <= NLOCAL
 
 
+def finish(dq_in, ig_in, w_in, dq_out, ig_out, kw_out, vw_out):
+    for c in range(CHUNKS):
+        for kvh in range(2):
+            for g in range(GROUP):
+                at = (kvh * GROUP + g) * HEAD
+                dq_out[c * 16 : (c + 1) * 16, at : at + HEAD] = dq_in[kvh, c, g]
+    ig_out[...] = ig_in[...]
+    for t, out in enumerate((kw_out, vw_out)):
+        for n in range(2):
+            out[:, n * HEAD : (n + 1) * HEAD] = w_in[t, n]
+
+
 def local_step(q, k, v, g, x, mk, mv, placement):
-    core = lax.axis_index(CORE)
-    pos = (
-        (jnp.arange(64, dtype=jnp.int32) * 128)[:, None, None]
-        + placement[:, :, None] * 2
-        + jnp.arange(2, dtype=jnp.int32)
-    ).astype(F32)
-    pos = pos.reshape(CHUNKS, 8, 4, 2, 4, 2, 2)
-    kpos = lax.dynamic_index_in_dim(pos, core, 5, keepdims=False)
-    kpos = kpos.reshape(2, 4, 8, 4, 2, 4, 2)
-    half_a = kpos[0].transpose(2, 0, 4, 3, 1, 5)
-    half_b = kpos[1].transpose(4, 0, 2, 3, 1, 5)
-    kp = jnp.stack([half_a, half_b]).reshape(32, KROWS)
-    qpos = lax.dynamic_index_in_dim(pos, lax.axis_index(Y), 2, keepdims=False)
-    qpos = lax.dynamic_index_in_dim(qpos, lax.axis_index(X), 3, keepdims=False)
-    qpos = qpos.transpose(0, 2, 3, 1, 4).reshape(CHUNKS, 4, 1, 16)
-    qp = jnp.broadcast_to(qpos, (CHUNKS, 4, GROUP, 16)).reshape(CHUNKS, QROWS)
-
     anywhere = pl.BlockSpec(memory_space=pl.ANY)
     vmem = pl.BlockSpec(memory_space=pltpu.VMEM)
     dq, ig, w = pl.pallas_call(
@@ -590,7 +639,7 @@
             jax.ShapeDtypeStruct((128, FEATS // 2), BF16),
             jax.ShapeDtypeStruct((2, 2, 64, HEAD), F32),
         ),
-        in_specs=[anywhere] * 7 + [vmem] * 2,
+        in_specs=[anywhere] * 7 + [vmem],
         out_specs=(vmem, vmem, vmem),
         scratch_shapes=[pltpu.VMEM(shape, dtype) for shape, dtype in BUFFERS.values()]
         + [
@@ -609,12 +658,19 @@
         x.reshape(CHUNKS, 16, -1),
         mk,
         mv,
-        kp,
-        qp,
+        placement,
     )
-    query_grad = dq.transpose(1, 3, 0, 2, 4).reshape(128, -1)
-    weights = [w[t].transpose(1, 0, 2).reshape(64, 2 * HEAD) for t in range(2)]
-    return (query_grad, ig, weights[0], weights[1])
+    return pl.pallas_call(
+        finish,
+        out_shape=(
+            jax.ShapeDtypeStruct((128, 2 * GROUP * HEAD), BF16),
+            jax.ShapeDtypeStruct((128, FEATS // 2), BF16),
+            jax.ShapeDtypeStruct((64, 2 * HEAD), F32),
+            jax.ShapeDtypeStruct((64, 2 * HEAD), F32),
+        ),
+        in_specs=[vmem] * 3,
+        out_specs=(vmem,) * 4,
+    )(dq, ig, w)
 
 
 def solution(mesh):

time: 99 us -> 87.6 us (0.88)
  local copies, waits for them, and re-layouts: 8.39 us -> 0 us
  Pallas kernels: 88.6 us -> 86.8 us
    pallas_call x1, Pallas kernels: 88.6 us -> 84.6 us  [local_step(): pl.pallas_call(kernel, out_shape=(jax.ShapeDtypeStruct((2, CHUNKS, GROUP,...]
    reshape x5 -> x0, local copies, waits for them, and re-layouts: 3.27 us -> none  [the longest x2 1.02 us: local_step(): kp = jnp.stack([half_a, half_b]).reshape(32, KROWS)]
    unnamed x3 -> x0, local copies, waits for them, and re-layouts: 2.77 us -> none
    pallas_call x0 -> x1, Pallas kernels: none -> 2.13 us  [local_step(): pl.pallas_call(finish, out_shape=(jax.ShapeDtypeStruct((128, 2 * GROUP *...]
    transpose x3 -> x0, local copies, waits for them, and re-layouts: 1.15 us -> none  [the longest x1 1.05 us: local_step(): query_grad = dq.transpose(1, 3, 0, 2, 4).reshape(128, -1)]
where the time goes in v2:
time: 87.6 us; the launch traced here: 87.4 us
  Pallas kernels  86.8 us (99%)
    pallas_call x1, Pallas kernels, local_step(): pl.pallas_call(kernel, out_shape=(jax.ShapeDtypeStruct((2, CHUNKS, GROUP,...  84.6 us
    pallas_call x1, Pallas kernels, local_step(): pl.pallas_call(finish, out_shape=(jax.ShapeDtypeStruct((128, 2 * GROUP *...  2.13 us

profile of v2, /device:TPU:0, one launch (start us, length us, event | category | flops | bytes accessed | tf_op | source)
XLA Modules:
  0.0 87.4 jit_solution(7141653296163043469)
XLA Ops:
  0.6 84.6 %shard_map.111 = (bf16[2,8,4,16,128]{4,3,2,1,0:T(8,128)(2,1)}, bf16[128,2048]{1,0:T(8,128)(2,1)}, f32[2,2,64,128]{3,2,1,0:T(8,128)}) custom-call(bf16[8,16,1024]{2,1,0:T(8,128)(2,1)} %bitcast.6, bf16[8,16,1024]{2,1,0:T(8,128)(2,1)} %bitcast.7, bf16[8,16,256]{2,1,0:T(8,128)(2,1)} %bitcast.8, bf16[8,16,256]{2,1,0:T(8,128)(2,1)} %bitcast.9, ...), custom_call_target="tpu_custom_call" | custom-call | tf_op jit(solution)/shard_map/pallas_call | solution.py:635
  85.3 2.1 %shard_map.112 = (bf16[128,1024]{1,0:T(8,128)(2,1)}, bf16[128,2048]{1,0:T(8,128)(2,1)}, f32[64,256]{1,0:T(8,128)}, f32[64,256]{1,0:T(8,128)}) custom-call(bf16[2,8,4,16,128]{4,3,2,1,0:T(8,128)(2,1)} %get-tuple-element.7.dq_in, bf16[128,2048]{1,0:T(8,128)(2,1)} %get-tuple-element.8.ig_in, f32[2,2,64,128]{3,2,1,0:T(8,128)} %get-tuple-element.9.w_in), custom_call_target="tpu_custom_call" | custom-call | tf_op jit(solution)/shard_map/pallas_call | solution.py:663

commit v3 on v2

--- a/solution.py
+++ b/solution.py
@@ -25,7 +25,7 @@
 MASKED = -1e30
 QROWS = 256
 KROWS = 128
-NSEM = 96
+NSEM = 192
 NLOCAL = 24
 
 
@@ -44,10 +44,9 @@
     half = unit[1:]
     return {
         name + "_far": ((2, 4) + unit, BF16),
-        name + "_rfar": ((2, 2, 2) + unit, BF16),
+        name + "_rfar": ((2, 2, 4) + half, BF16),
         name + "_near": ((2, 2, 4) + unit, BF16),
         name + "_rnear": ((2, 2, 4) + unit, BF16),
-        name + "_row": ((2, 4) + unit, F32),
         name + "_far2": ((2,) + unit, BF16),
         name + "_rfar2": ((2, 2) + half, BF16),
         name + "_near2": ((2, 2) + unit, BF16),
@@ -70,20 +69,20 @@
     "dqt": ((CHUNKS, HEAD, QROWS), F32),
     "dqf": ((CHUNKS, 2, 2, GROUP, 16, HEAD), F32),
     "dqr": ((CHUNKS, 2, GROUP, 16, HEAD), F32),
-    "dqs": ((CHUNKS, GROUP, 16, HEAD), BF16),
-    "dqz": ((CHUNKS, GROUP, 16, HEAD), BF16),
+    "dqs": ((2, CHUNKS, GROUP, 16, HEAD), BF16),
+    "dqz": ((2, CHUNKS, GROUP, 16, HEAD), BF16),
     "kt": ((CHUNKS, HEAD, KROWS), BF16),
     "qp": ((CHUNKS, QROWS), F32),
     "xg": ((CHUNKS, 2, 16, FEATS), BF16),
-    "xt": ((FEATS, 256), BF16),
+    "xt": ((32, 2, 64, 256), BF16),
+    "xo": ((32, 64, 256), BF16),
     "mat": ((2, FEATS, 2 * HEAD), BF16),
     "d2": ((2, CHUNKS, 2, 16, HEAD), BF16),
+    "d2o": ((2, CHUNKS, 2, 16, HEAD), BF16),
     "dd": ((4, CHUNKS, 16, HEAD), BF16),
     "wown": ((2, 4, 4) + UNIT_W, F32),
-    "wsend": ((2, 4, 4) + UNIT_W, BF16),
-    "wrecv": ((2, 4, 4) + UNIT_W, BF16),
-    "wfin": ((2,) + UNIT_W, F32),
-    "wswap": ((2, 64, HEAD), F32),
+    "wfin": ((2,) + UNIT_W, BF16),
+    "wz": ((2, 2, 64, HEAD), BF16),
     "igs": ((128, FEATS // 2), BF16),
     "igr": ((128, FEATS // 2), BF16),
     "igo": ((128, FEATS // 2), F32),
@@ -159,7 +158,8 @@
     zp_h, zp_l = lax.div(zp, 2), lax.rem(zp, 2)
     zm_h, zm_l = lax.div(zm, 2), lax.rem(zm, 2)
     oh, oc, ol = 1 - zh, 1 - core, 1 - zl
-    d_zh, d_core, d_tp = {ZH: oh}, {CORE: oc}, {ZL: ol}
+    d_core, d_tp = {CORE: oc}, {ZL: ol}
+    across = ((d_tp, zh), ({ZH: oh, ZL: ol}, oh))
     d_zp, d_zm = {ZH: zp_h, ZL: zp_l}, {ZH: zm_h, ZL: zm_l}
     step_of = {a: ({a: turn(i, 1)}, {a: turn(i, 3)}) for a, i in ((X, x), (Y, y))}
     qi, pi = (y, x), (x, y)
@@ -197,70 +197,66 @@
         return pl.ds(pl.multiple_of(start, 128), width)
 
     kv, qg, xg, mat = b["kv"], b["qg"], b["xg"], b["mat"]
-    own_kv = []
-    for h in range(2):
-        for t, ref in enumerate((k_in, v_in)):
-            own_kv.append(
-                local(
-                    ("kv", h, t),
-                    ref.at[pl.ds(4 * h, 4), :, lanes(zh * HEAD)],
-                    kv.at[h, qi[h], pi[h], t, :, zh],
-                )
-            )
-    own_q = []
-    for t, ref in enumerate((q_in, g_in)):
-        for g in range(GROUP):
-            own_q.append(
-                local(
-                    ("qg", t, g),
-                    ref.at[:, :, lanes(zh * GROUP * HEAD + g * HEAD)],
-                    qg.at[t, :, 2 * zh + core, g],
-                )
-            )
     own_x = local("x", x_in, xg.at[:, zh, :, lanes(zl * (FEATS // 2), FEATS // 2)])
     own_m = [local("mk", mk_in, mat.at[0]), local("mv", mv_in, mat.at[1])]
-    for c in own_kv + own_q:
-        c.start()
 
     barrier = pltpu.get_barrier_semaphore()
-    peers = [d_zh, d_core, *step_of[X], *step_of[Y], d_zp, d_zm]
+    peers = [d_core, *step_of[X], *step_of[Y], d_zp, d_zm]
     for dev in peers:
         pl.semaphore_signal(barrier, inc=1, device_id=dev, device_id_type=MESH)
     pl.semaphore_wait(barrier, len(peers))
 
     for h in range(2):
-        for t, ref in enumerate((k_in, v_in)):
-            send(
-                ("zkv", h, t),
-                ref.at[pl.ds(4 * h, 4), :, lanes(oh * HEAD)],
-                kv.at[h, qi[h], pi[h], t, :, zh],
-                d_zh,
-            )
+        for r, (dev, head) in enumerate(across):
+            for t, ref in enumerate((k_in, v_in)):
+                send(
+                    ("zkv", h, t, r),
+                    ref.at[pl.ds(4 * h, 4), :, lanes(head * HEAD)],
+                    kv.at[h, qi[h], pi[h], t, :, zh],
+                    dev,
+                )
     for t, ref in enumerate((q_in, g_in)):
-        for g in range(GROUP):
-            send(
-                ("qz", t, g),
-                ref.at[:, :, lanes(oh * GROUP * HEAD + g * HEAD)],
-                qg.at[t, :, 2 * zh + core, g],
-                d_zh,
-            )
-    for t, ref in enumerate((q_in, g_in)):
-        for g in range(GROUP):
-            send(
-                ("qc", t, g),
-                ref.at[:, :, lanes(zh * GROUP * HEAD + g * HEAD)],
-                qg.at[t, :, 2 * zh + core, g],
-                d_core,
-            )
-    for c in own_kv:
-        c.wait()
+        for r, (dev, head) in enumerate(across):
+            for g in range(GROUP):
+                send(
+                    ("qz", t, r, g),
+                    ref.at[:, :, lanes(head * GROUP * HEAD + g * HEAD)],
+                    qg.at[t, :, 2 * zh + core, g],
+                    dev,
+                )
+
+    unit_offs = (0, 3, 1, 2)
+
+    def unit_piece(h, n, side):
+        unit = kv.at[h, qi[h], turn(pi[h], unit_offs[n])]
+        return ("q", h, n, side), unit, unit, q_to[h][side]
+
+    def send_unit(h, n):
+        for side in range(2):
+            send(*unit_piece(h, n, side))
+
+    def near_piece(h, n, side):
+        return kv.at[h, turn(qi[h], 3 if side == 0 else 1), turn(pi[h], unit_offs[n])]
+
+    def forward_piece(h, n, side):
+        src = near_piece(h, n, side).at[side]
+        return ("qf", h, n, side), src, src, q_to[h][side]
+
+    def forward_unit(h, n):
+        for side in range(2):
+            arrived(("q", h, n, side), near_piece(h, n, side))
+            remote(*forward_piece(h, n, side)).start()
+            if n == 0:
+                pending.append(forward_piece(h, n, side))
 
     for h in range(2):
-        for t in range(2):
-            arrived(("zkv", h, t), kv.at[h, qi[h], pi[h], t, :, oh])
+        for r, (dev, head) in enumerate(across):
+            for t in range(2):
+                arrived(("zkv", h, t, r), kv.at[h, qi[h], pi[h], t, :, head])
+        unit = kv.at[h, qi[h], pi[h]]
         for side in range(2):
-            unit = kv.at[h, qi[h], pi[h]]
             send(("p", h, side), unit, unit, p_to[h][side])
+        send_unit(h, 0)
     own_x.start()
     for c in own_m:
         c.start()
@@ -274,29 +270,28 @@
             src = kv.at[h, qi[h], turn(pi[h], 3 if side == 0 else 1)]
             arrived(("p", h, side), src)
             send(("pf", h, side), src.at[side], src.at[side], p_to[h][side])
+        for side in range(2):
+            send_unit(h, 1 + side)
     for h in range(2):
-        for side in range(2):
-            arrived(("pf", h, side), kv.at[h, qi[h], turn(pi[h], 2), side])
-        for side in range(2):
-            row = kv.at[h, qi[h]]
-            send(("q", h, side), row, row, q_to[h][side])
-
+        forward_unit(h, 0)
     for t in range(2):
-        for g in range(GROUP):
-            arrived(("qz", t, g), qg.at[t, :, 2 * oh + core, g])
-        src = qg.at[t, :, 2 * oh + core]
-        send(("qf", t), src, src, d_core)
+        for r, (dev, head) in enumerate(across):
+            for g in range(GROUP):
+                arrived(("qz", t, r, g), qg.at[t, :, 2 * head + core, g])
+            src = qg.at[t, :, 2 * head + core]
+            send(("qc", t, r), src, src, d_core)
     half_feats = FEATS // 2
     quarter_feats = FEATS // 4
     mine = xg.at[:, zh, :, lanes(zl * half_feats, half_feats)]
     send("x+", x_in, mine, d_zp)
     send("x-", x_in, mine, d_zm)
-    for c in own_q:
-        c.wait()
+    for h in range(2):
+        for side in range(2):
+            arrived(("pf", h, side), kv.at[h, qi[h], turn(pi[h], 2), side])
+        send_unit(h, 3)
     for t in range(2):
-        for g in range(GROUP):
-            arrived(("qc", t, g), qg.at[t, :, 2 * zh + oc, g])
-        arrived(("qf", t), qg.at[t, :, 2 * oh + oc])
+        for r, (dev, head) in enumerate(across):
+            arrived(("qc", t, r), qg.at[t, :, 2 * head + oc])
 
     def queries(t, cq):
         return qg[t, cq].reshape(QROWS, HEAD)
@@ -306,16 +301,6 @@
             [kv[ck // 4, at[ck // 4], :, t, ck % 4].reshape(KROWS, HEAD) for ck in cks]
         )
 
-    def row_far(h, side):
-        return kv.at[h, turn(qi[h], 2), pl.ds(2 * side, 2)]
-
-    def row_near(h, side):
-        return kv.at[h, turn(qi[h], 3 if side == 0 else 1)]
-
-    def forward(h, side):
-        src = row_near(h, side).at[pl.ds(2 * side, 2)]
-        return ("qfar", h, side), src, src, q_to[h][side]
-
     st, e_ref, dp_ref = b["st"], b["e"], b["dp"]
 
     def first_pass(s, carry):
@@ -324,16 +309,19 @@
 
         @pl.when(s == 1)
         def _():
-            for h in range(2):
-                for side in range(2):
-                    arrived(("q", h, side), row_near(h, side))
-                    remote(*forward(h, side)).start()
+            for n in range(1, 4):
+                for h in range(2):
+                    forward_unit(h, n)
 
         @pl.when(s == 3)
         def _():
-            for h in range(2):
-                for side in range(2):
-                    arrived(("qfar", h, side), row_far(h, side))
+            for n in range(4):
+                for h in range(2):
+                    for side in range(2):
+                        arrived(
+                            ("qf", h, n, side),
+                            kv.at[h, turn(qi[h], 2), turn(pi[h], unit_offs[n]), side],
+                        )
 
         at = (turn(y, off), turn(x, off))
         for cq in range(CHUNKS):
@@ -362,8 +350,10 @@
 
     lax.fori_loop(0, 4, first_pass, 0)
     for h in range(2):
-        for side in range(2):
-            pending.append(forward(h, side))
+        for n in range(4):
+            for side in range(2):
+                if n:
+                    pending.append(forward_piece(h, n, side))
 
     ss, sr = b["ss"], b["sr"]
     top_l = jnp.max(st[0], axis=(0, 1))
@@ -374,12 +364,19 @@
     ss[1] = sum_l
     ss[2] = wgt_l
     send("stat", ss, sr, d_core)
-    arrived("x+", xg.at[:, zm_h, :, lanes(zm_l * half_feats, half_feats)])
-    src = xg.at[:, zm_h, :, lanes(zm_l * half_feats, quarter_feats)]
-    send("xf+", src, src, d_zp)
-    arrived("x-", xg.at[:, zp_h, :, lanes(zp_l * half_feats, half_feats)])
-    src = xg.at[:, zp_h, :, lanes(zp_l * half_feats + quarter_feats, quarter_feats)]
-    send("xf-", src, src, d_zm)
+
+    def forward_input(names_only=False):
+        for name, src_h, src_l, start, dev in (
+            ("x+", zm_h, zm_l, 0, d_zp),
+            ("x-", zp_h, zp_l, quarter_feats, d_zm),
+        ):
+            src = xg.at[:, src_h, :, lanes(src_l * half_feats + start, quarter_feats)]
+            if names_only:
+                pending.append(("far " + name, src, src, dev))
+            else:
+                arrived(name, xg.at[:, src_h, :, lanes(src_l * half_feats, half_feats)])
+                remote("far " + name, src, src, dev).start()
+
     arrived("stat", sr)
     top = jnp.maximum(top_l, sr[0])
     mine_f = jnp.exp2(top_l - top)
@@ -388,87 +385,105 @@
     b["delta"][...] = (wgt_l * mine_f + sr[2] * other_f) / total
     b["fac"][...] = fac_l * (mine_f / total)[None, None]
 
-    def reducer(name, row):
+    offs = (2, 1, 3, 0)
+
+    def reducer(name, unit_at):
         far, rfar = b[name + "_far"], b[name + "_rfar"]
         near, rnear = b[name + "_near"], b[name + "_rnear"]
-        rows = b[name + "_row"]
         far2, rfar2 = b[name + "_far2"], b[name + "_rfar2"]
         near2, rnear2 = b[name + "_near2"], b[name + "_rnear2"]
 
-        def far_copy(h, side):
+        def place(h, n):
+            return turn(pi[h], offs[n])
+
+        def far_copy(h, n, side):
+            p = place(h, n)
             return (
-                (name, "far", h, side),
-                far.at[h, pl.ds(2 * side, 2)],
-                rfar.at[h, side],
+                (name, "far", h, n, side),
+                far.at[h, p, side],
+                rfar.at[h, side, p],
                 q_to[h][side],
             )
 
-        def near_copy(h, side):
-            return (name, "near", h, side), near.at[h, side], rnear.at[h, side], q_to[h][side]
+        def near_copy(h, n, side):
+            p = place(h, n)
+            return (
+                (name, "near", h, n, side),
+                near.at[h, side, p],
+                rnear.at[h, side, p],
+                q_to[h][side],
+            )
 
         def start_far():
-            for h in range(2):
-                far[h] = row(h, turn(qi[h], 2)).astype(BF16)
-                for side in range(2):
-                    remote(*far_copy(h, side)).start()
+            for n in range(4):
+                for h in range(2):
+                    p = place(h, n)
+                    far[h, p] = unit_at(h, turn(qi[h], 2), p).astype(BF16)
+                    for side in range(2):
+                        remote(*far_copy(h, n, side)).start()
 
         def start_near(side):
-            for h in range(2):
-                value = row(h, turn(qi[h], 1 if side == 0 else 3))
-                arrived((name, "far", h, side), rfar.at[h, side])
-                lo, hi = value[:2], value[2:]
-                if side == 0:
-                    lo = lo + rfar[h, side].astype(F32)
-                else:
-                    hi = hi + rfar[h, side].astype(F32)
-                near[h, side, :2] = lo.astype(BF16)
-                near[h, side, 2:] = hi.astype(BF16)
-                remote(*near_copy(h, side)).start()
+            for n in range(4):
+                for h in range(2):
+                    p = place(h, n)
+                    value = unit_at(h, turn(qi[h], 1 if side == 0 else 3), p)
+                    arrived((name, "far", h, n, side), rfar.at[h, side, p])
+                    near[h, side, p, 1 - side] = value[1 - side].astype(BF16)
+                    near[h, side, p, side] = (value[side] + rfar[h, side, p].astype(F32)).astype(
+                        BF16
+                    )
+                    remote(*near_copy(h, n, side)).start()
 
         def note_sends():
             for h in range(2):
+                for n in range(4):
+                    for side in range(2):
+                        pending.append(far_copy(h, n, side))
+                        pending.append(near_copy(h, n, side))
+
+        def own_unit(n):
+            out = []
+            for h in range(2):
+                p = place(h, n)
                 for side in range(2):
-                    pending.append(far_copy(h, side))
-                    pending.append(near_copy(h, side))
-
-        def own_row():
-            for h in range(2):
-                for side in range(2):
-                    arrived((name, "near", h, side), rnear.at[h, side])
-                rows[h] = row(h, qi[h]) + rnear[h, 0].astype(F32) + rnear[h, 1].astype(F32)
-                far2[h] = rows[h, turn(pi[h], 2)].astype(BF16)
-                for side in range(2):
+                    arrived((name, "near", h, n, side), rnear.at[h, side, p])
+                value = (
+                    unit_at(h, qi[h], p)
+                    + rnear[h, 0, p].astype(F32)
+                    + rnear[h, 1, p].astype(F32)
+                )
+                if n == 0:
+                    far2[h] = value.astype(BF16)
+                    for side in range(2):
+                        send(
+                            (name, "far2", h, side),
+                            far2.at[h, side],
+                            rfar2.at[h, side],
+                            p_to[h][side],
+                        )
+                elif n < 3:
+                    side = n - 1
+                    arrived((name, "far2", h, side), rfar2.at[h, side])
+                    near2[h, side, 1 - side] = value[1 - side].astype(BF16)
+                    near2[h, side, side] = (value[side] + rfar2[h, side].astype(F32)).astype(BF16)
                     send(
-                        (name, "far2", h, side),
-                        far2.at[h, side],
-                        rfar2.at[h, side],
+                        (name, "near2", h, side),
+                        near2.at[h, side],
+                        rnear2.at[h, side],
                         p_to[h][side],
                     )
-
-        def near_unit():
-            for h in range(2):
-                for side in range(2):
-                    arrived((name, "far2", h, side), rfar2.at[h, side])
-                    at = turn(pi[h], 1 if side == 0 else 3)
-                    near2[h, side, 1 - side] = rows[h, at, 1 - side].astype(BF16)
-                    near2[h, side, side] = (
-                        rows[h, at, side] + rfar2[h, side].astype(F32)
-                    ).astype(BF16)
-                    send(
-                        (name, "near2", h, side), near2.at[h, side], rnear2.at[h, side], p_to[h][side]
+                else:
+                    for side in range(2):
+                        arrived((name, "near2", h, side), rnear2.at[h, side])
+                    out.append(
+                        value + rnear2[h, 0].astype(F32) + rnear2[h, 1].astype(F32)
                     )
-
-        def final(h):
-            for side in range(2):
-                arrived((name, "near2", h, side), rnear2.at[h, side])
-            return rows[h, pi[h]] + rnear2[h, 0].astype(F32) + rnear2[h, 1].astype(F32)
-
-        return start_far, start_near, note_sends, own_row, near_unit, final
+            return out
+
+        return start_far, start_near, note_sends, own_unit
 
     acc = b["acc"]
-    start_far, start_near, note_sends, own_row, near_unit, final = reducer(
-        "a", lambda h, at: acc[h]
-    )
+    start_far, start_near, note_sends, own_unit = reducer("a", lambda h, q, p: acc[h, p])
 
     fac, delta, kt = b["fac"], b["delta"], b["kt"]
 
@@ -506,6 +521,7 @@
         @pl.when(s == 1)
         def _():
             start_near(1)
+            forward_input()
 
         @pl.when(s == 2)
         def _():
@@ -515,63 +531,82 @@
 
     lax.fori_loop(0, 4, second_pass, 0)
     note_sends()
+    forward_input(names_only=True)
 
     dqf, dqr, dqs, dqz = b["dqf"], b["dqr"], b["dqs"], b["dqz"]
     for cq in range(CHUNKS):
         dqf[cq] = (dqt[cq].T * SCALE).reshape(2, 2, GROUP, 16, HEAD)
     send("dqc", dqf.at[:, :, oc], dqr, d_core)
+    own_unit(0)
     own_x.wait()
+    far_h = 1 - zh
+    arrived("far x+", xg.at[:, far_h, :, lanes(zl * half_feats, quarter_feats)])
+    arrived("far x-", xg.at[:, far_h, :, lanes(zl * half_feats + quarter_feats, quarter_feats)])
+    xt, xo = b["xt"], b["xo"]
+
+    def flip_input(i, carry):
+        for n in range(4):
+            at = i * 4 + n
+            block = xg[:, :, :, lanes(at * 128)].reshape(256, 128)
+            xt[at] = block.T.reshape(2, 64, 256)
+        return carry
+
+    lax.fori_loop(0, 8, flip_input, 0)
+    send("xt", xt.at[:, oc], xo, d_core)
+    own_unit(1)
+    own_unit(2)
+    arrived("dqc", dqr)
+    for n in range(2):
+        dqs[n] = (dqf[:, n, core] + dqr[:, n]).astype(BF16)
+    for r, (dev, other) in enumerate(across):
+        send(("dqz", r), dqs.at[other], dqz.at[zh], dev)
+    d2, d2o, dd = b["d2"], b["d2o"], b["dd"]
+    for h, value in enumerate(own_unit(3)):
+        d2[0, 4 * h : 4 * h + 4] = (value[0] * SCALE).astype(BF16)
+        d2[1, 4 * h : 4 * h + 4] = value[1].astype(BF16)
+    send("d2", d2, d2o, d_core)
+    for r, (dev, other) in enumerate(across):
+        for t in range(2):
+            send(("dz", t, r), d2.at[t, :, other], dd.at[2 * t + zh], dev)
+
+    wown = b["wown"]
+
+    def grad_cols(ref):
+        return jnp.concatenate([ref[0].reshape(256, HEAD), ref[1].reshape(256, HEAD)], axis=1)
+
+    def weight_blocks(first):
+        cols = grad_cols(d2 if first else d2o)
+
+        def body(i, carry):
+            wz = lax.rem(i, 2)
+            wy = lax.div(i, 2)
+            at = pl.ds(i * 4, 4)
+            rows = (xt[at, core] if first else xo[at]).reshape(256, 256)
+            part = dot_nn(rows, cols)
+            for wx in range(4):
+                for h, (wq, wp) in enumerate(((wy, wx), (wx, wy))):
+                    block = part[wx * 64 : (wx + 1) * 64, h * HEAD : (h + 1) * HEAD]
+                    if first:
+                        wown[h, wq, wp, wz] = block
+                    else:
+                        wown[h, wq, wp, wz] = wown[h, wq, wp, wz] + block
+            return carry
+
+        lax.fori_loop(0, 8, body, 0)
+
+    weight_blocks(True)
+    arrived("xt", xo)
+    arrived("d2", d2o)
+    weight_blocks(False)
+    w_far, w_near, w_note, w_unit = reducer("w", lambda h, q, p: wown[h, q, p])
+    w_far()
+
+    igs, igr, igo, mat = b["igs"], b["igr"], b["igo"], b["mat"]
     for c in own_m:
         c.wait()
-    far_h = 1 - zh
-    arrived("xf+", xg.at[:, far_h, :, lanes(zl * half_feats, quarter_feats)])
-    arrived("xf-", xg.at[:, far_h, :, lanes(zl * half_feats + quarter_feats, quarter_feats)])
-    xt = b["xt"]
-
-    def flip_input(i, carry):
-        for n in range(4):
-            at = i * 512 + n * 128
-            xt[pl.ds(pl.multiple_of(at, 128), 128), :] = xg[:, :, :, lanes(at)].reshape(256, 128).T
-        return carry
-
-    lax.fori_loop(0, 8, flip_input, 0)
-    own_row()
-    arrived("dqc", dqr)
-    dqs[...] = (dqf[:, oh, core] + dqr[:, oh]).astype(BF16)
-    send("dqz", dqs, dqz, d_zh)
-    dq_out[zh] = (dqf[:, zh, core] + dqr[:, zh]).astype(BF16)
-    near_unit()
-    arrived("dqz", dqz)
-    dq_out[oh] = dqz[...]
-    d2, dd = b["d2"], b["dd"]
-    for h in range(2):
-        value = final(h)
-        d2[0, 4 * h : 4 * h + 4] = (value[0] * SCALE).astype(BF16)
-        d2[1, 4 * h : 4 * h + 4] = value[1].astype(BF16)
-    for t in range(2):
-        send(("dz", t), d2.at[t, :, oh], dd.at[2 * t + zh], d_zh)
-        dd[2 * t + zh] = d2[t, :, zh]
-
-    wown, wsend, wrecv = b["wown"], b["wsend"], b["wrecv"]
-    grad_cols = jnp.concatenate([d2[0].reshape(256, HEAD), d2[1].reshape(256, HEAD)], axis=1)
-
-    def weight_block(i, carry):
-        wz = lax.rem(i, 2)
-        wy = lax.div(i, 2)
-        part = dot_nn(xt[pl.ds(pl.multiple_of(i * 512, 512), 512), :], grad_cols)
-        for wx in range(4):
-            for h, (wq, wp) in enumerate(((wy, wx), (wx, wy))):
-                cols = part[wx * 128 : (wx + 1) * 128, h * HEAD : (h + 1) * HEAD]
-                wown[h, wq, wp, wz] = jnp.where(core == 0, cols[:64], cols[64:])
-                wsend[h, wq, wp, wz] = jnp.where(core == 0, cols[64:], cols[:64]).astype(BF16)
-        return carry
-
-    lax.fori_loop(0, 8, weight_block, 0)
-    send("wc", wsend, wrecv, d_core)
-
-    igs, igr, igo = b["igs"], b["igr"], b["igo"]
-    for t in range(2):
-        arrived(("dz", t), dd.at[2 * t + oh])
+    for r, (dev, other) in enumerate(across):
+        for t in range(2):
+            arrived(("dz", t, r), dd.at[2 * t + other])
     dk_dv = [
         jnp.concatenate([dd[2 * t].reshape(128, HEAD), dd[2 * t + 1].reshape(128, HEAD)], axis=1)
         for t in range(2)
@@ -588,29 +623,26 @@
 
     input_block(ol * half_feats, igs)
     send("ig", igs, igr, d_tp)
-
-    arrived("wc", wrecv)
-    w_far, w_near, w_note, w_own, w_unit, w_final = reducer(
-        "w", lambda h, at: wown[h, at] + wrecv[h, at].astype(F32)
-    )
-    w_far()
-    input_block(zl * half_feats, igo)
     w_near(0)
     w_near(1)
     w_note()
-    w_own()
-    w_unit()
-    wfin, wswap = b["wfin"], b["wswap"]
-    for h in range(2):
-        wfin[h] = w_final(h)
-    for h in range(2):
-        send(("ws", h), wfin.at[h, oh], wswap.at[h], d_zh)
-        w_out[h, zh] = wfin[h, zh]
+    input_block(zl * half_feats, igo)
+    for r, (dev, other) in enumerate(across):
+        arrived(("dqz", r), dqz.at[other])
+    dq_out[...] = dqz[...]
+    w_unit(0)
+    w_unit(1)
+    w_unit(2)
+    wfin, wz_ref = b["wfin"], b["wz"]
+    for h, value in enumerate(w_unit(3)):
+        wfin[h] = value.astype(BF16)
+    for r, (dev, other) in enumerate(across):
+        send(("ws", r), wfin.at[:, other], wz_ref.at[:, zh], dev)
     arrived("ig", igr)
     ig_out[...] = (igo[...] + igr[...].astype(F32)).astype(BF16)
-    for h in range(2):
-        arrived(("ws", h), wswap.at[h])
-        w_out[h, oh] = wswap[h]
+    for r, (dev, other) in enumerate(across):
+        arrived(("ws", r), wz_ref.at[:, other])
+    w_out[...] = wz_ref[...].astype(F32)
 
     for copy in pending:
         remote(*copy).wait_send()

time: 87.6 us -> 81.4 us (0.929)
  Pallas kernels: 86.8 us -> 80.5 us
    pallas_call x1, Pallas kernels: 84.6 us -> 78.4 us  [local_step(): pl.pallas_call(kernel, out_shape=(jax.ShapeDtypeStruct((2, CHUNKS, GROUP,...]
where the time goes in v3:
time: 81.4 us; the launch traced here: 81.2 us
  Pallas kernels  80.5 us (99%)
    pallas_call x1, Pallas kernels, local_step(): pl.pallas_call(kernel, out_shape=(jax.ShapeDtypeStruct((2, CHUNKS, GROUP,...  78.4 us
    pallas_call x1, Pallas kernels, local_step(): pl.pallas_call(finish, out_shape=(jax.ShapeDtypeStruct((128, 2 * GROUP *...  2.13 us

profile of v3, /device:TPU:0, one launch (start us, length us, event | category | flops | bytes accessed | tf_op | source)
XLA Modules:
  0.0 81.2 jit_solution(4557729104744355557)
XLA Ops:
  0.6 78.4 %shard_map.111 = (bf16[2,8,4,16,128]{4,3,2,1,0:T(8,128)(2,1)}, bf16[128,2048]{1,0:T(8,128)(2,1)}, f32[2,2,64,128]{3,2,1,0:T(8,128)}) custom-call(bf16[8,16,1024]{2,1,0:T(8,128)(2,1)} %bitcast.6, bf16[8,16,1024]{2,1,0:T(8,128)(2,1)} %bitcast.7, bf16[8,16,256]{2,1,0:T(8,128)(2,1)} %bitcast.8, bf16[8,16,256]{2,1,0:T(8,128)(2,1)} %bitcast.9, ...), custom_call_target="tpu_custom_call" | custom-call | tf_op jit(solution)/shard_map/pallas_call | solution.py:667
  79.0 2.1 %shard_map.112 = (bf16[128,1024]{1,0:T(8,128)(2,1)}, bf16[128,2048]{1,0:T(8,128)(2,1)}, f32[64,256]{1,0:T(8,128)}, f32[64,256]{1,0:T(8,128)}) custom-call(bf16[2,8,4,16,128]{4,3,2,1,0:T(8,128)(2,1)} %get-tuple-element.7.dq_in, bf16[128,2048]{1,0:T(8,128)(2,1)} %get-tuple-element.8.ig_in, f32[2,2,64,128]{3,2,1,0:T(8,128)} %get-tuple-element.9.w_in), custom_call_target="tpu_custom_call" | custom-call | tf_op jit(solution)/shard_map/pallas_call | solution.py:695

commit v4 on v3

--- a/solution.py
+++ b/solution.py
@@ -48,7 +48,7 @@
         name + "_near": ((2, 2, 4) + unit, BF16),
         name + "_rnear": ((2, 2, 4) + unit, BF16),
         name + "_far2": ((2,) + unit, BF16),
-        name + "_rfar2": ((2, 2) + half, BF16),
+        name + "_rfar2": ((2,) + unit, BF16),
         name + "_near2": ((2, 2) + unit, BF16),
         name + "_rnear2": ((2, 2) + unit, BF16),
     }
@@ -76,16 +76,14 @@
     "xg": ((CHUNKS, 2, 16, FEATS), BF16),
     "xt": ((32, 2, 64, 256), BF16),
     "xo": ((32, 64, 256), BF16),
-    "mat": ((2, FEATS, 2 * HEAD), BF16),
+    "kst": ((2, CHUNKS, 16, 2 * HEAD), BF16),
+    "mat": ((2, 2, FEATS // 2, 2 * HEAD), BF16),
     "d2": ((2, CHUNKS, 2, 16, HEAD), BF16),
     "d2o": ((2, CHUNKS, 2, 16, HEAD), BF16),
-    "dd": ((4, CHUNKS, 16, HEAD), BF16),
+    "dd": ((2, 2, 2, CHUNKS, 16, HEAD), BF16),
     "wown": ((2, 4, 4) + UNIT_W, F32),
     "wfin": ((2,) + UNIT_W, BF16),
     "wz": ((2, 2, 64, HEAD), BF16),
-    "igs": ((128, FEATS // 2), BF16),
-    "igr": ((128, FEATS // 2), BF16),
-    "igo": ((128, FEATS // 2), F32),
     **reduce_buffers("a", UNIT_KV),
     **reduce_buffers("w", UNIT_W),
 }
@@ -162,9 +160,12 @@
     across = ((d_tp, zh), ({ZH: oh, ZL: ol}, oh))
     d_zp, d_zm = {ZH: zp_h, ZL: zp_l}, {ZH: zm_h, ZL: zm_l}
     step_of = {a: ({a: turn(i, 1)}, {a: turn(i, 3)}) for a, i in ((X, x), (Y, y))}
+    far_of = {X: {X: turn(x, 2)}, Y: {Y: turn(y, 2)}}
+    d_zh = {ZH: oh}
     qi, pi = (y, x), (x, y)
     q_to = (step_of[Y], step_of[X])
     p_to = (step_of[X], step_of[Y])
+    p_far = (far_of[X], far_of[Y])
 
     names = {}
     pending = []
@@ -198,20 +199,32 @@
 
     kv, qg, xg, mat = b["kv"], b["qg"], b["xg"], b["mat"]
     own_x = local("x", x_in, xg.at[:, zh, :, lanes(zl * (FEATS // 2), FEATS // 2)])
-    own_m = [local("mk", mk_in, mat.at[0]), local("mv", mv_in, mat.at[1])]
+    half_feats = FEATS // 2
+    quarter_feats = FEATS // 4
+    own_m = [
+        local(("m", t), ref.at[pl.ds(pl.multiple_of(zl * half_feats, half_feats), half_feats), :], mat.at[0, t])
+        for t, ref in enumerate((mk_in, mv_in))
+    ]
+    kst = b["kst"]
+    stage = [local(("kst", t), ref, kst.at[t]) for t, ref in enumerate((k_in, v_in))]
+    for c in stage:
+        c.start()
 
     barrier = pltpu.get_barrier_semaphore()
-    peers = [d_core, *step_of[X], *step_of[Y], d_zp, d_zm]
+    peers = [d_core, *step_of[X], *step_of[Y], *far_of.values(), d_zp, d_zm, d_zh]
     for dev in peers:
         pl.semaphore_signal(barrier, inc=1, device_id=dev, device_id_type=MESH)
     pl.semaphore_wait(barrier, len(peers))
 
+    for c in stage:
+        c.wait()
+
     for h in range(2):
         for r, (dev, head) in enumerate(across):
-            for t, ref in enumerate((k_in, v_in)):
+            for t in range(2):
                 send(
                     ("zkv", h, t, r),
-                    ref.at[pl.ds(4 * h, 4), :, lanes(head * HEAD)],
+                    kst.at[t, pl.ds(4 * h, 4), :, lanes(head * HEAD)],
                     kv.at[h, qi[h], pi[h], t, :, zh],
                     dev,
                 )
@@ -280,11 +293,23 @@
                 arrived(("qz", t, r, g), qg.at[t, :, 2 * head + core, g])
             src = qg.at[t, :, 2 * head + core]
             send(("qc", t, r), src, src, d_core)
-    half_feats = FEATS // 2
-    quarter_feats = FEATS // 4
+
+    def send_matrix(t):
+        ref = (mk_in, mv_in)[t]
+        for r, (dev, _) in enumerate(across):
+            at = (2 * r + core) * 512
+            src = ref.at[pl.ds(pl.multiple_of(ol * half_feats + at, 512), 512), :]
+            dst = mat.at[1, t, pl.ds(pl.multiple_of(at, 512), 512), :]
+            yield ("m", t, r), src, dst, dev
+
+    def matrix_part(t, r, which):
+        return mat.at[1, t, pl.ds(pl.multiple_of((2 * r + which) * 512, 512), 512), :]
+
     mine = xg.at[:, zh, :, lanes(zl * half_feats, half_feats)]
     send("x+", x_in, mine, d_zp)
     send("x-", x_in, mine, d_zm)
+    for copy in send_matrix(0):
+        send(*copy)
     for h in range(2):
         for side in range(2):
             arrived(("pf", h, side), kv.at[h, qi[h], turn(pi[h], 2), side])
@@ -454,18 +479,10 @@
                 )
                 if n == 0:
                     far2[h] = value.astype(BF16)
-                    for side in range(2):
-                        send(
-                            (name, "far2", h, side),
-                            far2.at[h, side],
-                            rfar2.at[h, side],
-                            p_to[h][side],
-                        )
+                    send((name, "far2", h), far2.at[h], rfar2.at[h], p_far[h])
                 elif n < 3:
                     side = n - 1
-                    arrived((name, "far2", h, side), rfar2.at[h, side])
-                    near2[h, side, 1 - side] = value[1 - side].astype(BF16)
-                    near2[h, side, side] = (value[side] + rfar2[h, side].astype(F32)).astype(BF16)
+                    near2[h, side] = value.astype(BF16)
                     send(
                         (name, "near2", h, side),
                         near2.at[h, side],
@@ -475,8 +492,10 @@
                 else:
                     for side in range(2):
                         arrived((name, "near2", h, side), rnear2.at[h, side])
+                    arrived((name, "far2", h), rfar2.at[h])
                     out.append(
-                        value + rnear2[h, 0].astype(F32) + rnear2[h, 1].astype(F32)
+                        (value + rfar2[h].astype(F32))
+                        + (rnear2[h, 0].astype(F32) + rnear2[h, 1].astype(F32))
                     )
             return out
 
@@ -517,11 +536,13 @@
         @pl.when(s == 0)
         def _():
             start_far()
+            forward_input()
+            for copy in send_matrix(1):
+                remote(*copy).start()
 
         @pl.when(s == 1)
         def _():
             start_near(1)
-            forward_input()
 
         @pl.when(s == 2)
         def _():
@@ -532,6 +553,7 @@
     lax.fori_loop(0, 4, second_pass, 0)
     note_sends()
     forward_input(names_only=True)
+    pending.extend(send_matrix(1))
 
     dqf, dqr, dqs, dqz = b["dqf"], b["dqr"], b["dqs"], b["dqz"]
     for cq in range(CHUNKS):
@@ -567,7 +589,10 @@
     send("d2", d2, d2o, d_core)
     for r, (dev, other) in enumerate(across):
         for t in range(2):
-            send(("dz", t, r), d2.at[t, :, other], dd.at[2 * t + zh], dev)
+            send(("dz", t, r), d2.at[t, :, other], dd.at[0, t, zh], dev)
+    for t in range(2):
+        send(("dy", t), d2.at[t, :, oh], dd.at[1, t, zh], d_zh)
+        dd[1, t, zh] = d2[t, :, zh]
 
     wown = b["wown"]
 
@@ -577,22 +602,22 @@
     def weight_blocks(first):
         cols = grad_cols(d2 if first else d2o)
 
-        def body(i, carry):
-            wz = lax.rem(i, 2)
-            wy = lax.div(i, 2)
-            at = pl.ds(i * 4, 4)
-            rows = (xt[at, core] if first else xo[at]).reshape(256, 256)
+        def body(wy, carry):
+            at = pl.ds(wy * 8, 8)
+            rows = (xt[at, core] if first else xo[at]).reshape(512, 256)
             part = dot_nn(rows, cols)
-            for wx in range(4):
-                for h, (wq, wp) in enumerate(((wy, wx), (wx, wy))):
-                    block = part[wx * 64 : (wx + 1) * 64, h * HEAD : (h + 1) * HEAD]
-                    if first:
-                        wown[h, wq, wp, wz] = block
-                    else:
-                        wown[h, wq, wp, wz] = wown[h, wq, wp, wz] + block
+            for wz in range(2):
+                for wx in range(4):
+                    for h, (wq, wp) in enumerate(((wy, wx), (wx, wy))):
+                        base = (wz * 4 + wx) * 64
+                        block = part[base : base + 64, h * HEAD : (h + 1) * HEAD]
+                        if first:
+                            wown[h, wq, wp, wz] = block
+                        else:
+                            wown[h, wq, wp, wz] = wown[h, wq, wp, wz] + block
             return carry
 
-        lax.fori_loop(0, 8, body, 0)
+        lax.fori_loop(0, 4, body, 0)
 
     weight_blocks(True)
     arrived("xt", xo)
@@ -601,32 +626,36 @@
     w_far, w_near, w_note, w_unit = reducer("w", lambda h, q, p: wown[h, q, p])
     w_far()
 
-    igs, igr, igo, mat = b["igs"], b["igr"], b["igo"], b["mat"]
     for c in own_m:
         c.wait()
-    for r, (dev, other) in enumerate(across):
-        for t in range(2):
-            arrived(("dz", t, r), dd.at[2 * t + other])
-    dk_dv = [
-        jnp.concatenate([dd[2 * t].reshape(128, HEAD), dd[2 * t + 1].reshape(128, HEAD)], axis=1)
-        for t in range(2)
-    ]
-
-    def input_block(base, out):
-        def body(i, carry):
-            rows = pl.ds(pl.multiple_of(base + i * 512, 512), 512)
-            part = dot_tt(dk_dv[0], mat[0, rows, :]) + dot_tt(dk_dv[1], mat[1, rows, :])
-            out[:, lanes(i * 512, 512)] = part.astype(out.dtype)
-            return carry
-
-        lax.fori_loop(0, 4, body, 0)
-
-    input_block(ol * half_feats, igs)
-    send("ig", igs, igr, d_tp)
+    for t in range(2):
+        for r in range(2):
+            arrived(("m", t, r), matrix_part(t, r, core))
+            src = matrix_part(t, r, core)
+            send(("mc", t, r), src, src, d_core)
     w_near(0)
     w_near(1)
     w_note()
-    input_block(zl * half_feats, igo)
+    for t in range(2):
+        for r, (dev, other) in enumerate(across):
+            arrived(("dz", t, r), dd.at[0, t, other])
+            arrived(("mc", t, r), matrix_part(t, r, oc))
+        arrived(("dy", t), dd.at[1, t, oh])
+
+    def tokens(which, t):
+        return jnp.concatenate(
+            [dd[which, t, a].reshape(128, HEAD) for a in range(2)], axis=1
+        )
+
+    token_grads = jnp.concatenate([tokens(w, t) for w in range(2) for t in range(2)], axis=1)
+
+    def input_block(i, carry):
+        rows = pl.ds(pl.multiple_of(i * 512, 512), 512)
+        cols = jnp.concatenate([mat[w, t, rows, :] for w in range(2) for t in range(2)], axis=1)
+        ig_out[:, lanes(i * 512, 512)] = dot_tt(token_grads, cols).astype(BF16)
+        return carry
+
+    lax.fori_loop(0, 4, input_block, 0)
     for r, (dev, other) in enumerate(across):
         arrived(("dqz", r), dqz.at[other])
     dq_out[...] = dqz[...]
@@ -638,8 +667,6 @@
         wfin[h] = value.astype(BF16)
     for r, (dev, other) in enumerate(across):
         send(("ws", r), wfin.at[:, other], wz_ref.at[:, zh], dev)
-    arrived("ig", igr)
-    ig_out[...] = (igo[...] + igr[...].astype(F32)).astype(BF16)
     for r, (dev, other) in enumerate(across):
         arrived(("ws", r), wz_ref.at[:, other])
     w_out[...] = wz_ref[...].astype(F32)

time: 81.4 us -> 75.8 us (0.931)
  Pallas kernels: 80.5 us -> 75 us
    pallas_call x1, Pallas kernels: 78.4 us -> 72.8 us  [local_step(): pl.pallas_call(kernel, out_shape=(jax.ShapeDtypeStruct((2, CHUNKS, GROUP,...]
where the time goes in v4:
time: 75.8 us; the launch traced here: 75.6 us
  Pallas kernels  75 us (99%)
    pallas_call x1, Pallas kernels, local_step(): pl.pallas_call(kernel, out_shape=(jax.ShapeDtypeStruct((2, CHUNKS, GROUP,...  72.8 us
    pallas_call x1, Pallas kernels, local_step(): pl.pallas_call(finish, out_shape=(jax.ShapeDtypeStruct((128, 2 * GROUP *...  2.13 us

profile of v4, /device:TPU:0, one launch (start us, length us, event | category | flops | bytes accessed | tf_op | source)
XLA Modules:
  0.0 75.6 jit_solution(7976865598002346462)
XLA Ops:
  0.6 72.8 %shard_map.111 = (bf16[2,8,4,16,128]{4,3,2,1,0:T(8,128)(2,1)}, bf16[128,2048]{1,0:T(8,128)(2,1)}, f32[2,2,64,128]{3,2,1,0:T(8,128)}) custom-call(bf16[8,16,1024]{2,1,0:T(8,128)(2,1)} %bitcast.6, bf16[8,16,1024]{2,1,0:T(8,128)(2,1)} %bitcast.7, bf16[8,16,256]{2,1,0:T(8,128)(2,1)} %bitcast.8, bf16[8,16,256]{2,1,0:T(8,128)(2,1)} %bitcast.9, ...), custom_call_target="tpu_custom_call" | custom-call | tf_op jit(solution)/shard_map/pallas_call | solution.py:694
  73.5 2.1 %shard_map.112 = (bf16[128,1024]{1,0:T(8,128)(2,1)}, bf16[128,2048]{1,0:T(8,128)(2,1)}, f32[64,256]{1,0:T(8,128)}, f32[64,256]{1,0:T(8,128)}) custom-call(bf16[2,8,4,16,128]{4,3,2,1,0:T(8,128)(2,1)} %get-tuple-element.7.dq_in, bf16[128,2048]{1,0:T(8,128)(2,1)} %get-tuple-element.8.ig_in, f32[2,2,64,128]{3,2,1,0:T(8,128)} %get-tuple-element.9.w_in), custom_call_target="tpu_custom_call" | custom-call | tf_op jit(solution)/shard_map/pallas_call | solution.py:722

commit v5 on v4

--- a/solution.py
+++ b/solution.py
@@ -82,8 +82,10 @@
     "d2o": ((2, CHUNKS, 2, 16, HEAD), BF16),
     "dd": ((2, 2, 2, CHUNKS, 16, HEAD), BF16),
     "wown": ((2, 4, 4) + UNIT_W, F32),
-    "wfin": ((2,) + UNIT_W, BF16),
-    "wz": ((2, 2, 64, HEAD), BF16),
+    "wmine": ((2,) + UNIT_W, BF16),
+    "wz": ((4, 2, 2, 64, HEAD), BF16),
+    "wv": ((2, 2, 64, HEAD), F32),
+    "igv": ((128, FEATS // 2), BF16),
     **reduce_buffers("a", UNIT_KV),
     **reduce_buffers("w", UNIT_W),
 }
@@ -269,6 +271,7 @@
         unit = kv.at[h, qi[h], pi[h]]
         for side in range(2):
             send(("p", h, side), unit, unit, p_to[h][side])
+        send(("pf", h), unit, unit, p_far[h])
         send_unit(h, 0)
     own_x.start()
     for c in own_m:
@@ -282,7 +285,6 @@
         for side in range(2):
             src = kv.at[h, qi[h], turn(pi[h], 3 if side == 0 else 1)]
             arrived(("p", h, side), src)
-            send(("pf", h, side), src.at[side], src.at[side], p_to[h][side])
         for side in range(2):
             send_unit(h, 1 + side)
     for h in range(2):
@@ -311,8 +313,7 @@
     for copy in send_matrix(0):
         send(*copy)
     for h in range(2):
-        for side in range(2):
-            arrived(("pf", h, side), kv.at[h, qi[h], turn(pi[h], 2), side])
+        arrived(("pf", h), kv.at[h, qi[h], turn(pi[h], 2)])
         send_unit(h, 3)
     for t in range(2):
         for r, (dev, head) in enumerate(across):
@@ -412,7 +413,7 @@
 
     offs = (2, 1, 3, 0)
 
-    def reducer(name, unit_at):
+    def reducer(name, unit_at, deliver=None):
         far, rfar = b[name + "_far"], b[name + "_rfar"]
         near, rnear = b[name + "_near"], b[name + "_rnear"]
         far2, rfar2 = b[name + "_far2"], b[name + "_rfar2"]
@@ -477,7 +478,9 @@
                     + rnear[h, 0, p].astype(F32)
                     + rnear[h, 1, p].astype(F32)
                 )
-                if n == 0:
+                if deliver:
+                    deliver(h, n, value.astype(BF16))
+                elif n == 0:
                     far2[h] = value.astype(BF16)
                     send((name, "far2", h), far2.at[h], rfar2.at[h], p_far[h])
                 elif n < 3:
@@ -602,28 +605,41 @@
     def weight_blocks(first):
         cols = grad_cols(d2 if first else d2o)
 
-        def body(wy, carry):
-            at = pl.ds(wy * 8, 8)
-            rows = (xt[at, core] if first else xo[at]).reshape(512, 256)
-            part = dot_nn(rows, cols)
-            for wz in range(2):
-                for wx in range(4):
-                    for h, (wq, wp) in enumerate(((wy, wx), (wx, wy))):
-                        base = (wz * 4 + wx) * 64
-                        block = part[base : base + 64, h * HEAD : (h + 1) * HEAD]
-                        if first:
-                            wown[h, wq, wp, wz] = block
-                        else:
-                            wown[h, wq, wp, wz] = wown[h, wq, wp, wz] + block
+        def body(i, carry):
+            for wy in (2 * i, 2 * i + 1):
+                rows = (xt[pl.ds(wy * 8, 8), core] if first else xo[pl.ds(wy * 8, 8)]).reshape(512, 256)
+                part = dot_nn(rows, cols)
+                for wz in range(2):
+                    for wx in range(4):
+                        for h, (wq, wp) in enumerate(((wy, wx), (wx, wy))):
+                            base = (wz * 4 + wx) * 64
+                            block = part[base : base + 64, h * HEAD : (h + 1) * HEAD]
+                            if first:
+                                wown[h, wq, wp, wz] = block
+                            else:
+                                wown[h, wq, wp, wz] = wown[h, wq, wp, wz] + block
             return carry
 
-        lax.fori_loop(0, 4, body, 0)
+        lax.fori_loop(0, 2, body, 0)
 
     weight_blocks(True)
     arrived("xt", xo)
     arrived("d2", d2o)
     weight_blocks(False)
-    w_far, w_near, w_note, w_unit = reducer("w", lambda h, q, p: wown[h, q, p])
+    wz_ref = b["wz"]
+
+    def deliver(h, n, value):
+        kind, ref, hop = (
+            (3, b["w_far2"].at[h], p_far[h]),
+            (1, b["w_near2"].at[h, 0], p_to[h][0]),
+            (2, b["w_near2"].at[h, 1], p_to[h][1]),
+            (0, b["wmine"].at[h], {}),
+        )[n]
+        ref[...] = value
+        for r, (dev, other) in enumerate(across):
+            send(("ws", kind, h, r), ref.at[other], wz_ref.at[kind, h, zh], {**hop, **dev})
+
+    w_far, w_near, w_note, w_unit = reducer("w", lambda h, q, p: wown[h, q, p], deliver)
     w_far()
 
     for c in own_m:
@@ -652,24 +668,32 @@
     def input_block(i, carry):
         rows = pl.ds(pl.multiple_of(i * 512, 512), 512)
         cols = jnp.concatenate([mat[w, t, rows, :] for w in range(2) for t in range(2)], axis=1)
-        ig_out[:, lanes(i * 512, 512)] = dot_tt(token_grads, cols).astype(BF16)
+        igv[:, lanes(i * 512, 512)] = dot_tt(token_grads, cols).astype(BF16)
         return carry
 
+    igv = b["igv"]
     lax.fori_loop(0, 4, input_block, 0)
+    ig_copy = local("ig out", igv, ig_out)
+    ig_copy.start()
     for r, (dev, other) in enumerate(across):
         arrived(("dqz", r), dqz.at[other])
-    dq_out[...] = dqz[...]
-    w_unit(0)
-    w_unit(1)
-    w_unit(2)
-    wfin, wz_ref = b["wfin"], b["wz"]
-    for h, value in enumerate(w_unit(3)):
-        wfin[h] = value.astype(BF16)
-    for r, (dev, other) in enumerate(across):
-        send(("ws", r), wfin.at[:, other], wz_ref.at[:, zh], dev)
-    for r, (dev, other) in enumerate(across):
-        arrived(("ws", r), wz_ref.at[:, other])
-    w_out[...] = wz_ref[...].astype(F32)
+    outs = [local("dq out", dqz, dq_out)]
+    outs[0].start()
+    for n in range(4):
+        w_unit(n)
+    for kind in (3, 1, 2, 0):
+        for h in range(2):
+            for r, (dev, other) in enumerate(across):
+                arrived(("ws", kind, h, r), wz_ref.at[kind, h, other])
+    total_w = wz_ref[0].astype(F32)
+    for kind in range(1, 4):
+        total_w = total_w + wz_ref[kind].astype(F32)
+    b["wv"][...] = total_w
+    outs.append(local("w out", b["wv"], w_out))
+    outs[-1].start()
+    outs.append(ig_copy)
+    for c in outs:
+        c.wait()
 
     for copy in pending:
         remote(*copy).wait_send()
@@ -699,7 +723,7 @@
             jax.ShapeDtypeStruct((2, 2, 64, HEAD), F32),
         ),
         in_specs=[anywhere] * 7 + [vmem],
-        out_specs=(vmem, vmem, vmem),
+        out_specs=(anywhere,) * 3,
         scratch_shapes=[pltpu.VMEM(shape, dtype) for shape, dtype in BUFFERS.values()]
         + [
             pltpu.SemaphoreType.DMA((NSEM,)),

time: 75.8 us -> 70.8 us (0.934)
  Pallas kernels: 75 us -> 69.9 us
    pallas_call x1, Pallas kernels: 72.8 us -> 67.8 us  [local_step(): pl.pallas_call(kernel, out_shape=(jax.ShapeDtypeStruct((2, CHUNKS, GROUP,...]
where the time goes in v5:
time: 70.8 us; the launch traced here: 70.6 us
  Pallas kernels  69.9 us (99%)
    pallas_call x1, Pallas kernels, local_step(): pl.pallas_call(kernel, out_shape=(jax.ShapeDtypeStruct((2, CHUNKS, GROUP,...  67.8 us
    pallas_call x1, Pallas kernels, local_step(): pl.pallas_call(finish, out_shape=(jax.ShapeDtypeStruct((128, 2 * GROUP *...  2.13 us

profile of v5, /device:TPU:0, one launch (start us, length us, event | category | flops | bytes accessed | tf_op | source)
XLA Modules:
  0.0 70.6 jit_solution(1285981071960823584)
XLA Ops:
  0.6 67.8 %shard_map.111 = (bf16[2,8,4,16,128]{4,3,2,1,0:T(8,128)(2,1)}, bf16[128,2048]{1,0:T(8,128)(2,1)}, f32[2,2,64,128]{3,2,1,0:T(8,128)}) custom-call(bf16[8,16,1024]{2,1,0:T(8,128)(2,1)} %bitcast.6, bf16[8,16,1024]{2,1,0:T(8,128)(2,1)} %bitcast.7, bf16[8,16,256]{2,1,0:T(8,128)(2,1)} %bitcast.8, bf16[8,16,256]{2,1,0:T(8,128)(2,1)} %bitcast.9, ...), custom_call_target="tpu_custom_call" | custom-call | tf_op jit(solution)/shard_map/pallas_call | solution.py:718
  68.4 2.1 %shard_map.112 = (bf16[128,1024]{1,0:T(8,128)(2,1)}, bf16[128,2048]{1,0:T(8,128)(2,1)}, f32[64,256]{1,0:T(8,128)}, f32[64,256]{1,0:T(8,128)}) custom-call(bf16[2,8,4,16,128]{4,3,2,1,0:T(8,128)(2,1)} %get-tuple-element.7.dq_in, bf16[128,2048]{1,0:T(8,128)(2,1)} %get-tuple-element.8.ig_in, f32[2,2,64,128]{3,2,1,0:T(8,128)} %get-tuple-element.9.w_in), custom_call_target="tpu_custom_call" | custom-call | tf_op jit(solution)/shard_map/pallas_call | solution.py:746

commit v6 on v5

--- a/solution.py
+++ b/solution.py
@@ -25,8 +25,9 @@
 MASKED = -1e30
 QROWS = 256
 KROWS = 128
-NSEM = 192
-NLOCAL = 24
+NSEM = 69
+NSEND = 5
+NLOCAL = 8
 
 
 def key_chunks(cq):
@@ -170,25 +171,30 @@
     p_far = (far_of[X], far_of[Y])
 
     names = {}
-    pending = []
-
-    def remote(name, src, dst, dev):
+    sent = {}
+    filled = [0] * NSEND
+
+    def remote(name, src, dst, dev, group=0):
         i = names.setdefault(name, len(names))
         return pltpu.make_async_remote_copy(
             src_ref=src,
             dst_ref=dst,
-            send_sem=ssem.at[i],
+            send_sem=ssem.at[group],
             recv_sem=rsem.at[i],
             device_id=dev,
             device_id_type=MESH,
         )
 
-    def send(name, src, dst, dev):
-        remote(name, src, dst, dev).start()
-        pending.append((name, src, dst, dev))
-
-    def arrived(name, dst):
-        remote(name, dst, dst, d_core).wait_recv()
+    def send(name, part, src, dst, dev):
+        kib = math.prod(src.shape) * src.dtype.itemsize // 1024
+        if (name, part) not in sent:
+            group = min(range(NSEND), key=lambda n: filled[n])
+            filled[group] += kib
+            sent[name, part] = group
+        remote(name, src, dst, dev, sent[name, part]).start()
+
+    def arrived(name, size_of):
+        remote(name, size_of, size_of, d_core).wait_recv()
 
     local_names = {}
 
@@ -225,7 +231,8 @@
         for r, (dev, head) in enumerate(across):
             for t in range(2):
                 send(
-                    ("zkv", h, t, r),
+                    ("zkv", h),
+                    (t, r),
                     kst.at[t, pl.ds(4 * h, 4), :, lanes(head * HEAD)],
                     kv.at[h, qi[h], pi[h], t, :, zh],
                     dev,
@@ -234,7 +241,8 @@
         for r, (dev, head) in enumerate(across):
             for g in range(GROUP):
                 send(
-                    ("qz", t, r, g),
+                    ("qz", t, r),
+                    g,
                     ref.at[:, :, lanes(head * GROUP * HEAD + g * HEAD)],
                     qg.at[t, :, 2 * zh + core, g],
                     dev,
@@ -244,7 +252,7 @@
 
     def unit_piece(h, n, side):
         unit = kv.at[h, qi[h], turn(pi[h], unit_offs[n])]
-        return ("q", h, n, side), unit, unit, q_to[h][side]
+        return ("q", h, n), side, unit, unit, q_to[h][side]
 
     def send_unit(h, n):
         for side in range(2):
@@ -255,23 +263,19 @@
 
     def forward_piece(h, n, side):
         src = near_piece(h, n, side).at[side]
-        return ("qf", h, n, side), src, src, q_to[h][side]
+        return ("qf", h, side), n, src, src, q_to[h][side]
 
     def forward_unit(h, n):
+        arrived(("q", h, n), kv.at[h, 0, pl.ds(0, 2)])
         for side in range(2):
-            arrived(("q", h, n, side), near_piece(h, n, side))
-            remote(*forward_piece(h, n, side)).start()
-            if n == 0:
-                pending.append(forward_piece(h, n, side))
+            send(*forward_piece(h, n, side))
 
     for h in range(2):
-        for r, (dev, head) in enumerate(across):
-            for t in range(2):
-                arrived(("zkv", h, t, r), kv.at[h, qi[h], pi[h], t, :, head])
+        arrived(("zkv", h), kv.at[h, qi[h], pi[h]])
         unit = kv.at[h, qi[h], pi[h]]
         for side in range(2):
-            send(("p", h, side), unit, unit, p_to[h][side])
-        send(("pf", h), unit, unit, p_far[h])
+            send(("p", h, side), 0, unit, unit, p_to[h][side])
+        send(("pf", h), 0, unit, unit, p_far[h])
         send_unit(h, 0)
     own_x.start()
     for c in own_m:
@@ -291,10 +295,9 @@
         forward_unit(h, 0)
     for t in range(2):
         for r, (dev, head) in enumerate(across):
-            for g in range(GROUP):
-                arrived(("qz", t, r, g), qg.at[t, :, 2 * head + core, g])
             src = qg.at[t, :, 2 * head + core]
-            send(("qc", t, r), src, src, d_core)
+            arrived(("qz", t, r), src)
+            send(("qc", t), r, src, src, d_core)
 
     def send_matrix(t):
         ref = (mk_in, mv_in)[t]
@@ -302,22 +305,21 @@
             at = (2 * r + core) * 512
             src = ref.at[pl.ds(pl.multiple_of(ol * half_feats + at, 512), 512), :]
             dst = mat.at[1, t, pl.ds(pl.multiple_of(at, 512), 512), :]
-            yield ("m", t, r), src, dst, dev
+            yield ("m", t, r), 0, src, dst, dev
 
     def matrix_part(t, r, which):
         return mat.at[1, t, pl.ds(pl.multiple_of((2 * r + which) * 512, 512), 512), :]
 
     mine = xg.at[:, zh, :, lanes(zl * half_feats, half_feats)]
-    send("x+", x_in, mine, d_zp)
-    send("x-", x_in, mine, d_zm)
+    send("x+", 0, x_in, mine, d_zp)
+    send("x-", 0, x_in, mine, d_zm)
     for copy in send_matrix(0):
         send(*copy)
     for h in range(2):
         arrived(("pf", h), kv.at[h, qi[h], turn(pi[h], 2)])
         send_unit(h, 3)
     for t in range(2):
-        for r, (dev, head) in enumerate(across):
-            arrived(("qc", t, r), qg.at[t, :, 2 * head + oc])
+        arrived(("qc", t), qg.at[t, pl.ds(0, CHUNKS // 2)])
 
     def queries(t, cq):
         return qg[t, cq].reshape(QROWS, HEAD)
@@ -341,13 +343,9 @@
 
         @pl.when(s == 3)
         def _():
-            for n in range(4):
-                for h in range(2):
-                    for side in range(2):
-                        arrived(
-                            ("qf", h, n, side),
-                            kv.at[h, turn(qi[h], 2), turn(pi[h], unit_offs[n]), side],
-                        )
+            for h in range(2):
+                for side in range(2):
+                    arrived(("qf", h, side), kv.at[h, turn(qi[h], 2), :, side])
 
         at = (turn(y, off), turn(x, off))
         for cq in range(CHUNKS):
@@ -375,12 +373,6 @@
         return carry
 
     lax.fori_loop(0, 4, first_pass, 0)
-    for h in range(2):
-        for n in range(4):
-            for side in range(2):
-                if n:
-                    pending.append(forward_piece(h, n, side))
-
     ss, sr = b["ss"], b["sr"]
     top_l = jnp.max(st[0], axis=(0, 1))
     fac_l = jnp.exp2(st[0] - top_l[None, None])
@@ -389,19 +381,16 @@
     ss[0] = top_l
     ss[1] = sum_l
     ss[2] = wgt_l
-    send("stat", ss, sr, d_core)
-
-    def forward_input(names_only=False):
+    send("stat", 0, ss, sr, d_core)
+
+    def forward_input():
         for name, src_h, src_l, start, dev in (
             ("x+", zm_h, zm_l, 0, d_zp),
             ("x-", zp_h, zp_l, quarter_feats, d_zm),
         ):
             src = xg.at[:, src_h, :, lanes(src_l * half_feats + start, quarter_feats)]
-            if names_only:
-                pending.append(("far " + name, src, src, dev))
-            else:
-                arrived(name, xg.at[:, src_h, :, lanes(src_l * half_feats, half_feats)])
-                remote("far " + name, src, src, dev).start()
+            arrived(name, xg.at[:, src_h, :, lanes(src_l * half_feats, half_feats)])
+            send("far " + name, 0, src, src, dev)
 
     arrived("stat", sr)
     top = jnp.maximum(top_l, sr[0])
@@ -425,7 +414,8 @@
         def far_copy(h, n, side):
             p = place(h, n)
             return (
-                (name, "far", h, n, side),
+                (name, "far", n, side),
+                h,
                 far.at[h, p, side],
                 rfar.at[h, side, p],
                 q_to[h][side],
@@ -434,7 +424,8 @@
         def near_copy(h, n, side):
             p = place(h, n)
             return (
-                (name, "near", h, n, side),
+                (name, "near", n),
+                (h, side),
                 near.at[h, side, p],
                 rnear.at[h, side, p],
                 q_to[h][side],
@@ -446,33 +437,25 @@
                     p = place(h, n)
                     far[h, p] = unit_at(h, turn(qi[h], 2), p).astype(BF16)
                     for side in range(2):
-                        remote(*far_copy(h, n, side)).start()
+                        send(*far_copy(h, n, side))
 
         def start_near(side):
             for n in range(4):
+                arrived((name, "far", n, side), rfar.at[0, side, pl.ds(0, 2)])
                 for h in range(2):
                     p = place(h, n)
                     value = unit_at(h, turn(qi[h], 1 if side == 0 else 3), p)
-                    arrived((name, "far", h, n, side), rfar.at[h, side, p])
                     near[h, side, p, 1 - side] = value[1 - side].astype(BF16)
                     near[h, side, p, side] = (value[side] + rfar[h, side, p].astype(F32)).astype(
                         BF16
                     )
-                    remote(*near_copy(h, n, side)).start()
-
-        def note_sends():
-            for h in range(2):
-                for n in range(4):
-                    for side in range(2):
-                        pending.append(far_copy(h, n, side))
-                        pending.append(near_copy(h, n, side))
+                    send(*near_copy(h, n, side))
 
         def own_unit(n):
             out = []
+            arrived((name, "near", n), rnear.at[0, 0])
             for h in range(2):
                 p = place(h, n)
-                for side in range(2):
-                    arrived((name, "near", h, n, side), rnear.at[h, side, p])
                 value = (
                     unit_at(h, qi[h], p)
                     + rnear[h, 0, p].astype(F32)
@@ -482,30 +465,29 @@
                     deliver(h, n, value.astype(BF16))
                 elif n == 0:
                     far2[h] = value.astype(BF16)
-                    send((name, "far2", h), far2.at[h], rfar2.at[h], p_far[h])
+                    send((name, "p", h), 2, far2.at[h], rfar2.at[h], p_far[h])
                 elif n < 3:
                     side = n - 1
                     near2[h, side] = value.astype(BF16)
                     send(
-                        (name, "near2", h, side),
+                        (name, "p", h),
+                        side,
                         near2.at[h, side],
                         rnear2.at[h, side],
                         p_to[h][side],
                     )
                 else:
-                    for side in range(2):
-                        arrived((name, "near2", h, side), rnear2.at[h, side])
-                    arrived((name, "far2", h), rfar2.at[h])
+                    arrived((name, "p", h), rnear.at[0, 0, pl.ds(0, 3)])
                     out.append(
                         (value + rfar2[h].astype(F32))
                         + (rnear2[h, 0].astype(F32) + rnear2[h, 1].astype(F32))
                     )
             return out
 
-        return start_far, start_near, note_sends, own_unit
+        return start_far, start_near, own_unit
 
     acc = b["acc"]
-    start_far, start_near, note_sends, own_unit = reducer("a", lambda h, q, p: acc[h, p])
+    start_far, start_near, own_unit = reducer("a", lambda h, q, p: acc[h, p])
 
     fac, delta, kt = b["fac"], b["delta"], b["kt"]
 
@@ -541,7 +523,7 @@
             start_far()
             forward_input()
             for copy in send_matrix(1):
-                remote(*copy).start()
+                send(*copy)
 
         @pl.when(s == 1)
         def _():
@@ -554,14 +536,10 @@
         return carry
 
     lax.fori_loop(0, 4, second_pass, 0)
-    note_sends()
-    forward_input(names_only=True)
-    pending.extend(send_matrix(1))
-
     dqf, dqr, dqs, dqz = b["dqf"], b["dqr"], b["dqs"], b["dqz"]
     for cq in range(CHUNKS):
         dqf[cq] = (dqt[cq].T * SCALE).reshape(2, 2, GROUP, 16, HEAD)
-    send("dqc", dqf.at[:, :, oc], dqr, d_core)
+    send("dqc", 0, dqf.at[:, :, oc], dqr, d_core)
     own_unit(0)
     own_x.wait()
     far_h = 1 - zh
@@ -577,24 +555,24 @@
         return carry
 
     lax.fori_loop(0, 8, flip_input, 0)
-    send("xt", xt.at[:, oc], xo, d_core)
+    send("xt", 0, xt.at[:, oc], xo, d_core)
     own_unit(1)
     own_unit(2)
     arrived("dqc", dqr)
     for n in range(2):
         dqs[n] = (dqf[:, n, core] + dqr[:, n]).astype(BF16)
     for r, (dev, other) in enumerate(across):
-        send(("dqz", r), dqs.at[other], dqz.at[zh], dev)
+        send("dqz", r, dqs.at[other], dqz.at[zh], dev)
     d2, d2o, dd = b["d2"], b["d2o"], b["dd"]
     for h, value in enumerate(own_unit(3)):
         d2[0, 4 * h : 4 * h + 4] = (value[0] * SCALE).astype(BF16)
         d2[1, 4 * h : 4 * h + 4] = value[1].astype(BF16)
-    send("d2", d2, d2o, d_core)
+    send("d2", 0, d2, d2o, d_core)
     for r, (dev, other) in enumerate(across):
         for t in range(2):
-            send(("dz", t, r), d2.at[t, :, other], dd.at[0, t, zh], dev)
+            send("dz", (t, r), d2.at[t, :, other], dd.at[0, t, zh], dev)
     for t in range(2):
-        send(("dy", t), d2.at[t, :, oh], dd.at[1, t, zh], d_zh)
+        send("dy", t, d2.at[t, :, oh], dd.at[1, t, zh], d_zh)
         dd[1, t, zh] = d2[t, :, zh]
 
     wown = b["wown"]
@@ -637,9 +615,9 @@
         )[n]
         ref[...] = value
         for r, (dev, other) in enumerate(across):
-            send(("ws", kind, h, r), ref.at[other], wz_ref.at[kind, h, zh], {**hop, **dev})
-
-    w_far, w_near, w_note, w_unit = reducer("w", lambda h, q, p: wown[h, q, p], deliver)
+            send("ws", (kind, h, r), ref.at[other], wz_ref.at[kind, h, zh], {**hop, **dev})
+
+    w_far, w_near, w_unit = reducer("w", lambda h, q, p: wown[h, q, p], deliver)
     w_far()
 
     for c in own_m:
@@ -648,15 +626,12 @@
         for r in range(2):
             arrived(("m", t, r), matrix_part(t, r, core))
             src = matrix_part(t, r, core)
-            send(("mc", t, r), src, src, d_core)
+            send("mc", (t, r), src, src, d_core)
     w_near(0)
     w_near(1)
-    w_note()
-    for t in range(2):
-        for r, (dev, other) in enumerate(across):
-            arrived(("dz", t, r), dd.at[0, t, other])
-            arrived(("mc", t, r), matrix_part(t, r, oc))
-        arrived(("dy", t), dd.at[1, t, oh])
+    arrived("dz", dd.at[0])
+    arrived("dy", dd.at[1, :, oh])
+    arrived("mc", mat.at[1, 0])
 
     def tokens(which, t):
         return jnp.concatenate(
@@ -675,16 +650,12 @@
     lax.fori_loop(0, 4, input_block, 0)
     ig_copy = local("ig out", igv, ig_out)
     ig_copy.start()
-    for r, (dev, other) in enumerate(across):
-        arrived(("dqz", r), dqz.at[other])
+    arrived("dqz", dqz)
     outs = [local("dq out", dqz, dq_out)]
     outs[0].start()
     for n in range(4):
         w_unit(n)
-    for kind in (3, 1, 2, 0):
-        for h in range(2):
-            for r, (dev, other) in enumerate(across):
-                arrived(("ws", kind, h, r), wz_ref.at[kind, h, other])
+    arrived("ws", wz_ref)
     total_w = wz_ref[0].astype(F32)
     for kind in range(1, 4):
         total_w = total_w + wz_ref[kind].astype(F32)
@@ -695,8 +666,9 @@
     for c in outs:
         c.wait()
 
-    for copy in pending:
-        remote(*copy).wait_send()
+    for group, kib in enumerate(filled):
+        size_of = e_ref.at[0, pl.ds(0, kib), :]
+        pltpu.make_async_copy(size_of, size_of, ssem.at[group]).wait()
     assert len(names) <= NSEM and len(local_names) <= NLOCAL
 
 
@@ -726,7 +698,7 @@
         out_specs=(anywhere,) * 3,
         scratch_shapes=[pltpu.VMEM(shape, dtype) for shape, dtype in BUFFERS.values()]
         + [
-            pltpu.SemaphoreType.DMA((NSEM,)),
+            pltpu.SemaphoreType.DMA((NSEND,)),
             pltpu.SemaphoreType.DMA((NSEM,)),
             pltpu.SemaphoreType.DMA((NLOCAL,)),
         ],

time: 70.8 us -> 67.7 us (0.956)
  Pallas kernels: 69.9 us -> 66.9 us
    pallas_call x1, Pallas kernels: 67.8 us -> 64.7 us  [local_step(): pl.pallas_call(kernel, out_shape=(jax.ShapeDtypeStruct((2, CHUNKS, GROUP,...]
where the time goes in v6:
time: 67.7 us; the launch traced here: 67.5 us
  Pallas kernels  66.9 us (99%)
    pallas_call x1, Pallas kernels, local_step(): pl.pallas_call(kernel, out_shape=(jax.ShapeDtypeStruct((2, CHUNKS, GROUP,...  64.7 us
    pallas_call x1, Pallas kernels, local_step(): pl.pallas_call(finish, out_shape=(jax.ShapeDtypeStruct((128, 2 * GROUP *...  2.13 us

profile of v6, /device:TPU:0, one launch (start us, length us, event | category | flops | bytes accessed | tf_op | source)
XLA Modules:
  0.0 67.5 jit_solution(443226430437243885)
XLA Ops:
  0.6 64.7 %shard_map.111 = (bf16[2,8,4,16,128]{4,3,2,1,0:T(8,128)(2,1)}, bf16[128,2048]{1,0:T(8,128)(2,1)}, f32[2,2,64,128]{3,2,1,0:T(8,128)}) custom-call(bf16[8,16,1024]{2,1,0:T(8,128)(2,1)} %bitcast.6, bf16[8,16,1024]{2,1,0:T(8,128)(2,1)} %bitcast.7, bf16[8,16,256]{2,1,0:T(8,128)(2,1)} %bitcast.8, bf16[8,16,256]{2,1,0:T(8,128)(2,1)} %bitcast.9, ...), custom_call_target="tpu_custom_call" | custom-call | tf_op jit(solution)/shard_map/pallas_call | solution.py:690
  65.4 2.1 %shard_map.112 = (bf16[128,1024]{1,0:T(8,128)(2,1)}, bf16[128,2048]{1,0:T(8,128)(2,1)}, f32[64,256]{1,0:T(8,128)}, f32[64,256]{1,0:T(8,128)}) custom-call(bf16[2,8,4,16,128]{4,3,2,1,0:T(8,128)(2,1)} %get-tuple-element.7.dq_in, bf16[128,2048]{1,0:T(8,128)(2,1)} %get-tuple-element.8.ig_in, f32[2,2,64,128]{3,2,1,0:T(8,128)} %get-tuple-element.9.w_in), custom_call_target="tpu_custom_call" | custom-call | tf_op jit(solution)/shard_map/pallas_call | solution.py:718

commit v7 on v6

--- a/solution.py
+++ b/solution.py
@@ -25,7 +25,7 @@
 MASKED = -1e30
 QROWS = 256
 KROWS = 128
-NSEM = 69
+NSEM = 71
 NSEND = 5
 NLOCAL = 8
 
@@ -66,13 +66,12 @@
     "sr": ((3, CHUNKS, QROWS), F32),
     "fac": ((4, BAND + 1, CHUNKS, QROWS), F32),
     "delta": ((CHUNKS, QROWS), F32),
-    "acc": ((2, 4) + UNIT_KV, F32),
-    "dqt": ((CHUNKS, HEAD, QROWS), F32),
+    "acc": ((2, 2, 4) + UNIT_KV, F32),
     "dqf": ((CHUNKS, 2, 2, GROUP, 16, HEAD), F32),
     "dqr": ((CHUNKS, 2, GROUP, 16, HEAD), F32),
     "dqs": ((2, CHUNKS, GROUP, 16, HEAD), BF16),
     "dqz": ((2, CHUNKS, GROUP, 16, HEAD), BF16),
-    "kt": ((CHUNKS, HEAD, KROWS), BF16),
+    "kt": ((4, CHUNKS, HEAD, KROWS), BF16),
     "qp": ((CHUNKS, QROWS), F32),
     "xg": ((CHUNKS, 2, 16, FEATS), BF16),
     "xt": ((32, 2, 64, 256), BF16),
@@ -84,8 +83,6 @@
     "dd": ((2, 2, 2, CHUNKS, 16, HEAD), BF16),
     "wown": ((2, 4, 4) + UNIT_W, F32),
     "wmine": ((2,) + UNIT_W, BF16),
-    "wz": ((4, 2, 2, 64, HEAD), BF16),
-    "wv": ((2, 2, 64, HEAD), F32),
     "igv": ((128, FEATS // 2), BF16),
     **reduce_buffers("a", UNIT_KV),
     **reduce_buffers("w", UNIT_W),
@@ -280,8 +277,6 @@
     own_x.start()
     for c in own_m:
         c.start()
-    dqt = b["dqt"]
-    dqt[...] = jnp.zeros(dqt.shape, F32)
     b["st"][0] = jnp.full(b["st"].shape[1:], MASKED, F32)
     b["st"][1:] = jnp.zeros((2,) + b["st"].shape[1:], F32)
     positions(rp_in, b["kpb"], b["qp"], y, x, core)
@@ -310,17 +305,45 @@
     def matrix_part(t, r, which):
         return mat.at[1, t, pl.ds(pl.multiple_of((2 * r + which) * 512, 512), 512), :]
 
-    mine = xg.at[:, zh, :, lanes(zl * half_feats, half_feats)]
-    send("x+", 0, x_in, mine, d_zp)
-    send("x-", 0, x_in, mine, d_zm)
-    for copy in send_matrix(0):
-        send(*copy)
+    ring = (
+        ("x+", d_zp, zm_h, zm_l, 0),
+        ("x-", d_zm, zp_h, zp_l, quarter_feats),
+    )
+    for second in range(2):
+        for name, dev, _, _, first in ring:
+            at = quarter_feats - first if second else first
+            send(
+                (name, second),
+                0,
+                x_in.at[:, :, pl.ds(at, quarter_feats)],
+                xg.at[:, zh, :, lanes(zl * half_feats + at, quarter_feats)],
+                dev,
+            )
+
+    def ring_part(src_h, src_l, at):
+        return xg.at[:, src_h, :, lanes(src_l * half_feats + at, quarter_feats)]
+
+    def forward_input():
+        for name, dev, src_h, src_l, first in ring:
+            src = ring_part(src_h, src_l, first)
+            arrived((name, 0), src)
+            send((name, 2), 0, src, src, dev)
+
+    def wait_input():
+        own_x.wait()
+        for name, _, src_h, src_l, first in ring:
+            arrived((name, 1), ring_part(src_h, src_l, quarter_feats - first))
+            arrived((name, 2), ring_part(oh, zl, first))
+
     for h in range(2):
         arrived(("pf", h), kv.at[h, qi[h], turn(pi[h], 2)])
         send_unit(h, 3)
     for t in range(2):
         arrived(("qc", t), qg.at[t, pl.ds(0, CHUNKS // 2)])
 
+    def tile_rows(cq, ck):
+        return pl.ds(TILE_AT[cq] + (ck - key_chunks(cq)[0]) * KROWS, KROWS)
+
     def queries(t, cq):
         return qg[t, cq].reshape(QROWS, HEAD)
 
@@ -346,6 +369,10 @@
             for h in range(2):
                 for side in range(2):
                     arrived(("qf", h, side), kv.at[h, turn(qi[h], 2), :, side])
+            forward_input()
+            for t in range(2):
+                for copy in send_matrix(t):
+                    send(*copy)
 
         at = (turn(y, off), turn(x, off))
         for cq in range(CHUNKS):
@@ -363,7 +390,7 @@
                     score = jnp.where(seen, score, MASKED)
                 top = jnp.max(score, axis=0, keepdims=True)
                 expo = jnp.exp2(score - top)
-                rows = pl.ds(TILE_AT[cq] + n * KROWS, KROWS)
+                rows = tile_rows(cq, ck)
                 e_ref[off, rows, :] = expo
                 dp_ref[off, rows, :] = dprob
                 row = slice(cq, cq + 1)
@@ -383,15 +410,6 @@
     ss[2] = wgt_l
     send("stat", 0, ss, sr, d_core)
 
-    def forward_input():
-        for name, src_h, src_l, start, dev in (
-            ("x+", zm_h, zm_l, 0, d_zp),
-            ("x-", zp_h, zp_l, quarter_feats, d_zm),
-        ):
-            src = xg.at[:, src_h, :, lanes(src_l * half_feats + start, quarter_feats)]
-            arrived(name, xg.at[:, src_h, :, lanes(src_l * half_feats, half_feats)])
-            send("far " + name, 0, src, src, dev)
-
     arrived("stat", sr)
     top = jnp.maximum(top_l, sr[0])
     mine_f = jnp.exp2(top_l - top)
@@ -435,16 +453,16 @@
             for n in range(4):
                 for h in range(2):
                     p = place(h, n)
-                    far[h, p] = unit_at(h, turn(qi[h], 2), p).astype(BF16)
+                    far[h, p] = unit_at(h, turn(qi[h], 2), p, 0).astype(BF16)
                     for side in range(2):
                         send(*far_copy(h, n, side))
 
-        def start_near(side):
-            for n in range(4):
+        def start_near(n):
+            for side in (1, 0):
                 arrived((name, "far", n, side), rfar.at[0, side, pl.ds(0, 2)])
                 for h in range(2):
                     p = place(h, n)
-                    value = unit_at(h, turn(qi[h], 1 if side == 0 else 3), p)
+                    value = unit_at(h, turn(qi[h], 1 if side == 0 else 3), p, 1 - side)
                     near[h, side, p, 1 - side] = value[1 - side].astype(BF16)
                     near[h, side, p, side] = (value[side] + rfar[h, side, p].astype(F32)).astype(
                         BF16
@@ -457,7 +475,7 @@
             for h in range(2):
                 p = place(h, n)
                 value = (
-                    unit_at(h, qi[h], p)
+                    unit_at(h, qi[h], p, 0)
                     + rnear[h, 0, p].astype(F32)
                     + rnear[h, 1, p].astype(F32)
                 )
@@ -487,64 +505,46 @@
         return start_far, start_near, own_unit
 
     acc = b["acc"]
-    start_far, start_near, own_unit = reducer("a", lambda h, q, p: acc[h, p])
+    start_far, start_near, own_unit = reducer(
+        "a", lambda h, q, p, slot: acc[slot, h, p]
+    )
 
     fac, delta, kt = b["fac"], b["delta"], b["kt"]
 
     def second_pass(s, carry):
         late = lax.div(s, 2)
         off = (1 - late) * (2 + s) + late * (3 - s)
-        at = (turn(y, off), turn(x, off))
+        slot = late * (3 - s)
         for ck in range(CHUNKS):
-            kt[ck] = keys(0, at, [ck]).T
-        for cq in range(CHUNKS):
-            cks = key_chunks(cq)
             probs, dscores = [], []
-            for n, ck in enumerate(cks):
-                rows = pl.ds(TILE_AT[cq] + n * KROWS, KROWS)
+            cqs = [cq for cq in range(CHUNKS) if ck in key_chunks(cq)]
+            for cq in cqs:
+                rows = tile_rows(cq, ck)
                 prob = e_ref[off, rows, :] * fac[off, cq - ck, cq : cq + 1, :]
-                diff = dp_ref[off, rows, :] - delta[cq : cq + 1, :]
+                dscore = prob * (dp_ref[off, rows, :] - delta[cq : cq + 1, :])
+                e_ref[off, rows, :] = dscore
                 probs.append(prob.astype(BF16))
-                dscores.append((prob * diff).astype(BF16))
-            prob, dscore = stack_rows(probs), stack_rows(dscores)
-            grads = (dot_nn(dscore, queries(0, cq)), dot_nn(prob, queries(1, cq)))
-            for t in range(2):
-                for n, ck in enumerate(cks):
-                    part = grads[t][n * KROWS : (n + 1) * KROWS].reshape(4, 2, 16, HEAD)
-                    if ck == cq:
-                        acc[ck // 4, :, t, ck % 4] = part
-                    else:
-                        acc[ck // 4, :, t, ck % 4] = acc[ck // 4, :, t, ck % 4] + part
-            flipped = jnp.concatenate([kt[ck] for ck in cks], axis=1)
-            dqt[cq] = dqt[cq] + dot_nn(flipped, dscore)
+                dscores.append(dscore.astype(BF16))
+            for t, parts in enumerate((dscores, probs)):
+                depth = qg[t, ck : ck + len(cqs)].reshape(len(cqs) * QROWS, HEAD)
+                grad = dot_nn(jnp.concatenate(parts, axis=1), depth)
+                acc[slot, ck // 4, :, t, ck % 4] = grad.reshape(4, 2, 16, HEAD)
 
         @pl.when(s == 0)
         def _():
             start_far()
-            forward_input()
-            for copy in send_matrix(1):
-                send(*copy)
-
-        @pl.when(s == 1)
-        def _():
-            start_near(1)
 
         @pl.when(s == 2)
         def _():
-            start_near(0)
+            for n in range(4):
+                start_near(n)
 
         return carry
 
     lax.fori_loop(0, 4, second_pass, 0)
     dqf, dqr, dqs, dqz = b["dqf"], b["dqr"], b["dqs"], b["dqz"]
-    for cq in range(CHUNKS):
-        dqf[cq] = (dqt[cq].T * SCALE).reshape(2, 2, GROUP, 16, HEAD)
-    send("dqc", 0, dqf.at[:, :, oc], dqr, d_core)
     own_unit(0)
-    own_x.wait()
-    far_h = 1 - zh
-    arrived("far x+", xg.at[:, far_h, :, lanes(zl * half_feats, quarter_feats)])
-    arrived("far x-", xg.at[:, far_h, :, lanes(zl * half_feats + quarter_feats, quarter_feats)])
+    wait_input()
     xt, xo = b["xt"], b["xo"]
 
     def flip_input(i, carry):
@@ -558,11 +558,17 @@
     send("xt", 0, xt.at[:, oc], xo, d_core)
     own_unit(1)
     own_unit(2)
-    arrived("dqc", dqr)
-    for n in range(2):
-        dqs[n] = (dqf[:, n, core] + dqr[:, n]).astype(BF16)
-    for r, (dev, other) in enumerate(across):
-        send("dqz", r, dqs.at[other], dqz.at[zh], dev)
+    for off in range(4):
+        at = (turn(y, off), turn(x, off))
+        for ck in range(CHUNKS):
+            kt[off, ck] = keys(0, at, [ck]).T
+    for cq in range(CHUNKS):
+        cks = key_chunks(cq)
+        rows = pl.ds(TILE_AT[cq], KROWS * len(cks))
+        flipped = jnp.concatenate([kt[off, ck] for off in range(4) for ck in cks], axis=1)
+        dscore = jnp.concatenate([e_ref[off, rows, :].astype(BF16) for off in range(4)], axis=0)
+        dqf[cq] = (dot_nn(flipped, dscore).T * SCALE).reshape(2, 2, GROUP, 16, HEAD)
+    send("dqc", 0, dqf.at[:, :, oc], dqr, d_core)
     d2, d2o, dd = b["d2"], b["d2o"], b["dd"]
     for h, value in enumerate(own_unit(3)):
         d2[0, 4 * h : 4 * h + 4] = (value[0] * SCALE).astype(BF16)
@@ -601,11 +607,14 @@
         lax.fori_loop(0, 2, body, 0)
 
     weight_blocks(True)
+    arrived("dqc", dqr)
+    for n in range(2):
+        dqs[n] = (dqf[:, n, core] + dqr[:, n]).astype(BF16)
+    for r, (dev, other) in enumerate(across):
+        send("dqz", r, dqs.at[other], dqz.at[zh], dev)
     arrived("xt", xo)
     arrived("d2", d2o)
     weight_blocks(False)
-    wz_ref = b["wz"]
-
     def deliver(h, n, value):
         kind, ref, hop = (
             (3, b["w_far2"].at[h], p_far[h]),
@@ -615,20 +624,22 @@
         )[n]
         ref[...] = value
         for r, (dev, other) in enumerate(across):
-            send("ws", (kind, h, r), ref.at[other], wz_ref.at[kind, h, zh], {**hop, **dev})
-
-    w_far, w_near, w_unit = reducer("w", lambda h, q, p: wown[h, q, p], deliver)
+            send("ws", (kind, h, r), ref.at[other], w_out.at[kind, h, zh], {**hop, **dev})
+
+    w_far, w_near, w_unit = reducer("w", lambda h, q, p, slot: wown[h, q, p], deliver)
     w_far()
 
+    for n in range(4):
+        w_near(n)
     for c in own_m:
         c.wait()
     for t in range(2):
         for r in range(2):
-            arrived(("m", t, r), matrix_part(t, r, core))
             src = matrix_part(t, r, core)
+            arrived(("m", t, r), src)
             send("mc", (t, r), src, src, d_core)
-    w_near(0)
-    w_near(1)
+    for n in range(4):
+        w_unit(n)
     arrived("dz", dd.at[0])
     arrived("dy", dd.at[1, :, oh])
     arrived("mc", mat.at[1, 0])
@@ -653,15 +664,7 @@
     arrived("dqz", dqz)
     outs = [local("dq out", dqz, dq_out)]
     outs[0].start()
-    for n in range(4):
-        w_unit(n)
-    arrived("ws", wz_ref)
-    total_w = wz_ref[0].astype(F32)
-    for kind in range(1, 4):
-        total_w = total_w + wz_ref[kind].astype(F32)
-    b["wv"][...] = total_w
-    outs.append(local("w out", b["wv"], w_out))
-    outs[-1].start()
+    arrived("ws", w_out)
     outs.append(ig_copy)
     for c in outs:
         c.wait()
@@ -681,7 +684,8 @@
     ig_out[...] = ig_in[...]
     for t, out in enumerate((kw_out, vw_out)):
         for n in range(2):
-            out[:, n * HEAD : (n + 1) * HEAD] = w_in[t, n]
+            parts = [w_in[kind, t, n].astype(F32) for kind in range(4)]
+            out[:, n * HEAD : (n + 1) * HEAD] = (parts[0] + parts[1]) + (parts[2] + parts[3])
 
 
 def local_step(q, k, v, g, x, mk, mv, placement):
@@ -692,7 +696,7 @@
         out_shape=(
             jax.ShapeDtypeStruct((2, CHUNKS, GROUP, 16, HEAD), BF16),
             jax.ShapeDtypeStruct((128, FEATS // 2), BF16),
-            jax.ShapeDtypeStruct((2, 2, 64, HEAD), F32),
+            jax.ShapeDtypeStruct((4, 2, 2, 64, HEAD), BF16),
         ),
         in_specs=[anywhere] * 7 + [vmem],
         out_specs=(anywhere,) * 3,

time: 67.7 us -> 63 us (0.931)
  Pallas kernels: 66.9 us -> 62.2 us
    pallas_call x1, Pallas kernels: 64.7 us -> 60 us  [local_step(): pl.pallas_call(kernel, out_shape=(jax.ShapeDtypeStruct((2, CHUNKS, GROUP,...]
where the time goes in v7:
time: 63 us; the launch traced here: 62.8 us
  Pallas kernels  62.2 us (99%)
  between operations  0.64 us (1%)
    pallas_call x1, Pallas kernels, local_step(): pl.pallas_call(kernel, out_shape=(jax.ShapeDtypeStruct((2, CHUNKS, GROUP,...  60 us
    pallas_call x1, Pallas kernels, local_step(): pl.pallas_call(finish, out_shape=(jax.ShapeDtypeStruct((128, 2 * GROUP *...  2.18 us

profile of v7, /device:TPU:0, one launch (start us, length us, event | category | flops | bytes accessed | tf_op | source)
XLA Modules:
  0.0 62.8 jit_solution(16113359028483619655)
XLA Ops:
  0.6 60.0 %shard_map.111 = (bf16[2,8,4,16,128]{4,3,2,1,0:T(8,128)(2,1)}, bf16[128,2048]{1,0:T(8,128)(2,1)}, bf16[4,2,2,64,128]{4,3,2,1,0:T(8,128)(2,1)}) custom-call(bf16[8,16,1024]{2,1,0:T(8,128)(2,1)} %bitcast.6, bf16[8,16,1024]{2,1,0:T(8,128)(2,1)} %bitcast.7, bf16[8,16,256]{2,1,0:T(8,128)(2,1)} %bitcast.8, bf16[8,16,256]{2,1,0:T(8,128)(2,1)} %bitcast.9, ...), custom_call_target="tpu_custom_call" | custom-call | tf_op jit(solution)/shard_map/pallas_call | solution.py:694
  60.7 2.2 %shard_map.112 = (bf16[128,1024]{1,0:T(8,128)(2,1)}, bf16[128,2048]{1,0:T(8,128)(2,1)}, f32[64,256]{1,0:T(8,128)}, f32[64,256]{1,0:T(8,128)}) custom-call(bf16[2,8,4,16,128]{4,3,2,1,0:T(8,128)(2,1)} %get-tuple-element.7.dq_in, bf16[128,2048]{1,0:T(8,128)(2,1)} %get-tuple-element.8.ig_in, bf16[4,2,2,64,128]{4,3,2,1,0:T(8,128)(2,1)} %get-tuple-element.9.w_in), custom_call_target="tpu_custom_call" | custom-call | tf_op jit(solution)/shard_map/pallas_call | solution.py:722

commit v8 on v7

--- a/solution.py
+++ b/solution.py
@@ -27,7 +27,7 @@
 KROWS = 128
 NSEM = 71
 NSEND = 5
-NLOCAL = 8
+NLOCAL = 9
 
 
 def key_chunks(cq):
@@ -84,6 +84,7 @@
     "wown": ((2, 4, 4) + UNIT_W, F32),
     "wmine": ((2,) + UNIT_W, BF16),
     "igv": ((128, FEATS // 2), BF16),
+    "rp": ((64, 64), jnp.int32),
     **reduce_buffers("a", UNIT_KV),
     **reduce_buffers("w", UNIT_W),
 }
@@ -144,8 +145,8 @@
 def kernel(
     q_in, g_in, k_in, v_in, x_in, mk_in, mv_in, rp_in, dq_out, ig_out, w_out, *scratch
 ):
-    ssem, rsem, lsem = scratch[-3:]
-    b = dict(zip(BUFFERS, scratch[:-3]))
+    ssem, rsem, lsem, relay = scratch[-4:]
+    b = dict(zip(BUFFERS, scratch[:-4]))
     y, zh, x, core, zl = (lax.axis_index(a) for a in (Y, ZH, X, CORE, ZL))
 
     def turn(i, by):
@@ -212,14 +213,17 @@
     ]
     kst = b["kst"]
     stage = [local(("kst", t), ref, kst.at[t]) for t, ref in enumerate((k_in, v_in))]
-    for c in stage:
+    stage_rp = local("rp", rp_in, b["rp"])
+    for c in stage + [stage_rp]:
         c.start()
 
     barrier = pltpu.get_barrier_semaphore()
-    peers = [d_core, *step_of[X], *step_of[Y], *far_of.values(), d_zp, d_zm, d_zh]
+    peers = [d_core, *step_of[X], *step_of[Y], d_zp, d_zm]
     for dev in peers:
         pl.semaphore_signal(barrier, inc=1, device_id=dev, device_id_type=MESH)
     pl.semaphore_wait(barrier, len(peers))
+    for a in (X, Y):
+        pl.semaphore_signal(relay, inc=1, device_id=step_of[a][0], device_id_type=MESH)
 
     for c in stage:
         c.wait()
@@ -267,27 +271,32 @@
         for side in range(2):
             send(*forward_piece(h, n, side))
 
+    pl.semaphore_wait(relay, 2)
     for h in range(2):
         arrived(("zkv", h), kv.at[h, qi[h], pi[h]])
         unit = kv.at[h, qi[h], pi[h]]
         for side in range(2):
             send(("p", h, side), 0, unit, unit, p_to[h][side])
+    for h in range(2):
+        unit = kv.at[h, qi[h], pi[h]]
         send(("pf", h), 0, unit, unit, p_far[h])
+
+    for h in range(2):
         send_unit(h, 0)
+
     own_x.start()
     for c in own_m:
         c.start()
     b["st"][0] = jnp.full(b["st"].shape[1:], MASKED, F32)
     b["st"][1:] = jnp.zeros((2,) + b["st"].shape[1:], F32)
-    positions(rp_in, b["kpb"], b["qp"], y, x, core)
+    stage_rp.wait()
+    positions(b["rp"], b["kpb"], b["qp"], y, x, core)
     for h in range(2):
         for side in range(2):
             src = kv.at[h, qi[h], turn(pi[h], 3 if side == 0 else 1)]
             arrived(("p", h, side), src)
         for side in range(2):
             send_unit(h, 1 + side)
-    for h in range(2):
-        forward_unit(h, 0)
     for t in range(2):
         for r, (dev, head) in enumerate(across):
             src = qg.at[t, :, 2 * head + core]
@@ -360,7 +369,7 @@
 
         @pl.when(s == 1)
         def _():
-            for n in range(1, 4):
+            for n in range(4):
                 for h in range(2):
                     forward_unit(h, n)
 
@@ -675,22 +684,40 @@
     assert len(names) <= NSEM and len(local_names) <= NLOCAL
 
 
-def finish(dq_in, ig_in, w_in, dq_out, ig_out, kw_out, vw_out):
-    for c in range(CHUNKS):
-        for kvh in range(2):
-            for g in range(GROUP):
-                at = (kvh * GROUP + g) * HEAD
-                dq_out[c * 16 : (c + 1) * 16, at : at + HEAD] = dq_in[kvh, c, g]
-    ig_out[...] = ig_in[...]
-    for t, out in enumerate((kw_out, vw_out)):
+def finish(dq_in, ig_in, w_in, dq_out, ig_out, kw_out, vw_out, dq, ig, w, kv_w, sems):
+    copies = [pltpu.make_async_copy(w_in, w, sems.at[0])]
+    for kvh in range(2):
+        for g in range(GROUP):
+            at = (kvh * GROUP + g) * HEAD
+            copies.append(
+                pltpu.make_async_copy(dq_in.at[kvh, :, g], dq.at[:, :, at : at + HEAD], sems.at[1])
+            )
+    copies.append(pltpu.make_async_copy(ig_in, ig, sems.at[2]))
+    for c in copies:
+        c.start()
+    whole = [
+        pltpu.make_async_copy(dq, dq_out, sems.at[1]),
+        pltpu.make_async_copy(ig, ig_out, sems.at[2]),
+        pltpu.make_async_copy(kv_w.at[0], kw_out, sems.at[3]),
+        pltpu.make_async_copy(kv_w.at[1], vw_out, sems.at[4]),
+    ]
+    copies[0].wait()
+    for t in range(2):
         for n in range(2):
-            parts = [w_in[kind, t, n].astype(F32) for kind in range(4)]
-            out[:, n * HEAD : (n + 1) * HEAD] = (parts[0] + parts[1]) + (parts[2] + parts[3])
+            parts = [w[kind, t, n].astype(F32) for kind in range(4)]
+            kv_w[t, :, n * HEAD : (n + 1) * HEAD] = (parts[0] + parts[1]) + (parts[2] + parts[3])
+    whole[2].start()
+    whole[3].start()
+    whole[0].wait()
+    whole[0].start()
+    copies[-1].wait()
+    whole[1].start()
+    for c in whole:
+        c.wait()
 
 
 def local_step(q, k, v, g, x, mk, mv, placement):
     anywhere = pl.BlockSpec(memory_space=pl.ANY)
-    vmem = pl.BlockSpec(memory_space=pltpu.VMEM)
     dq, ig, w = pl.pallas_call(
         kernel,
         out_shape=(
@@ -698,13 +725,14 @@
             jax.ShapeDtypeStruct((128, FEATS // 2), BF16),
             jax.ShapeDtypeStruct((4, 2, 2, 64, HEAD), BF16),
         ),
-        in_specs=[anywhere] * 7 + [vmem],
+        in_specs=[anywhere] * 8,
         out_specs=(anywhere,) * 3,
         scratch_shapes=[pltpu.VMEM(shape, dtype) for shape, dtype in BUFFERS.values()]
         + [
             pltpu.SemaphoreType.DMA((NSEND,)),
             pltpu.SemaphoreType.DMA((NSEM,)),
             pltpu.SemaphoreType.DMA((NLOCAL,)),
+            pltpu.SemaphoreType.REGULAR,
         ],
         compiler_params=pltpu.CompilerParams(
             collective_id=0, has_side_effects=True, vmem_limit_bytes=67043328
@@ -719,17 +747,25 @@
         mv,
         placement,
     )
-    return pl.pallas_call(
+    query_grad, *rest = pl.pallas_call(
         finish,
         out_shape=(
-            jax.ShapeDtypeStruct((128, 2 * GROUP * HEAD), BF16),
+            jax.ShapeDtypeStruct((CHUNKS, 16, 2 * GROUP * HEAD), BF16),
             jax.ShapeDtypeStruct((128, FEATS // 2), BF16),
             jax.ShapeDtypeStruct((64, 2 * HEAD), F32),
             jax.ShapeDtypeStruct((64, 2 * HEAD), F32),
         ),
-        in_specs=[vmem] * 3,
-        out_specs=(vmem,) * 4,
+        in_specs=[anywhere] * 3,
+        out_specs=(anywhere,) * 4,
+        scratch_shapes=[
+            pltpu.VMEM((CHUNKS, 16, 2 * GROUP * HEAD), BF16),
+            pltpu.VMEM((128, FEATS // 2), BF16),
+            pltpu.VMEM((4, 2, 2, 64, HEAD), BF16),
+            pltpu.VMEM((2, 64, 2 * HEAD), F32),
+            pltpu.SemaphoreType.DMA((5,)),
+        ],
     )(dq, ig, w)
+    return (query_grad.reshape(128, -1), *rest)
 
 
 def solution(mesh):

time: 63 us -> 62.2 us (0.987)
  Pallas kernels: 62.2 us -> 61.4 us
    pallas_call x1, Pallas kernels: 60 us -> 59.3 us  [local_step(): pl.pallas_call(kernel, out_shape=(jax.ShapeDtypeStruct((2, CHUNKS, GROUP,...]
where the time goes in v8:
time: 62.2 us; the launch traced here: 62.1 us
  Pallas kernels  61.4 us (99%)
  between operations  0.64 us (1%)
    pallas_call x1, Pallas kernels, local_step(): pl.pallas_call(kernel, out_shape=(jax.ShapeDtypeStruct((2, CHUNKS, GROUP,...  59.3 us
    pallas_call x1, Pallas kernels, local_step(): pl.pallas_call(finish, out_shape=(jax.ShapeDtypeStruct((CHUNKS, 16, 2 * G...  2.12 us

profile of v8, /device:TPU:0, one launch (start us, length us, event | category | flops | bytes accessed | tf_op | source)
XLA Modules:
  0.0 62.1 jit_solution(4435813466801711553)
XLA Ops:
  0.6 59.3 %shard_map.111 = (bf16[2,8,4,16,128]{4,3,2,1,0:T(8,128)(2,1)}, bf16[128,2048]{1,0:T(8,128)(2,1)}, bf16[4,2,2,64,128]{4,3,2,1,0:T(8,128)(2,1)}) custom-call(bf16[8,16,1024]{2,1,0:T(8,128)(2,1)} %bitcast.7, bf16[8,16,1024]{2,1,0:T(8,128)(2,1)} %bitcast.8, bf16[8,16,256]{2,1,0:T(8,128)(2,1)} %bitcast.9, bf16[8,16,256]{2,1,0:T(8,128)(2,1)} %bitcast.10, ...), custom_call_target="tpu_custom_call" | custom-call | tf_op jit(solution)/shard_map/pallas_call | solution.py:721
  59.9 2.1 %shard_map.112 = (bf16[8,16,1024]{2,1,0:T(8,128)(2,1)}, bf16[128,2048]{1,0:T(8,128)(2,1)}, f32[64,256]{1,0:T(8,128)}, f32[64,256]{1,0:T(8,128)}) custom-call(bf16[2,8,4,16,128]{4,3,2,1,0:T(8,128)(2,1)} %get-tuple-element.11.dq_in, bf16[128,2048]{1,0:T(8,128)(2,1)} %get-tuple-element.12.ig_in, bf16[4,2,2,64,128]{4,3,2,1,0:T(8,128)(2,1)} %get-tuple-element.13.w_in), custom_call_target="tpu_custom_call" | custom-call | tf_op jit(solution)/shard_map/pallas_call | solution.py:750

commit v9 on v8

--- a/solution.py
+++ b/solution.py
@@ -70,7 +70,6 @@
     "dqf": ((CHUNKS, 2, 2, GROUP, 16, HEAD), F32),
     "dqr": ((CHUNKS, 2, GROUP, 16, HEAD), F32),
     "dqs": ((2, CHUNKS, GROUP, 16, HEAD), BF16),
-    "dqz": ((2, CHUNKS, GROUP, 16, HEAD), BF16),
     "kt": ((4, CHUNKS, HEAD, KROWS), BF16),
     "qp": ((CHUNKS, QROWS), F32),
     "xg": ((CHUNKS, 2, 16, FEATS), BF16),
@@ -83,7 +82,6 @@
     "dd": ((2, 2, 2, CHUNKS, 16, HEAD), BF16),
     "wown": ((2, 4, 4) + UNIT_W, F32),
     "wmine": ((2,) + UNIT_W, BF16),
-    "igv": ((128, FEATS // 2), BF16),
     "rp": ((64, 64), jnp.int32),
     **reduce_buffers("a", UNIT_KV),
     **reduce_buffers("w", UNIT_W),
@@ -551,7 +549,7 @@
         return carry
 
     lax.fori_loop(0, 4, second_pass, 0)
-    dqf, dqr, dqs, dqz = b["dqf"], b["dqr"], b["dqs"], b["dqz"]
+    dqf, dqr, dqs = b["dqf"], b["dqr"], b["dqs"]
     own_unit(0)
     wait_input()
     xt, xo = b["xt"], b["xo"]
@@ -620,7 +618,7 @@
     for n in range(2):
         dqs[n] = (dqf[:, n, core] + dqr[:, n]).astype(BF16)
     for r, (dev, other) in enumerate(across):
-        send("dqz", r, dqs.at[other], dqz.at[zh], dev)
+        send("dqz", r, dqs.at[other], dq_out.at[zh], dev)
     arrived("xt", xo)
     arrived("d2", d2o)
     weight_blocks(False)
@@ -663,20 +661,12 @@
     def input_block(i, carry):
         rows = pl.ds(pl.multiple_of(i * 512, 512), 512)
         cols = jnp.concatenate([mat[w, t, rows, :] for w in range(2) for t in range(2)], axis=1)
-        igv[:, lanes(i * 512, 512)] = dot_tt(token_grads, cols).astype(BF16)
+        ig_out[:, lanes(i * 512, 512)] = dot_tt(token_grads, cols).astype(BF16)
         return carry
 
-    igv = b["igv"]
     lax.fori_loop(0, 4, input_block, 0)
-    ig_copy = local("ig out", igv, ig_out)
-    ig_copy.start()
-    arrived("dqz", dqz)
-    outs = [local("dq out", dqz, dq_out)]
-    outs[0].start()
+    arrived("dqz", dq_out)
     arrived("ws", w_out)
-    outs.append(ig_copy)
-    for c in outs:
-        c.wait()
 
     for group, kib in enumerate(filled):
         size_of = e_ref.at[0, pl.ds(0, kib), :]
@@ -684,49 +674,40 @@
     assert len(names) <= NSEM and len(local_names) <= NLOCAL
 
 
-def finish(dq_in, ig_in, w_in, dq_out, ig_out, kw_out, vw_out, dq, ig, w, kv_w, sems):
-    copies = [pltpu.make_async_copy(w_in, w, sems.at[0])]
+def finish(dq_in, ig_in, w_in, dq_out, ig_out, kw_out, vw_out, dq, kv_w, sems):
+    whole = [
+        pltpu.make_async_copy(ig_in, ig_out, sems.at[0]),
+        pltpu.make_async_copy(dq, dq_out, sems.at[1]),
+        pltpu.make_async_copy(kv_w.at[0], kw_out, sems.at[2]),
+        pltpu.make_async_copy(kv_w.at[1], vw_out, sems.at[3]),
+    ]
+    whole[0].start()
     for kvh in range(2):
         for g in range(GROUP):
             at = (kvh * GROUP + g) * HEAD
-            copies.append(
-                pltpu.make_async_copy(dq_in.at[kvh, :, g], dq.at[:, :, at : at + HEAD], sems.at[1])
-            )
-    copies.append(pltpu.make_async_copy(ig_in, ig, sems.at[2]))
-    for c in copies:
-        c.start()
-    whole = [
-        pltpu.make_async_copy(dq, dq_out, sems.at[1]),
-        pltpu.make_async_copy(ig, ig_out, sems.at[2]),
-        pltpu.make_async_copy(kv_w.at[0], kw_out, sems.at[3]),
-        pltpu.make_async_copy(kv_w.at[1], vw_out, sems.at[4]),
-    ]
-    copies[0].wait()
+            dq[:, :, at : at + HEAD] = dq_in[kvh, :, g]
+    whole[1].start()
     for t in range(2):
         for n in range(2):
-            parts = [w[kind, t, n].astype(F32) for kind in range(4)]
+            parts = [w_in[kind, t, n].astype(F32) for kind in range(4)]
             kv_w[t, :, n * HEAD : (n + 1) * HEAD] = (parts[0] + parts[1]) + (parts[2] + parts[3])
-    whole[2].start()
-    whole[3].start()
-    whole[0].wait()
-    whole[0].start()
-    copies[-1].wait()
-    whole[1].start()
+        whole[2 + t].start()
     for c in whole:
         c.wait()
 
 
 def local_step(q, k, v, g, x, mk, mv, placement):
     anywhere = pl.BlockSpec(memory_space=pl.ANY)
+    vmem = pl.BlockSpec(memory_space=pltpu.VMEM)
     dq, ig, w = pl.pallas_call(
         kernel,
         out_shape=(
-            jax.ShapeDtypeStruct((2, CHUNKS, GROUP, 16, HEAD), BF16),
-            jax.ShapeDtypeStruct((128, FEATS // 2), BF16),
-            jax.ShapeDtypeStruct((4, 2, 2, 64, HEAD), BF16),
+            pltpu.VMEM((2, CHUNKS, GROUP, 16, HEAD), BF16),
+            pltpu.VMEM((128, FEATS // 2), BF16),
+            pltpu.VMEM((4, 2, 2, 64, HEAD), BF16),
         ),
         in_specs=[anywhere] * 8,
-        out_specs=(anywhere,) * 3,
+        out_specs=(vmem,) * 3,
         scratch_shapes=[pltpu.VMEM(shape, dtype) for shape, dtype in BUFFERS.values()]
         + [
             pltpu.SemaphoreType.DMA((NSEND,)),
@@ -735,7 +716,7 @@
             pltpu.SemaphoreType.REGULAR,
         ],
         compiler_params=pltpu.CompilerParams(
-            collective_id=0, has_side_effects=True, vmem_limit_bytes=67043328
+            collective_id=0, has_side_effects=True, vmem_limit_bytes=65 * 1000 * 1000
         ),
     )(
         q.reshape(CHUNKS, 16, -1),
@@ -755,16 +736,14 @@
             jax.ShapeDtypeStruct((64, 2 * HEAD), F32),
             jax.ShapeDtypeStruct((64, 2 * HEAD), F32),
         ),
-        in_specs=[anywhere] * 3,
+        in_specs=[vmem] * 3,
         out_specs=(anywhere,) * 4,
         scratch_shapes=[
             pltpu.VMEM((CHUNKS, 16, 2 * GROUP * HEAD), BF16),
-            pltpu.VMEM((128, FEATS // 2), BF16),
-            pltpu.VMEM((4, 2, 2, 64, HEAD), BF16),
             pltpu.VMEM((2, 64, 2 * HEAD), F32),
-            pltpu.SemaphoreType.DMA((5,)),
+            pltpu.SemaphoreType.DMA((4,)),
         ],
-    )(dq, ig, w)
+    )(*[pltpu.with_memory_space_constraint(a, pltpu.VMEM) for a in (dq, ig, w)])
     return (query_grad.reshape(128, -1), *rest)
 
 

time: 62.2 us -> 60.9 us (0.979)
  Pallas kernels: 61.4 us -> 60.1 us
    pallas_call x1, Pallas kernels: 2.12 us -> 0.95 us  [local_step(): pl.pallas_call(finish, out_shape=(jax.ShapeDtypeStruct((CHUNKS, 16, 2 * G...]
where the time goes in v9:
time: 60.9 us; the launch traced here: 60.8 us
  Pallas kernels  60.1 us (99%)
  between operations  0.64 us (1%)
    pallas_call x1, Pallas kernels, local_step(): pl.pallas_call(kernel, out_shape=(pltpu.VMEM((2, CHUNKS, GROUP, 16, HEAD)...  59.2 us

profile of v9, /device:TPU:0, one launch (start us, length us, event | category | flops | bytes accessed | tf_op | source)
XLA Modules:
  0.0 60.8 jit_solution(5628668699691345588)
XLA Ops:
  0.6 59.2 %shard_map.111 = (bf16[2,8,4,16,128]{4,3,2,1,0:T(8,128)(2,1)S(1)}, bf16[128,2048]{1,0:T(8,128)(2,1)S(1)}, bf16[4,2,2,64,128]{4,3,2,1,0:T(8,128)(2,1)S(1)}) custom-call(bf16[8,16,1024]{2,1,0:T(8,128)(2,1)} %bitcast.7, bf16[8,16,1024]{2,1,0:T(8,128)(2,1)} %bitcast.8, bf16[8,16,256]{2,1,0:T(8,128)(2,1)} %bitcast.9, bf16[8,16,256]{2,1,0:T(8,128)(2,1)} %bitcast.10, ...), custom_call_target="tpu_custom_call" | custom-call | tf_op jit(solution)/shard_map/pallas_call | solution.py:702
  59.8 0.9 %shard_map.112 = (bf16[8,16,1024]{2,1,0:T(8,128)(2,1)}, bf16[128,2048]{1,0:T(8,128)(2,1)}, f32[64,256]{1,0:T(8,128)}, f32[64,256]{1,0:T(8,128)}) custom-call(bf16[2,8,4,16,128]{4,3,2,1,0:T(8,128)(2,1)S(1)} %get-tuple-element.11.dq_in, bf16[128,2048]{1,0:T(8,128)(2,1)S(1)} %get-tuple-element.12.ig_in, bf16[4,2,2,64,128]{4,3,2,1,0:T(8,128)(2,1)S(1)} %get-tuple-element.13.w_in), custom_call_target="tpu_custom_call" | custom-call | tf_op jit(solution)/shard_map/pallas_call | solution.py:731

commit v10 on v9

--- a/solution.py
+++ b/solution.py
@@ -613,15 +613,28 @@
 
         lax.fori_loop(0, 2, body, 0)
 
-    weight_blocks(True)
-    arrived("dqc", dqr)
-    for n in range(2):
-        dqs[n] = (dqf[:, n, core] + dqr[:, n]).astype(BF16)
-    for r, (dev, other) in enumerate(across):
-        send("dqz", r, dqs.at[other], dq_out.at[zh], dev)
+    def far_blocks(first):
+        cols = d2 if first else d2o
+        fy, fx = turn(y, 2), turn(x, 2)
+
+        def block(i, count):
+            return xt[pl.ds(i, count), core] if first else xo[pl.ds(i, count)]
+
+        rows = (
+            block(fy * 8, 8).reshape(512, 256),
+            jnp.concatenate([block(n * 4 + fx, 1).reshape(64, 256) for n in range(8)], axis=0),
+        )
+        for h in range(2):
+            part = dot_nn(rows[h], cols[h].reshape(256, HEAD))
+            for n in range(8):
+                piece = part[n * 64 : (n + 1) * 64]
+                at = (0, fy, n % 4, n // 4) if h == 0 else (1, fx, n // 2, n % 2)
+                wown[at] = piece if first else wown[at] + piece
+
+    far_blocks(True)
     arrived("xt", xo)
     arrived("d2", d2o)
-    weight_blocks(False)
+    far_blocks(False)
     def deliver(h, n, value):
         kind, ref, hop = (
             (3, b["w_far2"].at[h], p_far[h]),
@@ -635,6 +648,13 @@
 
     w_far, w_near, w_unit = reducer("w", lambda h, q, p, slot: wown[h, q, p], deliver)
     w_far()
+    weight_blocks(True)
+    arrived("dqc", dqr)
+    for n in range(2):
+        dqs[n] = (dqf[:, n, core] + dqr[:, n]).astype(BF16)
+    for r, (dev, other) in enumerate(across):
+        send("dqz", r, dqs.at[other], dq_out.at[zh], dev)
+    weight_blocks(False)
 
     for n in range(4):
         w_near(n)

time: 60.9 us -> 60.6 us (level)
  no operation moved by 1% of the time
where the time goes in v10:
time: 60.6 us; the launch traced here: 60.5 us
  Pallas kernels  59.9 us (99%)
  between operations  0.64 us (1%)
    pallas_call x1, Pallas kernels, local_step(): pl.pallas_call(kernel, out_shape=(pltpu.VMEM((2, CHUNKS, GROUP, 16, HEAD)...  58.9 us

profile of v10, /device:TPU:0, one launch (start us, length us, event | category | flops | bytes accessed | tf_op | source)
XLA Modules:
  0.0 60.5 jit_solution(17869475772245688590)
XLA Ops:
  0.6 58.9 %shard_map.111 = (bf16[2,8,4,16,128]{4,3,2,1,0:T(8,128)(2,1)S(1)}, bf16[128,2048]{1,0:T(8,128)(2,1)S(1)}, bf16[4,2,2,64,128]{4,3,2,1,0:T(8,128)(2,1)S(1)}) custom-call(bf16[8,16,1024]{2,1,0:T(8,128)(2,1)} %bitcast.7, bf16[8,16,1024]{2,1,0:T(8,128)(2,1)} %bitcast.8, bf16[8,16,256]{2,1,0:T(8,128)(2,1)} %bitcast.9, bf16[8,16,256]{2,1,0:T(8,128)(2,1)} %bitcast.10, ...), custom_call_target="tpu_custom_call" | custom-call | tf_op jit(solution)/shard_map/pallas_call | solution.py:722
  59.6 0.9 %shard_map.112 = (bf16[8,16,1024]{2,1,0:T(8,128)(2,1)}, bf16[128,2048]{1,0:T(8,128)(2,1)}, f32[64,256]{1,0:T(8,128)}, f32[64,256]{1,0:T(8,128)}) custom-call(bf16[2,8,4,16,128]{4,3,2,1,0:T(8,128)(2,1)S(1)} %get-tuple-element.11.dq_in, bf16[128,2048]{1,0:T(8,128)(2,1)S(1)} %get-tuple-element.12.ig_in, bf16[4,2,2,64,128]{4,3,2,1,0:T(8,128)(2,1)S(1)} %get-tuple-element.13.w_in), custom_call_target="tpu_custom_call" | custom-call | tf_op jit(solution)/shard_map/pallas_call | solution.py:751

commit v11 on v10

--- a/solution.py
+++ b/solution.py
@@ -25,7 +25,7 @@
 MASKED = -1e30
 QROWS = 256
 KROWS = 128
-NSEM = 71
+NSEM = 64
 NSEND = 5
 NLOCAL = 9
 
@@ -262,7 +262,7 @@
 
     def forward_piece(h, n, side):
         src = near_piece(h, n, side).at[side]
-        return ("qf", h, side), n, src, src, q_to[h][side]
+        return "qf", (h, n, side), src, src, q_to[h][side]
 
     def forward_unit(h, n):
         arrived(("q", h, n), kv.at[h, 0, pl.ds(0, 2)])
@@ -299,7 +299,7 @@
         for r, (dev, head) in enumerate(across):
             src = qg.at[t, :, 2 * head + core]
             arrived(("qz", t, r), src)
-            send(("qc", t), r, src, src, d_core)
+            send("qc", (t, r), src, src, d_core)
 
     def send_matrix(t):
         ref = (mk_in, mv_in)[t]
@@ -307,7 +307,7 @@
             at = (2 * r + core) * 512
             src = ref.at[pl.ds(pl.multiple_of(ol * half_feats + at, 512), 512), :]
             dst = mat.at[1, t, pl.ds(pl.multiple_of(at, 512), 512), :]
-            yield ("m", t, r), 0, src, dst, dev
+            yield "m", (t, r), src, dst, dev
 
     def matrix_part(t, r, which):
         return mat.at[1, t, pl.ds(pl.multiple_of((2 * r + which) * 512, 512), 512), :]
@@ -345,8 +345,7 @@
     for h in range(2):
         arrived(("pf", h), kv.at[h, qi[h], turn(pi[h], 2)])
         send_unit(h, 3)
-    for t in range(2):
-        arrived(("qc", t), qg.at[t, pl.ds(0, CHUNKS // 2)])
+    arrived("qc", qg.at[0])
 
     def tile_rows(cq, ck):
         return pl.ds(TILE_AT[cq] + (ck - key_chunks(cq)[0]) * KROWS, KROWS)
@@ -373,9 +372,7 @@
 
         @pl.when(s == 3)
         def _():
-            for h in range(2):
-                for side in range(2):
-                    arrived(("qf", h, side), kv.at[h, turn(qi[h], 2), :, side])
+            arrived("qf", kv.at[0, pl.ds(0, 2)])
             forward_input()
             for t in range(2):
                 for copy in send_matrix(t):
@@ -660,10 +657,10 @@
         w_near(n)
     for c in own_m:
         c.wait()
+    arrived("m", mat.at[1, 0])
     for t in range(2):
         for r in range(2):
             src = matrix_part(t, r, core)
-            arrived(("m", t, r), src)
             send("mc", (t, r), src, src, d_core)
     for n in range(4):
         w_unit(n)

time: 60.6 us -> 60.6 us (level)
  no operation moved by 1% of the time
where the time goes in v11:
time: 60.6 us; the launch traced here: 60.5 us
  Pallas kernels  59.8 us (99%)
  between operations  0.64 us (1%)
    pallas_call x1, Pallas kernels, local_step(): pl.pallas_call(kernel, out_shape=(pltpu.VMEM((2, CHUNKS, GROUP, 16, HEAD)...  58.9 us

profile of v11, /device:TPU:0, one launch (start us, length us, event | category | flops | bytes accessed | tf_op | source)
XLA Modules:
  0.0 60.5 jit_solution(5985350692785649528)
XLA Ops:
  0.6 58.9 %shard_map.111 = (bf16[2,8,4,16,128]{4,3,2,1,0:T(8,128)(2,1)S(1)}, bf16[128,2048]{1,0:T(8,128)(2,1)S(1)}, bf16[4,2,2,64,128]{4,3,2,1,0:T(8,128)(2,1)S(1)}) custom-call(bf16[8,16,1024]{2,1,0:T(8,128)(2,1)} %bitcast.7, bf16[8,16,1024]{2,1,0:T(8,128)(2,1)} %bitcast.8, bf16[8,16,256]{2,1,0:T(8,128)(2,1)} %bitcast.9, bf16[8,16,256]{2,1,0:T(8,128)(2,1)} %bitcast.10, ...), custom_call_target="tpu_custom_call" | custom-call | tf_op jit(solution)/shard_map/pallas_call | solution.py:719
  59.5 0.9 %shard_map.112 = (bf16[8,16,1024]{2,1,0:T(8,128)(2,1)}, bf16[128,2048]{1,0:T(8,128)(2,1)}, f32[64,256]{1,0:T(8,128)}, f32[64,256]{1,0:T(8,128)}) custom-call(bf16[2,8,4,16,128]{4,3,2,1,0:T(8,128)(2,1)S(1)} %get-tuple-element.11.dq_in, bf16[128,2048]{1,0:T(8,128)(2,1)S(1)} %get-tuple-element.12.ig_in, bf16[4,2,2,64,128]{4,3,2,1,0:T(8,128)(2,1)S(1)} %get-tuple-element.13.w_in), custom_call_target="tpu_custom_call" | custom-call | tf_op jit(solution)/shard_map/pallas_call | solution.py:748
